TPU v7x, 32 devices: a whole 2x2x4 slice. The times are simulated.
32 devices in a mesh: shot: 8 (over y, x, core), slab: 4 (over z).
Axes of the slice: x: 2, y: 2, z: 4, core: 2. Of those that a mesh axis runs over, the one named last changes fastest.
Arguments:
- model_tiles: float32 [64, 32, 1024], P('shot', 'slab'), may hold values from -0.3 to 0.3
- background: float32 [8, 32, 128, 128], P('shot', 'slab'), may hold values from 0.05 to 0.18
- u_prev: float32 [8, 32, 128, 128], P('shot', 'slab'), may hold values from -6 to 6
- u_now: float32 [8, 32, 128, 128], P('shot', 'slab'), may hold values from -6 to 6
- du_prev: float32 [8, 32, 128, 128], P('shot', 'slab'), may hold values from -2 to 2
- du_now: float32 [8, 32, 128, 128], P('shot', 'slab'), may hold values from -2 to 2
- w_prev: float32 [8, 32, 128, 128], P('shot', 'slab'), may hold values from -6 to 6
- w_now: float32 [8, 32, 128, 128], P('shot', 'slab'), may hold values from -6 to 6
- wavelet: float32 [8, 3], P('shot'), may hold values from -4 to 4
- source_cell: int32 [8], P('shot'), may hold values from 0 to 524287
- receiver_cells: int32 [8, 256], P('shot'), may hold values from 0 to 524287
- aperture: int32 [8, 16], replicated, may hold values from 0 to 63, as said below
- tile_slot: int32 [64], replicated, may hold values from 0 to 63, as said below
Outputs:
- sensitivity: float32 [64, 32, 1024], P('shot', 'slab')
- u_final: float32 [8, 32, 128, 128], P('shot', 'slab')
- du_final: float32 [8, 32, 128, 128], P('shot', 'slab')
- w_final: float32 [8, 32, 128, 128], P('shot', 'slab')
- record: float32 [8, 3, 256], P('shot')
Inputs may be any that keep to these rules, and one draw needn't show every extreme that they name: `aperture`: each row lists the 16 tiles of a square window of 4 x 4 tiles of the lateral tile grid (4 rows of 16 tiles, tile id = row * 4 * 4 + column), row by row; windows of different shots may intersect. `tile_slot`: A permutation of the 64 storage slots; slot q is stored by shot index q // 8 as its local tile q % 8. The shot indices fall into four sets of 2, each of which stores exactly 4 tiles of every aperture; so at most 4 tiles of one aperture lie on one shot index, and exactly 4 do for some shot index and aperture in every draw.
All inputs are finite; a program needn't handle non-finite values.
Results may differ from a plain program's by a relative error of at most 0.00002.
Values sent between devices are 32-bit elements; how exact they have to be, the bound alone decides.
No kernel may reach another device: no remote copies, remote signals or barrier semaphores. Data moves between devices by JAX's collectives and lax.ppermute only.
A program may use at most 128 MiB of HBM per device.

v0:
```python
import functools
import math

import jax
import jax.numpy as jnp
from jax import lax
from jax.experimental import pallas as pl
from jax.experimental.pallas import tpu as pltpu
from jax.sharding import PartitionSpec as P


COEFFS = (-205.0 / 72.0, 8.0 / 5.0, -1.0 / 5.0, 8.0 / 315.0, -1.0 / 560.0)
HALO = len(COEFFS) - 1
SUB = 8
F32 = jnp.float32
VMEM = pl.BlockSpec(memory_space=pltpu.VMEM)
SMEM = pl.BlockSpec(memory_space=pltpu.SMEM)
HBM = pl.BlockSpec(memory_space=pltpu.HBM)


def params(mib):
    return pltpu.CompilerParams(vmem_limit_bytes=mib * 1024 * 1024)


def sds(shape, dtype=F32):
    return jax.ShapeDtypeStruct(shape, dtype)


def place():
    slab, count = lax.axis_index("slab"), lax.axis_size("slab")
    odd = lax.bitwise_and(slab, 1)
    above, below = slab < count - 1, slab > 0
    is_odd = odd == 1
    return odd, (is_odd & below) | (~is_odd & above), (is_odd & above) | (~is_odd & below)


def quotient(x, m):
    return lax.shift_right_logical(x, m.bit_length() - 1) if m & (m - 1) == 0 else lax.div(x, m)


def remainder(x, m):
    return lax.bitwise_and(x, m - 1) if m & (m - 1) == 0 else lax.rem(x, m)


SCALE = 5040.0
PARTS = 4


def band_weights(side):
    i = lax.broadcasted_iota(jnp.int32, (2 * side, 2 * side), 0)
    j = lax.broadcasted_iota(jnp.int32, (2 * side, 2 * side), 1)
    far = jnp.where((i < side) == (j < side), jnp.abs(i - j), 0)
    out = jnp.zeros((2 * side, 2 * side), F32)
    for k in range(1, HALO + 1):
        out = jnp.where(far == k, round(COEFFS[k] * SCALE) * 1.0, out)
    out = out.astype(jnp.bfloat16)
    return jnp.concatenate([out, out, out], axis=0)


def split3(x):
    high = x.astype(jnp.bfloat16)
    rest = x - high.astype(F32)
    mid = rest.astype(jnp.bfloat16)
    low = (rest - mid.astype(F32)).astype(jnp.bfloat16)
    return high, mid, low


def prepare(work, now_ref, first_ref, second_ref, index, weights, inject=None):
    rows_ref, halo_ref, lanes_ref = work
    depth, side, _ = now_ref.shape
    odd, has_first, has_second = place()
    zeros = jnp.zeros((SUB, side), F32)
    half = depth // 2
    parts = []
    for low, high in zip(split3(now_ref[pl.ds(0, half)]), split3(now_ref[pl.ds(half, half)])):
        parts += [low.reshape(half * side, side), high.reshape(half * side, side)]
    lanes = jnp.dot(jnp.concatenate(parts, axis=1), weights, preferred_element_type=F32)
    lanes_ref[pl.ds(0, half)] = lanes[:, :side].reshape(half, side, side)
    lanes_ref[pl.ds(half, half)] = lanes[:, side:].reshape(half, side, side)
    for z in range(depth):
        rows_ref[z, pl.ds(0, SUB), :] = zeros
        rows_ref[z, pl.ds(SUB + side, SUB), :] = zeros
        rows_ref[z, pl.ds(SUB, side), :] = now_ref[z]

    def halo(z, carry):
        halo_ref[1 - odd, z] = jnp.where(has_first, first_ref[index, z], 0.0)
        halo_ref[odd, z] = jnp.where(has_second, second_ref[index, z], 0.0)
        return carry

    lax.fori_loop(0, HALO, halo, 0)
    if inject:
        outer_ref, other_ref = inject
        for end in range(2):
            for z in range(HALO):
                halo_ref[end, z] = halo_ref[end, z] + outer_ref[end, z] * other_ref[end, z]


def each_laplacian(work, now_ref, emit, finish=None, parts=1):
    rows_ref, halo_ref, lanes_ref = work
    depth, side, _ = now_ref.shape

    def block(g, carry):
        start = pl.multiple_of(g * SUB, SUB)
        rows = pl.ds(start, SUB)
        column = [halo_ref[0, z, rows, :] for z in range(HALO)]
        column += [now_ref[z, rows, :] for z in range(depth)]
        column += [halo_ref[1, z, rows, :] for z in range(HALO)]
        for z in range(depth):
            centre = column[HALO + z]
            total = (3.0 * COEFFS[0]) * centre + (1.0 / SCALE) * lanes_ref[z, rows, :]
            for k in range(1, HALO + 1):
                ring = (column[HALO + z + k] + column[HALO + z - k]) + (
                    rows_ref[z, pl.ds(start + (SUB + k), SUB), :] + rows_ref[z, pl.ds(start + (SUB - k), SUB), :]
                )
                total = total + COEFFS[k] * ring
            emit(z, rows, centre, total)
        return carry

    blocks = side // SUB // parts
    for part in range(parts):
        lax.fori_loop(part * blocks, (part + 1) * blocks, block, 0)
        if finish:
            finish(part, parts)


def work_space(depth, side):
    return [
        pltpu.VMEM((depth, side + 2 * SUB, side), F32),
        pltpu.VMEM((2, HALO, side, side), F32),
        pltpu.VMEM((depth, side, side), F32),
    ]


def copy_sends(next_ref, first_ref, second_ref, index):
    depth = next_ref.shape[0]
    odd = place()[0] == 1
    first = jnp.where(odd, 0, depth - HALO)
    second = jnp.where(odd, depth - HALO, 0)
    for z in range(HALO):
        first_ref[index, z] = next_ref[first + z]
        second_ref[index, z] = next_ref[second + z]


def store_out(next_ref, out_ref, sems, step, steps):
    rows = pl.ds(step * (next_ref.shape[1] // steps), next_ref.shape[1] // steps)
    return pltpu.make_async_copy(next_ref.at[:, rows], out_ref.at[0, :, rows], sems.at[step])


class Refs:
    def __init__(self, refs):
        self.refs = list(refs)

    def take(self, n=None):
        if n is None:
            return self.refs.pop(0)
        return [self.refs.pop(0) for _ in range(n)]


def u_kernel(step, last, tiles, *refs):
    refs = Refs(refs)
    source_ref, wavelet_ref, now_ref, prev_ref, ha_ref, hb_ref, speed_ref, w_ref = refs.take(8)
    corr_in = refs.take() if step else None
    if last:
        tables = refs.take(2)
        out_ref, lap_ref = refs.take(2)
        blocks = refs.take(tiles[0])
        sends = []
        next_ref, corr_ref = refs.take(2)
    else:
        next_ref, lap_ref, corr_ref = refs.take(3)
        sends = refs.take(2)
    work = refs.take(3)
    if last:
        fetched = refs.take(2)
        tiles_ref, seen_ref, place_ref, sems, table_sems = refs.take(5)
        copies = [pltpu.make_async_copy(a, b, table_sems.at[i]) for i, (a, b) in enumerate(zip(tables, fetched))]
        for copy in copies:
            copy.start()
    depth, side, _ = now_ref.shape
    prepare(work, now_ref, ha_ref, hb_ref, 0, band_weights(side))

    def emit(z, block, centre, lap):
        lap_ref[z, block, :] = lap
        part = lap * w_ref[z, block, :]
        corr_ref[z, block, :] = corr_in[z, block, :] + part if step else part
        next_ref[z, block, :] = (2.0 * centre - prev_ref[z, block, :]) + speed_ref[z, block, :] * lap

    local = source_ref[0] - lax.axis_index("slab") * (depth * side * side)
    mine = (local >= 0) & (local < depth * side * side)
    cell = jnp.where(mine, local, 0)
    z = quotient(cell, side * side)
    x = remainder(quotient(cell, side), side)
    lane = lax.broadcasted_iota(jnp.int32, (1, side), 1)
    add = jnp.where((lane == remainder(cell, side)) & mine, wavelet_ref[:, step : step + 1], 0.0)

    def finish(part, parts):
        size = side // parts

        @pl.when((x >= part * size) & (x < (part + 1) * size))
        def _():
            next_ref[z, pl.ds(x, 1), :] = next_ref[z, pl.ds(x, 1), :] + add

        if last:
            store_out(next_ref, out_ref, sems, part, parts).start()

    parts = PARTS if last else 1
    each_laplacian(work, now_ref, emit, finish, parts)
    if sends:
        copy_sends(next_ref, *sends, 0)
    if last:
        for copy in copies:
            copy.wait()
        pack_back(*tiles[1:], *fetched, corr_ref, blocks, tiles_ref, seen_ref, place_ref)
        for part in range(parts):
            store_out(next_ref, out_ref, sems, part, parts).wait()


def w_bare_kernel(index, now_ref, prev_ref, ha_ref, hb_ref, speed_ref, next_ref, *rest):
    sends, work = rest[:2], rest[2:]
    _, side, _ = now_ref.shape
    prepare(work, now_ref, ha_ref, hb_ref, index, band_weights(side))

    def emit(z, block, centre, lap):
        next_ref[z, block, :] = (2.0 * centre - prev_ref[z, block, :]) + speed_ref[z, block, :] * lap

    each_laplacian(work, now_ref, emit)
    copy_sends(next_ref, *sends, 0)


def d_kernel(index, now_ref, prev_ref, ha_ref, hb_ref, speed_ref, perturb_ref, lap_u_ref, bare_ref, count_ref, *rest):
    next_ref, w_ref, *sends = rest[:4]
    work = rest[4:]
    _, side, _ = now_ref.shape
    prepare(work, now_ref, ha_ref, hb_ref, index, band_weights(side))

    def emit(z, block, centre, lap):
        new = ((2.0 * centre - prev_ref[z, block, :]) + speed_ref[z, block, :] * lap) + (
            perturb_ref[z, block, :] * lap_u_ref[z, block, :]
        )
        next_ref[z, block, :] = new
        w_ref[z, block, :] = bare_ref[z, block, :] + count_ref[z, block, :] * new

    each_laplacian(work, now_ref, emit)
    copy_sends(next_ref, *sends, 0)


def dw_kernel(bare, *refs):
    refs = Refs(refs)
    speed_ref, d_ref, d_prev, w_ref, w_prev, perturb_ref, lap_u_ref, count_ref = refs.take(8)
    d_halo, w_halo = refs.take(2), refs.take(2)
    outer_ref = refs.take() if bare else None
    d_next, w_next = refs.take(2)
    d_sends, w_sends = refs.take(2), refs.take(2)
    d_work, w_work = refs.take(3), refs.take(3)
    _, side, _ = speed_ref.shape
    weights = band_weights(side)
    prepare(d_work, d_ref, *d_halo, 0, weights)
    prepare(w_work, w_ref, *w_halo, 0, weights, (outer_ref, d_work[1]) if bare else None)

    def emit_d(z, block, centre, lap):
        d_next[z, block, :] = ((2.0 * centre - d_prev[z, block, :]) + speed_ref[z, block, :] * lap) + (
            perturb_ref[z, block, :] * lap_u_ref[z, block, :]
        )

    def emit_w(z, block, centre, lap):
        w_next[z, block, :] = ((2.0 * centre - w_prev[z, block, :]) + speed_ref[z, block, :] * lap) + (
            count_ref[z, block, :] * d_next[z, block, :]
        )

    each_laplacian(d_work, d_ref, emit_d)
    copy_sends(d_next, *d_sends, 0)
    each_laplacian(w_work, w_ref, emit_w)
    copy_sends(w_next, *w_sends, 0)


def last_d_kernel(before, *refs):
    refs = Refs(refs)
    now_ref, prev_ref, ha_ref, hb_ref, speed_ref, perturb_ref, lap_u_ref, cells_hbm, cells_ref = refs.take(9)
    early_ref = refs.take() if before else None
    out_ref, next_ref, record_ref = refs.take(3)
    work = refs.take(3)
    cells_smem, rows_ref, sems, table_sem = refs.take(4)
    fetch = pltpu.make_async_copy(cells_hbm, cells_smem, table_sem)
    fetch.start()
    _, side, _ = now_ref.shape
    prepare(work, now_ref, ha_ref, hb_ref, 0, band_weights(side))

    def emit(z, block, centre, lap):
        next_ref[z, block, :] = ((2.0 * centre - prev_ref[z, block, :]) + speed_ref[z, block, :] * lap) + (
            perturb_ref[z, block, :] * lap_u_ref[z, block, :]
        )

    def finish(part, parts):
        store_out(next_ref, out_ref, sems, part, parts).start()

    each_laplacian(work, now_ref, emit, finish, PARTS)
    fetch.wait()
    if before:
        record_ref[pl.ds(0, before), :] = early_ref[...]
    fields = [now_ref, next_ref] if record_ref.shape[0] > before + 1 else [next_ref]
    gather_records(before, cells_smem, cells_ref, fields, record_ref, rows_ref)
    for part in range(PARTS):
        store_out(next_ref, out_ref, sems, part, PARTS).wait()


def last_w_kernel(bare, *refs):
    refs = Refs(refs)
    now_ref, prev_ref, ha_ref, hb_ref, speed_ref, count_ref, d_next, table_hbm = refs.take(8)
    d_halo = refs.take(2) if bare else None
    outer_ref = refs.take() if bare else None
    blocks = refs.take(lax.axis_size("shot"))
    out_ref, sum_ref = refs.take(2)
    next_ref = refs.take()
    work = refs.take(3)
    table_ref, sems, table_sem = refs.take(3)
    fetch = pltpu.make_async_copy(table_hbm, table_ref, table_sem)
    fetch.start()
    _, side, _ = now_ref.shape
    prepare(work, now_ref, ha_ref, hb_ref, 0, band_weights(side))

    def emit(z, block, centre, lap):
        next_ref[z, block, :] = ((2.0 * centre - prev_ref[z, block, :]) + speed_ref[z, block, :] * lap) + (
            count_ref[z, block, :] * d_next[z, block, :]
        )

    def finish(part, parts):
        store_out(next_ref, out_ref, sems, part, parts).start()

    each_laplacian(work, now_ref, emit, finish, PARTS)
    fetch.wait()
    sum_tiles(table_ref, blocks, sum_ref)
    for part in range(PARTS):
        store_out(next_ref, out_ref, sems, part, PARTS).wait()


def stencil_call(body, in_specs, args, outs, kinds, scratch):
    return pl.pallas_call(
        body, out_shape=outs, in_specs=in_specs, out_specs=kinds, scratch_shapes=scratch, compiler_params=params(20)
    )(*args)


def u_call(step, last, wavelet, source, u, u_prev, halo, speed, w, corr, aperture, tile_slot, lat_dev, tile_side):
    field = sds(u.shape)
    edge = sds((1, HALO) + u.shape[1:])
    args = [source, wavelet, u, u_prev, *halo, speed, w] + ([corr] if step else [])
    specs = [SMEM] + [VMEM] * (len(args) - 1)
    scratch = work_space(*u.shape[:2])
    n_shot, n_tiles = aperture.shape
    cells = tile_side * tile_side
    capacity = n_tiles // 4
    if last:
        args += [aperture, tile_slot]
        specs += [HBM, HBM]
        outs = [sds((1,) + u.shape), field] + [sds((capacity, u.shape[0], cells))] * n_shot
        kinds = [HBM] + [VMEM] * (1 + n_shot)
        scratch = [pltpu.VMEM(u.shape, F32)] * 2 + scratch + [
            pltpu.SMEM(aperture.shape, jnp.int32),
            pltpu.SMEM(tile_slot.shape, jnp.int32),
            *tile_scratch(n_shot, capacity, u.shape[0], cells, n_tiles),
            pltpu.SemaphoreType.DMA((PARTS,)),
            pltpu.SemaphoreType.DMA((2,)),
        ]
    else:
        outs, kinds = [field] * 3 + [edge] * 2, [VMEM] * 5
    body = functools.partial(u_kernel, step, last, (n_shot, lat_dev, tile_side))
    return stencil_call(body, specs, args, outs, kinds, scratch)


def w_bare_call(w, w_prev, halo, index, speed):
    field, edge = sds(w.shape), sds((1, HALO) + w.shape[1:])
    args = [w, w_prev, *halo, speed]
    body = functools.partial(w_bare_kernel, index)
    return stencil_call(body, [VMEM] * 5, args, [field, edge, edge], [VMEM] * 3, work_space(*w.shape[:2]))


def d_call(d, d_prev, halo, index, speed, perturb, lap_u, bare, count):
    field, edge = sds(d.shape), sds((1, HALO) + d.shape[1:])
    args = [d, d_prev, *halo, speed, perturb, lap_u, bare, count]
    body = functools.partial(d_kernel, index)
    outs = [field, field, edge, edge]
    return stencil_call(body, [VMEM] * 9, args, outs, [VMEM] * 4, work_space(*d.shape[:2]))


def dw_call(d, d_prev, w, w_prev, d_halo, w_halo, speed, perturb, lap_u, count, outer):
    field, edge = sds(d.shape), sds((1, HALO) + d.shape[1:])
    bare = outer is not None
    args = [speed, d, d_prev, w, w_prev, perturb, lap_u, count, *d_halo, *w_halo] + ([outer] if bare else [])
    outs = [field, field] + [edge] * 4
    body = functools.partial(dw_kernel, bare)
    return stencil_call(body, [VMEM] * len(args), args, outs, [VMEM] * 6, work_space(*d.shape[:2]) * 2)


def last_d_call(step, d, d_prev, halo, speed, perturb, lap_u, cells, early):
    before = 0 if early is None else early.shape[0]
    n = cells.shape[1]
    fields = step + 1 - before
    args = [d, d_prev, *halo, speed, perturb, lap_u, cells, cells] + ([early] if before else [])
    specs = [VMEM] * len(args)
    specs[7] = HBM
    scratch = work_space(*d.shape[:2]) + [
        pltpu.SMEM(cells.shape, jnp.int32),
        pltpu.VMEM((fields, n, d.shape[-1]), F32),
        pltpu.SemaphoreType.DMA((PARTS,)),
        pltpu.SemaphoreType.DMA(()),
    ]
    outs = [sds((1,) + d.shape), sds(d.shape), sds((step + 1, n))]
    body = functools.partial(last_d_kernel, before)
    return stencil_call(body, specs, args, outs, [HBM, VMEM, VMEM], scratch)


def last_w_call(w, w_prev, halo, speed, count, d_next, table, blocks, lat_dev):
    _, depth, cells = blocks[0].shape
    args = [w, w_prev, *halo, speed, count, d_next, table, *blocks]
    specs = [VMEM] * len(args)
    specs[7] = HBM
    scratch = [pltpu.VMEM(w.shape, F32)] + work_space(*w.shape[:2]) + [
        pltpu.SMEM(table.shape, jnp.int32),
        pltpu.SemaphoreType.DMA((PARTS,)),
        pltpu.SemaphoreType.DMA(()),
    ]
    outs = [sds((1,) + w.shape), sds((lat_dev, depth, cells))]
    body = functools.partial(last_w_kernel, False)
    return stencil_call(body, specs, args, outs, [HBM, VMEM], scratch)


def count_kernel(cells_ref, count_ref, outer_ref):
    depth, side, _ = count_ref.shape
    local = cells_ref[...] - (lax.axis_index("slab") * depth - HALO) * (side * side)
    n = local.shape[1]
    row_of = jnp.where(local >= 0, quotient(jnp.maximum(local, 0), side), -1)
    lane_of = remainder(jnp.maximum(local, 0), side)
    lanes = lax.broadcasted_iota(jnp.int32, (side, n), 0)
    lane_hot = jnp.where(lanes == lane_of, 1.0, 0.0).astype(jnp.bfloat16)
    for z in range(depth + 2 * HALO):
        row_hot = jnp.where(lanes + z * side == row_of, 1.0, 0.0).astype(jnp.bfloat16)
        plane = lax.dot_general(row_hot, lane_hot, (((1,), (1,)), ((), ())), preferred_element_type=F32)
        if z < HALO:
            outer_ref[0, z] = plane
        elif z < HALO + depth:
            count_ref[z - HALO] = plane
        else:
            outer_ref[1, z - HALO - depth] = plane


def count_call(cells, depth, side):
    return pl.pallas_call(
        count_kernel,
        out_shape=[sds((depth, side, side)), sds((2, HALO, side, side))],
        in_specs=[VMEM],
        out_specs=[VMEM, VMEM],
        compiler_params=params(8),
        name="count",
    )(cells)


def gather_records(before, cells_smem, cells_ref, fields, out_ref, rows_ref):
    depth, side, _ = fields[0].shape
    n = cells_ref.shape[1]
    total = depth * side * side
    start = lax.axis_index("slab") * total
    local = cells_ref[...] - start
    mine = (local >= 0) & (local < total)
    lane_of = jnp.where(mine, remainder(jnp.maximum(local, 0), side), -1)
    lanes = lax.broadcasted_iota(jnp.int32, (side, n), 0)
    hit = lanes == lane_of
    flat = [field_ref.reshape(depth * side, side) for field_ref in fields]

    def gather(r, carry):
        cell = jnp.clip(cells_smem[0, r] - start, 0, total - 1)
        row = quotient(cell, side)
        for step, field_ref in enumerate(flat):
            rows_ref[step, pl.ds(r, 1), :] = field_ref[pl.ds(row, 1), :]
        return carry

    lax.fori_loop(0, n, gather, 0, unroll=32)
    for step in range(len(fields)):
        turned = rows_ref[step].T
        out_ref[pl.ds(before + step, 1), :] = jnp.sum(jnp.where(hit, turned, 0.0), axis=0, keepdims=True)


def record_kernel(before, cells_smem, cells_ref, *rest):
    if before:
        early_ref, rest = rest[0], rest[1:]
    *fields, out_ref, rows_ref = rest
    if before:
        out_ref[pl.ds(0, before), :] = early_ref[...]
    gather_records(before, cells_smem, cells_ref, fields, out_ref, rows_ref)


def record_call(cells, early, fields):
    side = fields[0].shape[-1]
    n = cells.shape[1]
    before = 0 if early is None else early.shape[0]
    args = [cells, cells] + ([early] if before else []) + list(fields)
    return pl.pallas_call(
        functools.partial(record_kernel, before),
        out_shape=sds((before + len(fields), n)),
        in_specs=[SMEM] + [VMEM] * (len(args) - 1),
        out_specs=VMEM,
        scratch_shapes=[pltpu.VMEM((len(fields), n, side), F32)],
        compiler_params=params(8),
    )(*args)


def total_kernel(*refs):
    *parts, out_ref = refs
    total = parts[0][...]
    for part in parts[1:]:
        total = total + part[...]
    for step in range(total.shape[0]):
        out_ref[step] = total[step : step + 1]


def total_call(parts):
    steps, n = parts[0].shape
    return pl.pallas_call(
        total_kernel,
        out_shape=sds((steps, 1, n)),
        in_specs=[VMEM] * len(parts),
        out_specs=VMEM,
        compiler_params=params(4),
        name="total",
    )(*parts)


def swap_segments(parts, segment):
    count = len(parts)
    lanes = count * segment
    lane = lax.broadcasted_iota(jnp.int32, parts[0].shape, 1)
    parts = list(parts)
    bit = count // 2
    while bit:
        low = lax.rem(lax.div(lane, bit * segment), 2) == 0
        for a in range(count):
            if not a & bit:
                first, second = parts[a], parts[a + bit]
                parts[a] = jnp.where(low, first, pltpu.roll(second, bit * segment, 1))
                parts[a + bit] = jnp.where(low, pltpu.roll(first, lanes - bit * segment, 1), second)
        bit //= 2
    return parts


def partner_of(me, k, count):
    if count & (count - 1) == 0:
        return lax.bitwise_xor(me, k)
    return lax.rem(k - me + count, count)


def round_of(me, other, count):
    if count & (count - 1) == 0:
        return lax.bitwise_xor(me, other)
    return lax.rem(me + other, count)


def pack_kernel(aperture_hbm, slot_hbm, tiles_hbm, *rest):
    *outs, table_ref, aperture_ref, slot_ref, tiles_ref, sems = rest
    pairs = ((aperture_hbm, aperture_ref), (slot_hbm, slot_ref), (tiles_hbm, tiles_ref))
    copies = [pltpu.make_async_copy(a, b, sems.at[i]) for i, (a, b) in enumerate(pairs)]
    for copy in copies:
        copy.start()
    lat_dev = tiles_ref.shape[0]
    n_shot = len(outs)
    capacity = outs[0].shape[0]
    me = lax.axis_index("shot")
    n_tiles = aperture_ref.shape[1]
    copies[0].wait()
    copies[1].wait()

    def shot(s, carry):
        for r in range(capacity):
            table_ref[s * (capacity + 1) + r] = 0
        seen = jnp.int32(0)
        for p in range(n_tiles):
            slot = slot_ref[aperture_ref[s, p]]
            mine = quotient(slot, lat_dev) == me

            @pl.when(mine)
            def _():
                table_ref[s * (capacity + 1) + seen] = remainder(slot, lat_dev)

            seen = seen + mine.astype(jnp.int32)
        table_ref[s * (capacity + 1) + capacity] = seen
        return carry

    lax.fori_loop(0, n_shot, shot, 0)
    copies[2].wait()
    for k in range(n_shot):
        base = partner_of(me, k, n_shot) * (capacity + 1)
        for r in range(capacity):
            outs[k][r] = tiles_ref[table_ref[base + r]]


def pack_call(aperture, tile_slot, model_tiles, capacity):
    n_shot = aperture.shape[0]
    _, depth, cells = model_tiles.shape
    *blocks, table = pl.pallas_call(
        pack_kernel,
        out_shape=[sds((capacity, depth, cells))] * n_shot + [sds((n_shot * (capacity + 1),), jnp.int32)],
        in_specs=[HBM, HBM, HBM],
        out_specs=[VMEM] * n_shot + [SMEM],
        scratch_shapes=[
            pltpu.SMEM(aperture.shape, jnp.int32),
            pltpu.SMEM(tile_slot.shape, jnp.int32),
            pltpu.VMEM(model_tiles.shape, F32),
            pltpu.SemaphoreType.DMA((3,)),
        ],
        compiler_params=params(8),
        name="pack",
    )(aperture, tile_slot, model_tiles)
    return blocks, table


def places(aperture_ref, slot_ref, lat_dev, n_shot, capacity, seen_ref, place_ref):
    me = lax.axis_index("shot")
    for h in range(n_shot):
        seen_ref[h] = 0

    def tile(p, carry):
        holder = quotient(slot_ref[aperture_ref[me, p]], lat_dev)
        rank = seen_ref[holder]
        seen_ref[holder] = rank + 1
        place_ref[p] = round_of(me, holder, n_shot) * capacity + rank
        return carry

    lax.fori_loop(0, aperture_ref.shape[1], tile, 0)


def perturb_kernel(lat_dev, tile_side, aperture_ref, slot_ref, *rest):
    *blocks, out_ref, tiles_ref, seen_ref, place_ref = rest
    n_shot = len(blocks)
    capacity, depth, cells = blocks[0].shape
    side = out_ref.shape[1]
    across = side // tile_side
    flat_ref = out_ref.reshape(depth * side, side)
    places(aperture_ref, slot_ref, lat_dev, n_shot, capacity, seen_ref, place_ref)
    for k in range(n_shot):
        tiles_ref[pl.ds(k * capacity, capacity)] = blocks[k][...]

    def tile_row(i, carry):
        for high in range(cells // side):
            parts = [tiles_ref[place_ref[i * across + j], :, pl.ds(high * side, side)] for j in range(across)]
            for low, part in enumerate(swap_segments(parts, tile_side)):
                flat_ref[pl.ds(i * tile_side + high * across + low, depth, stride=side), :] = part
        return carry

    lax.fori_loop(0, across, tile_row, 0)


def pack_back(lat_dev, tile_side, aperture_ref, slot_ref, corr_ref, blocks, tiles_ref, seen_ref, place_ref):
    n_shot = len(blocks)
    capacity, depth, cells = blocks[0].shape
    side = corr_ref.shape[1]
    across = side // tile_side
    flat_ref = corr_ref.reshape(depth * side, side)
    places(aperture_ref, slot_ref, lat_dev, n_shot, capacity, seen_ref, place_ref)
    tiles_ref[...] = jnp.zeros(tiles_ref.shape, F32)

    def tile_row(i, carry):
        for high in range(cells // side):
            parts = [
                flat_ref[pl.ds(i * tile_side + high * across + low, depth, stride=side), :] for low in range(across)
            ]
            for j, part in enumerate(swap_segments(parts, tile_side)):
                tiles_ref[place_ref[i * across + j], :, pl.ds(high * side, side)] = part
        return carry

    lax.fori_loop(0, across, tile_row, 0)
    for k in range(n_shot):
        blocks[k][...] = tiles_ref[pl.ds(k * capacity, capacity)]


def tile_scratch(n_shot, capacity, depth, cells, n_tiles):
    return [
        pltpu.VMEM((n_shot * capacity, depth, cells), F32),
        pltpu.SMEM((n_shot,), jnp.int32),
        pltpu.SMEM((n_tiles,), jnp.int32),
    ]


def perturb_call(aperture, tile_slot, blocks, side, lat_dev, tile_side):
    capacity, depth, cells = blocks[0].shape
    return pl.pallas_call(
        functools.partial(perturb_kernel, lat_dev, tile_side),
        out_shape=sds((depth, side, side)),
        in_specs=[SMEM, SMEM] + [VMEM] * len(blocks),
        out_specs=VMEM,
        scratch_shapes=tile_scratch(len(blocks), capacity, depth, cells, aperture.shape[1]),
        compiler_params=params(8),
        name="perturb",
    )(aperture, tile_slot, *blocks)


def sum_tiles(table_ref, blocks, out_ref):
    n_shot = len(blocks)
    capacity = blocks[0].shape[0]
    out_ref[...] = jnp.zeros(out_ref.shape, F32)
    for k in range(n_shot):
        base = partner_of(lax.axis_index("shot"), k, n_shot) * (capacity + 1)
        for r in range(capacity):

            @pl.when(r < table_ref[base + capacity])
            def _():
                slot = table_ref[base + r]
                out_ref[slot] = out_ref[slot] + blocks[k][r]


def swap(edges):
    count = lax.axis_size("slab")
    shots = lax.axis_size("shot")
    got = []
    for start, edge in enumerate(edges):
        pairs = {}
        for shot in range(shots):
            for i in range(count):
                other = i + 1 if (i - start) % 2 == 0 else i - 1
                if 0 <= other < count:
                    pairs[shot * count + i] = shot * count + other
                elif shots % 2 == 0:
                    pairs[shot * count + i] = (shot ^ 1) * count + i
        got.append(lax.ppermute(edge, ("shot", "slab"), sorted(pairs.items())))
    return tuple(got)


def edges_kernel(groups, *refs):
    refs = Refs(refs)
    fields = [refs.take(n) for n in groups]
    for group in fields:
        depth = group[0].shape[1]
        low = jnp.where(place()[0] == 1, 0, depth - HALO)
        for out_ref, at in zip(refs.take(2), (low, depth - HALO - low)):
            for index, field_ref in enumerate(group):
                for z in range(HALO):
                    out_ref[index, z] = field_ref[0, at + z]


def first_edges(groups):
    outs = []
    for group in groups:
        outs += [sds((len(group), HALO) + group[0].shape[2:])] * 2
    fields = [field for group in groups for field in group]
    edges = pl.pallas_call(
        functools.partial(edges_kernel, [len(group) for group in groups]),
        out_shape=outs,
        in_specs=[VMEM] * len(fields),
        out_specs=[VMEM] * len(outs),
        compiler_params=params(8),
        name="edges",
    )(*fields)
    return [edges[2 * i : 2 * i + 2] for i in range(len(groups))]


def partners():
    count = lax.axis_size("shot")
    if count & (count - 1) == 0:
        return [[s ^ k for s in range(count)] for k in range(count)]
    return [[(k - s) % count for s in range(count)] for k in range(count)]


def rounds(count):
    return sorted(range(count), key=lambda k: (-(k >> 1).bit_count(), k))


def exchange(blocks):
    got = [None] * len(blocks)
    for k in rounds(len(blocks)):
        block, to = blocks[k], partners()[k]
        moves = [(s, t) for s, t in enumerate(to) if s != t]
        kept = [s for s, t in enumerate(to) if s == t]
        if kept and moves:
            moves = moves + [(s, s) for s in kept]
        got[k] = lax.ppermute(block, "shot", moves) if moves else block
    return got


def slab_sum(part):
    count = lax.axis_size("slab")
    parts = [part]
    for k in range(1, count):
        to = [s ^ k for s in range(count)] if count & (count - 1) == 0 else [(s + k) % count for s in range(count)]
        parts.append(lax.ppermute(part, "slab", list(enumerate(to))))
    return total_call(parts)


def per_device(
    model_tiles,
    background,
    u_prev,
    u_now,
    du_prev,
    du_now,
    w_prev,
    w_now,
    wavelet,
    source_cell,
    receiver_cells,
    aperture,
    tile_slot,
):
    lat_dev, depth, tile_cells = model_tiles.shape
    side = background.shape[-1]
    tile_side = math.isqrt(tile_cells)
    capacity = aperture.shape[1] // 4
    steps = wavelet.shape[1]
    speed = background[0]
    u, d, w = u_now[0], du_now[0], w_now[0]
    up, dp, wp = u_prev[0], du_prev[0], w_prev[0]

    tiling = (aperture, tile_slot, lat_dev, tile_side)
    u_edges, dw_edges = first_edges([[u_now], [du_now, w_now]])
    u_halo = swap(u_edges)
    dw_halo = swap(dw_edges)
    outgoing, table = pack_call(aperture, tile_slot, model_tiles, capacity)
    incoming = exchange(outgoing)
    count, outer = count_call(receiver_cells, depth, side)
    perturb = perturb_call(aperture, tile_slot, incoming, side, lat_dev, tile_side)

    u_next, lap, corr, *edges = u_call(0, False, wavelet, source_cell, u, up, u_halo, speed, w, None, *tiling)
    u_halo = swap(edges)
    bare, *edges = w_bare_call(w, wp, dw_halo, 1, speed)
    w_halo = swap(edges)
    d_next, w_next, *edges = d_call(d, dp, dw_halo, 0, speed, perturb, lap, bare, count)
    d_halo = swap(edges)
    traces = None
    for step in range(1, steps - 1):
        traces = record_call(receiver_cells, traces, [d_next])
        u, up, d, dp, w, wp = u_next, u, d_next, d, w_next, w
        u_next, lap, corr, *edges = u_call(step, False, wavelet, source_cell, u, up, u_halo, speed, w, corr, *tiling)
        u_halo = swap(edges)
        d_next, w_next, *edges = dw_call(
            d, dp, w, wp, d_halo, w_halo, speed, perturb, lap, count, outer if step == 1 else None
        )
        d_halo = swap(edges[:2])
        w_halo = swap(edges[2:])
    u, up, d, dp, w, wp = u_next, u, d_next, d, w_next, w
    step = steps - 1
    u_final, lap, *returning = u_call(step, True, wavelet, source_cell, u, up, u_halo, speed, w, corr, *tiling)
    arrived = exchange(returning)
    d_final, d_next, traces = last_d_call(step, d, dp, d_halo, speed, perturb, lap, receiver_cells, traces)
    traces = slab_sum(traces)
    w_final, sensitivity = last_w_call(w, wp, w_halo, speed, count, d_next, table, arrived, lat_dev)
    return (sensitivity, u_final, d_final, w_final, jnp.transpose(traces, (1, 0, 2)))


def solution(mesh):
    field = P("shot", "slab", None, None)
    tiles = P("shot", "slab", None)
    in_specs = (tiles,) + (field,) * 7 + (P("shot", None), P("shot"), P("shot", None), P(), P())
    out_specs = (tiles, field, field, field, P("shot", None, None))


    return jax.shard_map(per_device, mesh=mesh, in_specs=in_specs, out_specs=out_specs, check_vma=False)
```

profile of v0, /device:TPU:0, one launch (start us, length us, event | category | flops | bytes accessed | tf_op | source)
XLA Modules:
  0.0 94.4 jit_solution(18131537670079824086)
XLA Ops:
  2.9 1.7 %pack.1 = (f32[4,8,1024]{2,1,0:T(8,128)S(1)}, f32[4,8,1024]{2,1,0:T(8,128)S(1)}, f32[4,8,1024]{2,1,0:T(8,128)S(1)}, f32[4,8,1024]{2,1,0:T(8,128)S(1)}, f32[4,8,1...) custom-call(s32[8,16]{1,0:T(8,128)S(1)} %copy-done.11, ...), custom_call_target="tpu_custom_call" | custom-call | tf_op jit(solution)/shard_map/pack/pallas_call | solution.py:596
  5.2 2.6 %collective-permute-start.3 = (f32[4,8,1024]{2,1,0:T(8,128)S(1)}, f32[4,8,1024]{2,1,0:T(8,128)S(1)}, u32[]{:S(2)}, u32[]{:S(2)}) collective-permute-start(f32[4,8,1024]{2,1,0:T(8,128)S(1)} %get-tuple-element.62), channel_id=1, source_target_pairs={{0,8},{4,12},{8,0},{12,4},{16,24},{20,28},{24,16},{28,20},{1,9},{5... | collective-permute-start | bytes 393224 | tf_op jit(solution)/shard_map/ppermute | solution.py:771
  11.0 1.6 %collective-permute-start = (f32[2,4,128,128]{3,2,1,0:T(8,128)S(1)}, f32[2,4,128,128]{3,2,1,0:T(8,128)S(1)}, u32[]{:S(2)}, u32[]{:S(2)}) collective-permute-start(f32[2,4,128,128]{3,2,1,0:T(8,128)S(1)} %get-tuple-element.58), channel_id=1, source_target_pairs={{0,1},{1,0},{2,3},{3,2},{4,5},{5,4},{6,7},{7,6},{8,9},{9,8},{10,11... | collective-permute-start | bytes 1572872 | tf_op jit(solution)/shard_map/ppermute | solution.py:720
  14.8 2.9 %collective-permute-done.4.rest_3_ = f32[4,8,1024]{2,1,0:T(8,128)S(1)} collective-permute-done((f32[4,8,1024]{2,1,0:T(8,128)S(1)}, f32[4,8,1024]{2,1,0:T(8,128)S(1)}, u32[]{:S(2)}, u32[]{:S(2)}) %collective-permute-start.4) | collective-permute-done | bytes 131104 | tf_op jit(solution)/shard_map/ppermute | solution.py:771
  19.6 3.5 %collective-permute-start.9 = (f32[1,4,128,128]{3,2,1,0:T(8,128)S(1)}, f32[1,4,128,128]{3,2,1,0:T(8,128)S(1)}, u32[]{:S(2)}, u32[]{:S(2)}) collective-permute-start(f32[1,4,128,128]{3,2,1,0:T(8,128)S(1)} %get-tuple-element.68), channel_id=1, source_target_pairs={{0,1},{1,0},{2,3},{3,2},{4,5},{5,4},{6,7},{7,6},{8,9},{9,8},{10,11... | collective-permute-start | bytes 786440 | tf_op jit(solution)/shard_map/ppermute | solution.py:720
  23.1 1.8 %collective-permute-done.7.rest_6_ = f32[4,8,1024]{2,1,0:T(8,128)S(1)} collective-permute-done((f32[4,8,1024]{2,1,0:T(8,128)S(1)}, f32[4,8,1024]{2,1,0:T(8,128)S(1)}, u32[]{:S(2)}, u32[]{:S(2)}) %collective-permute-start.7) | collective-permute-done | bytes 131104 | tf_op jit(solution)/shard_map/ppermute | solution.py:771
  24.9 1.7 %collective-permute-start.8 = (f32[4,8,1024]{2,1,0:T(8,128)S(1)}, f32[4,8,1024]{2,1,0:T(8,128)S(1)}, u32[]{:S(2)}, u32[]{:S(2)}) collective-permute-start(f32[4,8,1024]{2,1,0:T(8,128)S(1)} %get-tuple-element.67), channel_id=1, source_target_pairs={{0,28},{4,24},{8,20},{12,16},{16,12},{20,8},{24,4},{28,0},{1,29},{... | collective-permute-start | bytes 393224 | tf_op jit(solution)/shard_map/ppermute | solution.py:771
  27.7 3.7 %collective-permute-done.8.rest_7_ = f32[4,8,1024]{2,1,0:T(8,128)S(1)} collective-permute-done((f32[4,8,1024]{2,1,0:T(8,128)S(1)}, f32[4,8,1024]{2,1,0:T(8,128)S(1)}, u32[]{:S(2)}, u32[]{:S(2)}) %collective-permute-start.8) | collective-permute-done | bytes 131104 | tf_op jit(solution)/shard_map/ppermute | solution.py:771
  31.5 1.7 %perturb.1.perturb_ref.refs_5_ = f32[8,128,128]{2,1,0:T(8,128)S(1)} custom-call(s32[8,16]{1,0:T(8,128)S(1)} %copy-done.12, s32[64]{0:T(128)S(1)} %copy-done.15, f32[4,8,1024]{2,1,0:T(8,128)S(1)} %get-tuple-element.60.rest_0_, f32[4,8,1024]{2,1,0:T(8,128)S(1)} %collective-permute-done.2.rest_1_, f32[4,8,1024]{2,1,0:T(8,128)S(1)} %collective-permute-done.3.rest_2_, ...), custom_call_target="tpu_custom_call" | custom-call | tf_op jit(solution)/shard_map/perturb/pallas_call | solution.py:682
  35.1 2.8 %collective-permute-start.11 = (f32[1,4,128,128]{3,2,1,0:T(8,128)S(1)}, f32[1,4,128,128]{3,2,1,0:T(8,128)S(1)}, u32[]{:S(2)}, u32[]{:S(2)}) collective-permute-start(f32[1,4,128,128]{3,2,1,0:T(8,128)S(1)} %get-tuple-element.76), channel_id=1, source_target_pairs={{0,1},{1,0},{2,3},{3,2},{4,5},{5,4},{6,7},{7,6},{8,9},{9,8},{10,11... | collective-permute-start | bytes 786440 | tf_op jit(solution)/shard_map/ppermute | solution.py:720
  41.7 2.0 %collective-permute-start.15 = (f32[1,4,128,128]{3,2,1,0:T(8,128)S(1)}, f32[1,4,128,128]{3,2,1,0:T(8,128)S(1)}, u32[]{:S(2)}, u32[]{:S(2)}) collective-permute-start(f32[1,4,128,128]{3,2,1,0:T(8,128)S(1)} %get-tuple-element.82), channel_id=1, source_target_pairs={{0,1},{1,0},{2,3},{3,2},{4,5},{5,4},{6,7},{7,6},{8,9},{9,8},{10,11... | collective-permute-start | bytes 786440 | tf_op jit(solution)/shard_map/ppermute | solution.py:720
  46.4 3.1 %collective-permute-start.21 = (f32[1,4,128,128]{3,2,1,0:T(8,128)S(1)}, f32[1,4,128,128]{3,2,1,0:T(8,128)S(1)}, u32[]{:S(2)}, u32[]{:S(2)}) collective-permute-start(f32[1,4,128,128]{3,2,1,0:T(8,128)S(1)} %get-tuple-element.92), channel_id=1, source_target_pairs={{0,1},{1,0},{2,3},{3,2},{4,5},{5,4},{6,7},{7,6},{8,9},{9,8},{10,11... | collective-permute-start | bytes 786440 | tf_op jit(solution)/shard_map/ppermute | solution.py:720
  50.8 5.6 %collective-permute-done.15.refs_10_ = f32[1,4,128,128]{3,2,1,0:T(8,128)S(1)} collective-permute-done((f32[1,4,128,128]{3,2,1,0:T(8,128)S(1)}, f32[1,4,128,128]{3,2,1,0:T(8,128)S(1)}, u32[]{:S(2)}, u32[]{:S(2)}) %collective-permute-start.15) | collective-permute-done | bytes 262176 | tf_op jit(solution)/shard_map/ppermute | solution.py:720
  56.4 2.8 %shard_map.168 = (f32[8,128,128]{2,1,0:T(8,128)S(1)}, f32[8,128,128]{2,1,0:T(8,128)S(1)}, f32[1,4,128,128]{3,2,1,0:T(8,128)S(1)}, f32[1,4,128,128]{3,2,1,0:T(8,1...) custom-call(f32[8,128,128]{2,1,0:T(8,128)S(1)} %bitcast.12, ...), custom_call_target="tpu_custom_call" | custom-call | tf_op jit(solution)/shard_map/pallas_call | solution.py:337
  59.2 2.2 %collective-permute-done.21.refs_4_ = f32[1,4,128,128]{3,2,1,0:T(8,128)S(1)} collective-permute-done((f32[1,4,128,128]{3,2,1,0:T(8,128)S(1)}, f32[1,4,128,128]{3,2,1,0:T(8,128)S(1)}, u32[]{:S(2)}, u32[]{:S(2)}) %collective-permute-start.21) | collective-permute-done | bytes 262176 | tf_op jit(solution)/shard_map/ppermute | solution.py:720
  61.4 2.5 %shard_map.169 = (f32[1,8,128,128]{3,2,1,0:T(8,128)}, f32[8,128,128]{2,1,0:T(8,128)S(1)}, f32[4,8,1024]{2,1,0:T(8,128)S(1)}, f32[4,8,1024]{2,1,0:T(8,128)S(1)}, ...) custom-call(s32[1]{0:T(128)S(6)} %copy.18.refs_0_, ...), custom_call_target="tpu_custom_call" | custom-call | tf_op jit(solution)/shard_map/pallas_call | solution.py:337
  64.0 1.9 %collective-permute-start.19 = (f32[1,4,128,128]{3,2,1,0:T(8,128)S(1)}, f32[1,4,128,128]{3,2,1,0:T(8,128)S(1)}, u32[]{:S(2)}, u32[]{:S(2)}) collective-permute-start(f32[1,4,128,128]{3,2,1,0:T(8,128)S(1)} %get-tuple-element.89), channel_id=1, source_target_pairs={{0,1},{1,0},{2,3},{3,2},{4,5},{5,4},{6,7},{7,6},{8,9},{9,8},{10,11... | collective-permute-start | bytes 786440 | tf_op jit(solution)/shard_map/ppermute | solution.py:720
  66.1 1.6 %collective-permute-start.24 = (f32[4,8,1024]{2,1,0:T(8,128)S(1)}, f32[4,8,1024]{2,1,0:T(8,128)S(1)}, u32[]{:S(2)}, u32[]{:S(2)}) collective-permute-start(f32[4,8,1024]{2,1,0:T(8,128)S(1)} %get-tuple-element.100), channel_id=1, source_target_pairs={{0,8},{4,12},{8,0},{12,4},{16,24},{20,28},{24,16},{28,20},{1,9},{5... | collective-permute-start | bytes 393224 | tf_op jit(solution)/shard_map/ppermute | solution.py:771
  69.2 3.2 %collective-permute-done.24.refs_10_ = f32[4,8,1024]{2,1,0:T(8,128)S(1)} collective-permute-done((f32[4,8,1024]{2,1,0:T(8,128)S(1)}, f32[4,8,1024]{2,1,0:T(8,128)S(1)}, u32[]{:S(2)}, u32[]{:S(2)}) %collective-permute-start.24) | collective-permute-done | bytes 131104 | tf_op jit(solution)/shard_map/ppermute | solution.py:771
  75.8 1.6 %collective-permute-start.28 = (f32[4,8,1024]{2,1,0:T(8,128)S(1)}, f32[4,8,1024]{2,1,0:T(8,128)S(1)}, u32[]{:S(2)}, u32[]{:S(2)}) collective-permute-start(f32[4,8,1024]{2,1,0:T(8,128)S(1)} %get-tuple-element.104), channel_id=1, source_target_pairs={{0,24},{4,28},{8,16},{12,20},{16,8},{20,12},{24,0},{28,4},{1,25},{... | collective-permute-start | bytes 393224 | tf_op jit(solution)/shard_map/ppermute | solution.py:771
  79.6 2.1 %shard_map.171 = (f32[1,8,128,128]{3,2,1,0:T(8,128)}, f32[8,128,128]{2,1,0:T(8,128)S(1)}, f32[3,256]{1,0:T(4,128)S(1)}) custom-call(f32[8,128,128]{2,1,0:T(8,128)S(1)} %get-tuple-element.88.refs_0_, f32[8,128,128]{2,1,0:T(8,128)S(1)} %get-tuple-element.73.refs_1_.rest_0_, f32[1,4,128,128]{3,2,1,0:T(8,128)S(1)} %collective-permute-done.19.refs_2_, ...), custom_call_target="tpu_custom_call" | custom-call | tf_op jit(solution)/shard_map/pallas_call | solution.py:337
  81.7 3.9 %collective-permute-done.27.refs_13_ = f32[4,8,1024]{2,1,0:T(8,128)S(1)} collective-permute-done((f32[4,8,1024]{2,1,0:T(8,128)S(1)}, f32[4,8,1024]{2,1,0:T(8,128)S(1)}, u32[]{:S(2)}, u32[]{:S(2)}) %collective-permute-start.27) | collective-permute-done | bytes 131104 | tf_op jit(solution)/shard_map/ppermute | solution.py:771
  88.4 1.6 %collective-permute-start.32 = (f32[3,256]{1,0:T(4,128)S(1)}, f32[3,256]{1,0:T(4,128)S(1)}, u32[]{:S(2)}, u32[]{:S(2)}) collective-permute-start(f32[3,256]{1,0:T(4,128)S(1)} %get-tuple-element.110.refs_0_), channel_id=1, source_target_pairs={{0,3},{1,2},{2,1},{3,0},{4,7},{5,6},{6,5},{7,4},{8,11},{9,10},{10,... | collective-permute-start | bytes 9224 | tf_op jit(solution)/shard_map/ppermute | solution.py:780
  90.0 2.6 %shard_map.172 = (f32[1,8,128,128]{3,2,1,0:T(8,128)}, f32[8,8,1024]{2,1,0:T(8,128)}) custom-call(f32[8,128,128]{2,1,0:T(8,128)S(1)} %get-tuple-element.85.refs_7_.refs_0_, f32[8,128,128]{2,1,0:T(8,128)S(1)} %get-tuple-element.74.refs_7_.refs_3_.refs_1_, f32[1,4,128,128]{3,2,1,0:T(8,128)S(1)} %collective-permute-done.17.refs_2_, ...), custom_call_target="tpu_custom_call" | custom-call | tf_op jit(solution)/shard_map/pallas_call | solution.py:337
  (90 shorter events, 31.9 us)
Async XLA Ops:
  4.7 8.6 %collective-permute-start.2 = (f32[4,8,1024]{2,1,0:T(8,128)S(1)}, f32[4,8,1024]{2,1,0:T(8,128)S(1)}, u32[]{:S(2)}, u32[]{:S(2)}) collective-permute-start(f32[4,8,1024]{2,1,0:T(8,128)S(1)} %get-tuple-element.61), channel_id=1, source_target_pairs={{0,4},{4,0},{8,12},{12,8},{16,20},{20,16},{24,28},{28,24},{1,5},{5... | collective-permute-start | bytes 393224 | tf_op jit(solution)/shard_map/ppermute | solution.py:771
  5.2 9.6 %collective-permute-start.3 = (f32[4,8,1024]{2,1,0:T(8,128)S(1)}, f32[4,8,1024]{2,1,0:T(8,128)S(1)}, u32[]{:S(2)}, u32[]{:S(2)}) collective-permute-start(f32[4,8,1024]{2,1,0:T(8,128)S(1)} %get-tuple-element.62), channel_id=1, source_target_pairs={{0,8},{4,12},{8,0},{12,4},{16,24},{20,28},{24,16},{28,20},{1,9},{5... | collective-permute-start | bytes 393224 | tf_op jit(solution)/shard_map/ppermute | solution.py:771
  11.0 27.0 %collective-permute-start = (f32[2,4,128,128]{3,2,1,0:T(8,128)S(1)}, f32[2,4,128,128]{3,2,1,0:T(8,128)S(1)}, u32[]{:S(2)}, u32[]{:S(2)}) collective-permute-start(f32[2,4,128,128]{3,2,1,0:T(8,128)S(1)} %get-tuple-element.58), channel_id=1, source_target_pairs={{0,1},{1,0},{2,3},{3,2},{4,5},{5,4},{6,7},{7,6},{8,9},{9,8},{10,11... | collective-permute-start | bytes 1572872 | tf_op jit(solution)/shard_map/ppermute | solution.py:720
  12.6 25.3 %collective-permute-start.1 = (f32[2,4,128,128]{3,2,1,0:T(8,128)S(1)}, f32[2,4,128,128]{3,2,1,0:T(8,128)S(1)}, u32[]{:S(2)}, u32[]{:S(2)}) collective-permute-start(f32[2,4,128,128]{3,2,1,0:T(8,128)S(1)} %get-tuple-element.59), channel_id=1, source_target_pairs={{0,4},{1,2},{2,1},{3,7},{4,0},{5,6},{6,5},{7,3},{8,12},{9,10},{10,... | collective-permute-start | bytes 1572872 | tf_op jit(solution)/shard_map/ppermute | solution.py:720
  14.8 8.2 %collective-permute-start.6 = (f32[4,8,1024]{2,1,0:T(8,128)S(1)}, f32[4,8,1024]{2,1,0:T(8,128)S(1)}, u32[]{:S(2)}, u32[]{:S(2)}) collective-permute-start(f32[4,8,1024]{2,1,0:T(8,128)S(1)} %get-tuple-element.65), channel_id=1, source_target_pairs={{0,20},{4,16},{8,28},{12,24},{16,4},{20,0},{24,12},{28,8},{1,21},{... | collective-permute-start | bytes 393224 | tf_op jit(solution)/shard_map/ppermute | solution.py:771
  17.8 7.1 %collective-permute-start.7 = (f32[4,8,1024]{2,1,0:T(8,128)S(1)}, f32[4,8,1024]{2,1,0:T(8,128)S(1)}, u32[]{:S(2)}, u32[]{:S(2)}) collective-permute-start(f32[4,8,1024]{2,1,0:T(8,128)S(1)} %get-tuple-element.66), channel_id=1, source_target_pairs={{0,24},{4,28},{8,16},{12,20},{16,8},{20,12},{24,0},{28,4},{1,25},{... | collective-permute-start | bytes 393224 | tf_op jit(solution)/shard_map/ppermute | solution.py:771
  19.6 13.6 %collective-permute-start.9 = (f32[1,4,128,128]{3,2,1,0:T(8,128)S(1)}, f32[1,4,128,128]{3,2,1,0:T(8,128)S(1)}, u32[]{:S(2)}, u32[]{:S(2)}) collective-permute-start(f32[1,4,128,128]{3,2,1,0:T(8,128)S(1)} %get-tuple-element.68), channel_id=1, source_target_pairs={{0,1},{1,0},{2,3},{3,2},{4,5},{5,4},{6,7},{7,6},{8,9},{9,8},{10,11... | collective-permute-start | bytes 786440 | tf_op jit(solution)/shard_map/ppermute | solution.py:720
  23.1 10.1 %collective-permute-start.10 = (f32[1,4,128,128]{3,2,1,0:T(8,128)S(1)}, f32[1,4,128,128]{3,2,1,0:T(8,128)S(1)}, u32[]{:S(2)}, u32[]{:S(2)}) collective-permute-start(f32[1,4,128,128]{3,2,1,0:T(8,128)S(1)} %get-tuple-element.69), channel_id=1, source_target_pairs={{0,4},{1,2},{2,1},{3,7},{4,0},{5,6},{6,5},{7,3},{8,12},{9,10},{10,... | collective-permute-start | bytes 786440 | tf_op jit(solution)/shard_map/ppermute | solution.py:720
  35.1 10.0 %collective-permute-start.11 = (f32[1,4,128,128]{3,2,1,0:T(8,128)S(1)}, f32[1,4,128,128]{3,2,1,0:T(8,128)S(1)}, u32[]{:S(2)}, u32[]{:S(2)}) collective-permute-start(f32[1,4,128,128]{3,2,1,0:T(8,128)S(1)} %get-tuple-element.76), channel_id=1, source_target_pairs={{0,1},{1,0},{2,3},{3,2},{4,5},{5,4},{6,7},{7,6},{8,9},{9,8},{10,11... | collective-permute-start | bytes 786440 | tf_op jit(solution)/shard_map/ppermute | solution.py:720
  38.0 7.2 %collective-permute-start.12 = (f32[1,4,128,128]{3,2,1,0:T(8,128)S(1)}, f32[1,4,128,128]{3,2,1,0:T(8,128)S(1)}, u32[]{:S(2)}, u32[]{:S(2)}) collective-permute-start(f32[1,4,128,128]{3,2,1,0:T(8,128)S(1)} %get-tuple-element.77), channel_id=1, source_target_pairs={{0,4},{1,2},{2,1},{3,7},{4,0},{5,6},{6,5},{7,3},{8,12},{9,10},{10,... | collective-permute-start | bytes 786440 | tf_op jit(solution)/shard_map/ppermute | solution.py:720
  40.6 10.2 %collective-permute-start.13 = (f32[1,4,128,128]{3,2,1,0:T(8,128)S(1)}, f32[1,4,128,128]{3,2,1,0:T(8,128)S(1)}, u32[]{:S(2)}, u32[]{:S(2)}) collective-permute-start(f32[1,4,128,128]{3,2,1,0:T(8,128)S(1)} %get-tuple-element.80), channel_id=1, source_target_pairs={{0,1},{1,0},{2,3},{3,2},{4,5},{5,4},{6,7},{7,6},{8,9},{9,8},{10,11... | collective-permute-start | bytes 786440 | tf_op jit(solution)/shard_map/ppermute | solution.py:720
  41.7 9.1 %collective-permute-start.14 = (f32[1,4,128,128]{3,2,1,0:T(8,128)S(1)}, f32[1,4,128,128]{3,2,1,0:T(8,128)S(1)}, u32[]{:S(2)}, u32[]{:S(2)}) collective-permute-start(f32[1,4,128,128]{3,2,1,0:T(8,128)S(1)} %get-tuple-element.81), channel_id=1, source_target_pairs={{0,4},{1,2},{2,1},{3,7},{4,0},{5,6},{6,5},{7,3},{8,12},{9,10},{10,... | collective-permute-start | bytes 786440 | tf_op jit(solution)/shard_map/ppermute | solution.py:720
  41.7 14.7 %collective-permute-start.15 = (f32[1,4,128,128]{3,2,1,0:T(8,128)S(1)}, f32[1,4,128,128]{3,2,1,0:T(8,128)S(1)}, u32[]{:S(2)}, u32[]{:S(2)}) collective-permute-start(f32[1,4,128,128]{3,2,1,0:T(8,128)S(1)} %get-tuple-element.82), channel_id=1, source_target_pairs={{0,1},{1,0},{2,3},{3,2},{4,5},{5,4},{6,7},{7,6},{8,9},{9,8},{10,11... | collective-permute-start | bytes 786440 | tf_op jit(solution)/shard_map/ppermute | solution.py:720
  45.1 11.2 %collective-permute-start.16 = (f32[1,4,128,128]{3,2,1,0:T(8,128)S(1)}, f32[1,4,128,128]{3,2,1,0:T(8,128)S(1)}, u32[]{:S(2)}, u32[]{:S(2)}) collective-permute-start(f32[1,4,128,128]{3,2,1,0:T(8,128)S(1)} %get-tuple-element.83), channel_id=1, source_target_pairs={{0,4},{1,2},{2,1},{3,7},{4,0},{5,6},{6,5},{7,3},{8,12},{9,10},{10,... | collective-permute-start | bytes 786440 | tf_op jit(solution)/shard_map/ppermute | solution.py:720
  46.4 15.0 %collective-permute-start.21 = (f32[1,4,128,128]{3,2,1,0:T(8,128)S(1)}, f32[1,4,128,128]{3,2,1,0:T(8,128)S(1)}, u32[]{:S(2)}, u32[]{:S(2)}) collective-permute-start(f32[1,4,128,128]{3,2,1,0:T(8,128)S(1)} %get-tuple-element.92), channel_id=1, source_target_pairs={{0,1},{1,0},{2,3},{3,2},{4,5},{5,4},{6,7},{7,6},{8,9},{9,8},{10,11... | collective-permute-start | bytes 786440 | tf_op jit(solution)/shard_map/ppermute | solution.py:720
  50.7 10.7 %collective-permute-start.22 = (f32[1,4,128,128]{3,2,1,0:T(8,128)S(1)}, f32[1,4,128,128]{3,2,1,0:T(8,128)S(1)}, u32[]{:S(2)}, u32[]{:S(2)}) collective-permute-start(f32[1,4,128,128]{3,2,1,0:T(8,128)S(1)} %get-tuple-element.93), channel_id=1, source_target_pairs={{0,4},{1,2},{2,1},{3,7},{4,0},{5,6},{6,5},{7,3},{8,12},{9,10},{10,... | collective-permute-start | bytes 786440 | tf_op jit(solution)/shard_map/ppermute | solution.py:720
  64.0 11.8 %collective-permute-start.19 = (f32[1,4,128,128]{3,2,1,0:T(8,128)S(1)}, f32[1,4,128,128]{3,2,1,0:T(8,128)S(1)}, u32[]{:S(2)}, u32[]{:S(2)}) collective-permute-start(f32[1,4,128,128]{3,2,1,0:T(8,128)S(1)} %get-tuple-element.89), channel_id=1, source_target_pairs={{0,1},{1,0},{2,3},{3,2},{4,5},{5,4},{6,7},{7,6},{8,9},{9,8},{10,11... | collective-permute-start | bytes 786440 | tf_op jit(solution)/shard_map/ppermute | solution.py:720
  65.9 11.5 %collective-permute-start.20 = (f32[1,4,128,128]{3,2,1,0:T(8,128)S(1)}, f32[1,4,128,128]{3,2,1,0:T(8,128)S(1)}, u32[]{:S(2)}, u32[]{:S(2)}) collective-permute-start(f32[1,4,128,128]{3,2,1,0:T(8,128)S(1)} %get-tuple-element.90), channel_id=1, source_target_pairs={{0,4},{1,2},{2,1},{3,7},{4,0},{5,6},{6,5},{7,3},{8,12},{9,10},{10,... | collective-permute-start | bytes 786440 | tf_op jit(solution)/shard_map/ppermute | solution.py:720
  72.4 17.6 %collective-permute-start.17 = (f32[1,4,128,128]{3,2,1,0:T(8,128)S(1)}, f32[1,4,128,128]{3,2,1,0:T(8,128)S(1)}, u32[]{:S(2)}, u32[]{:S(2)}) collective-permute-start(f32[1,4,128,128]{3,2,1,0:T(8,128)S(1)} %get-tuple-element.86), channel_id=1, source_target_pairs={{0,1},{1,0},{2,3},{3,2},{4,5},{5,4},{6,7},{7,6},{8,9},{9,8},{10,11... | collective-permute-start | bytes 786440 | tf_op jit(solution)/shard_map/ppermute | solution.py:720
  74.0 16.0 %collective-permute-start.18 = (f32[1,4,128,128]{3,2,1,0:T(8,128)S(1)}, f32[1,4,128,128]{3,2,1,0:T(8,128)S(1)}, u32[]{:S(2)}, u32[]{:S(2)}) collective-permute-start(f32[1,4,128,128]{3,2,1,0:T(8,128)S(1)} %get-tuple-element.87), channel_id=1, source_target_pairs={{0,4},{1,2},{2,1},{3,7},{4,0},{5,6},{6,5},{7,3},{8,12},{9,10},{10,... | collective-permute-start | bytes 786440 | tf_op jit(solution)/shard_map/ppermute | solution.py:720
  74.5 11.2 %collective-permute-start.27 = (f32[4,8,1024]{2,1,0:T(8,128)S(1)}, f32[4,8,1024]{2,1,0:T(8,128)S(1)}, u32[]{:S(2)}, u32[]{:S(2)}) collective-permute-start(f32[4,8,1024]{2,1,0:T(8,128)S(1)} %get-tuple-element.103), channel_id=1, source_target_pairs={{0,20},{4,16},{8,28},{12,24},{16,4},{20,0},{24,12},{28,8},{1,21},{... | collective-permute-start | bytes 393224 | tf_op jit(solution)/shard_map/ppermute | solution.py:771
  75.8 11.2 %collective-permute-start.28 = (f32[4,8,1024]{2,1,0:T(8,128)S(1)}, f32[4,8,1024]{2,1,0:T(8,128)S(1)}, u32[]{:S(2)}, u32[]{:S(2)}) collective-permute-start(f32[4,8,1024]{2,1,0:T(8,128)S(1)} %get-tuple-element.104), channel_id=1, source_target_pairs={{0,24},{4,28},{8,16},{12,20},{16,8},{20,12},{24,0},{28,4},{1,25},{... | collective-permute-start | bytes 393224 | tf_op jit(solution)/shard_map/ppermute | solution.py:771
  77.4 11.0 %collective-permute-start.29 = (f32[4,8,1024]{2,1,0:T(8,128)S(1)}, f32[4,8,1024]{2,1,0:T(8,128)S(1)}, u32[]{:S(2)}, u32[]{:S(2)}) collective-permute-start(f32[4,8,1024]{2,1,0:T(8,128)S(1)} %get-tuple-element.105), channel_id=1, source_target_pairs={{0,28},{4,24},{8,20},{12,16},{16,12},{20,8},{24,4},{28,0},{1,29},{... | collective-permute-start | bytes 393224 | tf_op jit(solution)/shard_map/ppermute | solution.py:771
  85.6 7.0 %collective-permute-start.30 = (f32[3,256]{1,0:T(4,128)S(1)}, f32[3,256]{1,0:T(4,128)S(1)}, u32[]{:S(2)}, u32[]{:S(2)}) collective-permute-start(f32[3,256]{1,0:T(4,128)S(1)} %get-tuple-element.110.refs_0_), channel_id=1, source_target_pairs={{0,1},{1,0},{2,3},{3,2},{4,5},{5,4},{6,7},{7,6},{8,9},{9,8},{10,11... | collective-permute-start | bytes 9224 | tf_op jit(solution)/shard_map/ppermute | solution.py:780
  (26 other events, 121.0 us)
where the time goes:
time: 94.8 us; the launch traced here: 94.4 us
  starting transfers between devices  37.7 us (40%)
  waiting for transfers between devices  28.1 us (30%)
  Pallas kernels  21 us (22%)
  local copies, waits for them, and re-layouts  6.07 us (6%)
  between operations  1.57 us (2%)
    ppermute x16, starting transfers between devices, swap(): got.append(lax.ppermute(edge, ('shot', 'slab'), sorted(pairs.items())))  17.9 us
    ppermute x14, waiting for transfers between devices, exchange(): got[k] = lax.ppermute(block, 'shot', moves) if moves else block  16.3 us
    ppermute x14, starting transfers between devices, exchange(): got[k] = lax.ppermute(block, 'shot', moves) if moves else block  15.4 us
    pallas_call x8, Pallas kernels, stencil_call(): pl.pallas_call(body, out_shape=outs, in_specs=in_specs, out_specs=kinds,...  15.1 us
    ppermute x16, waiting for transfers between devices, swap(): got.append(lax.ppermute(edge, ('shot', 'slab'), sorted(pairs.items())))  10.6 us
    unnamed x34, local copies, waits for them, and re-layouts  6.07 us
    ppermute x3, starting transfers between devices, slab_sum(): parts.append(lax.ppermute(part, 'slab', list(enumerate(to))))  4.39 us
  transfers between devices with their start and end apart: 33, of which 12 were waited for; matrix products, arithmetic and copies ran while one was open for 0% of the time, Pallas kernels for 17%

commit v1 on v0

--- a/solution.py
+++ b/solution.py
@@ -20,6 +20,10 @@
 
 def params(mib):
     return pltpu.CompilerParams(vmem_limit_bytes=mib * 1024 * 1024)
+
+
+def in_hbm(x):
+    return pltpu.with_memory_space_constraint(x, pltpu.HBM)
 
 
 def sds(shape, dtype=F32):
@@ -65,10 +69,8 @@
     return high, mid, low
 
 
-def prepare(work, now_ref, first_ref, second_ref, index, weights, inject=None):
-    rows_ref, halo_ref, lanes_ref = work
+def prepare_local(rows_ref, lanes_ref, now_ref, weights):
     depth, side, _ = now_ref.shape
-    odd, has_first, has_second = place()
     zeros = jnp.zeros((SUB, side), F32)
     half = depth // 2
     parts = []
@@ -82,6 +84,10 @@
         rows_ref[z, pl.ds(SUB + side, SUB), :] = zeros
         rows_ref[z, pl.ds(SUB, side), :] = now_ref[z]
 
+
+def prepare_halo(halo_ref, first_ref, second_ref, index, inject=None):
+    odd, has_first, has_second = place()
+
     def halo(z, carry):
         halo_ref[1 - odd, z] = jnp.where(has_first, first_ref[index, z], 0.0)
         halo_ref[odd, z] = jnp.where(has_second, second_ref[index, z], 0.0)
@@ -93,6 +99,12 @@
         for end in range(2):
             for z in range(HALO):
                 halo_ref[end, z] = halo_ref[end, z] + outer_ref[end, z] * other_ref[end, z]
+
+
+def prepare(work, now_ref, first_ref, second_ref, index, weights):
+    rows_ref, halo_ref, lanes_ref = work
+    prepare_local(rows_ref, lanes_ref, now_ref, weights)
+    prepare_halo(halo_ref, first_ref, second_ref, index)
 
 
 def each_laplacian(work, now_ref, emit, finish=None, parts=1):
@@ -123,12 +135,35 @@
             finish(part, parts)
 
 
+def halo_space(side):
+    return pltpu.VMEM((2, HALO, side, side), F32)
+
+
 def work_space(depth, side):
     return [
         pltpu.VMEM((depth, side + 2 * SUB, side), F32),
-        pltpu.VMEM((2, HALO, side, side), F32),
+        halo_space(side),
         pltpu.VMEM((depth, side, side), F32),
     ]
+
+
+def ahead_kernel(n, *refs):
+    weights = band_weights(refs[0].shape[-1])
+    for i in range(n):
+        prepare_local(refs[n + 2 * i], refs[n + 2 * i + 1], refs[i], weights)
+
+
+def ahead_call(fields):
+    depth, side, _ = fields[0].shape
+    outs = [sds((depth, side + 2 * SUB, side)), sds((depth, side, side))] * len(fields)
+    res = pl.pallas_call(
+        functools.partial(ahead_kernel, len(fields)),
+        out_shape=outs,
+        in_specs=[VMEM] * len(fields),
+        out_specs=[VMEM] * len(outs),
+        compiler_params=params(16),
+    )(*fields)
+    return [res[2 * i : 2 * i + 2] for i in range(len(fields))]
 
 
 def copy_sends(next_ref, first_ref, second_ref, index):
@@ -156,12 +191,13 @@
         return [self.refs.pop(0) for _ in range(n)]
 
 
-def u_kernel(step, last, tiles, *refs):
+def u_kernel(step, last, ahead, tiles, *refs):
     refs = Refs(refs)
-    source_ref, wavelet_ref, now_ref, prev_ref, ha_ref, hb_ref, speed_ref, w_ref = refs.take(8)
+    source_ref, wavelet_hbm, now_ref, prev_ref, ha_ref, hb_ref, speed_ref, w_in = refs.take(8)
     corr_in = refs.take() if step else None
+    local_work = refs.take(2) if ahead else None
+    tables = refs.take(2) if last else []
     if last:
-        tables = refs.take(2)
         out_ref, lap_ref = refs.take(2)
         blocks = refs.take(tiles[0])
         sends = []
@@ -169,15 +205,32 @@
     else:
         next_ref, lap_ref, corr_ref = refs.take(3)
         sends = refs.take(2)
-    work = refs.take(3)
+    halo_ref = refs.take()
+    if not ahead:
+        local_work = refs.take(2)
+    wavelet_ref, own_sems = refs.take(2)
+    copies = [pltpu.make_async_copy(wavelet_hbm, wavelet_ref, own_sems.at[0])]
+    w_ref = w_in
+    if not step:
+        w_ref = refs.take()
+        half = w_ref.shape[0] // 2
+        for i in range(2):
+            part = pl.ds(i * half, half)
+            copies.append(pltpu.make_async_copy(w_in.at[0, part], w_ref.at[part], own_sems.at[1 + i]))
     if last:
         fetched = refs.take(2)
-        tiles_ref, seen_ref, place_ref, sems, table_sems = refs.take(5)
-        copies = [pltpu.make_async_copy(a, b, table_sems.at[i]) for i, (a, b) in enumerate(zip(tables, fetched))]
-        for copy in copies:
-            copy.start()
+        tiles_ref, seen_ref, place_ref, sems = refs.take(4)
+        for i, (a, b) in enumerate(zip(tables, fetched)):
+            copies.append(pltpu.make_async_copy(a, b, own_sems.at[1 + i]))
+    for copy in copies:
+        copy.start()
     depth, side, _ = now_ref.shape
-    prepare(work, now_ref, ha_ref, hb_ref, 0, band_weights(side))
+    work = (local_work[0], halo_ref, local_work[1])
+    if not ahead:
+        prepare_local(*local_work, now_ref, band_weights(side))
+    prepare_halo(halo_ref, ha_ref, hb_ref, 0)
+    for copy in copies:
+        copy.wait()
 
     def emit(z, block, centre, lap):
         lap_ref[z, block, :] = lap
@@ -191,7 +244,7 @@
     z = quotient(cell, side * side)
     x = remainder(quotient(cell, side), side)
     lane = lax.broadcasted_iota(jnp.int32, (1, side), 1)
-    add = jnp.where((lane == remainder(cell, side)) & mine, wavelet_ref[:, step : step + 1], 0.0)
+    add = jnp.where((lane == remainder(cell, side)) & mine, wavelet_ref[0, step], 0.0)
 
     def finish(part, parts):
         size = side // parts
@@ -208,8 +261,6 @@
     if sends:
         copy_sends(next_ref, *sends, 0)
     if last:
-        for copy in copies:
-            copy.wait()
         pack_back(*tiles[1:], *fetched, corr_ref, blocks, tiles_ref, seen_ref, place_ref)
         for part in range(parts):
             store_out(next_ref, out_ref, sems, part, parts).wait()
@@ -248,14 +299,14 @@
     refs = Refs(refs)
     speed_ref, d_ref, d_prev, w_ref, w_prev, perturb_ref, lap_u_ref, count_ref = refs.take(8)
     d_halo, w_halo = refs.take(2), refs.take(2)
+    d_local, w_local = refs.take(2), refs.take(2)
     outer_ref = refs.take() if bare else None
     d_next, w_next = refs.take(2)
     d_sends, w_sends = refs.take(2), refs.take(2)
-    d_work, w_work = refs.take(3), refs.take(3)
-    _, side, _ = speed_ref.shape
-    weights = band_weights(side)
-    prepare(d_work, d_ref, *d_halo, 0, weights)
-    prepare(w_work, w_ref, *w_halo, 0, weights, (outer_ref, d_work[1]) if bare else None)
+    d_halos, w_halos = refs.take(2)
+    prepare_halo(d_halos, *d_halo, 0)
+    prepare_halo(w_halos, *w_halo, 0, (outer_ref, d_halos) if bare else None)
+    d_work, w_work = (d_local[0], d_halos, d_local[1]), (w_local[0], w_halos, w_local[1])
 
     def emit_d(z, block, centre, lap):
         d_next[z, block, :] = ((2.0 * centre - d_prev[z, block, :]) + speed_ref[z, block, :] * lap) + (
@@ -303,18 +354,12 @@
         store_out(next_ref, out_ref, sems, part, PARTS).wait()
 
 
-def last_w_kernel(bare, *refs):
+def last_w_kernel(*refs):
     refs = Refs(refs)
-    now_ref, prev_ref, ha_ref, hb_ref, speed_ref, count_ref, d_next, table_hbm = refs.take(8)
-    d_halo = refs.take(2) if bare else None
-    outer_ref = refs.take() if bare else None
-    blocks = refs.take(lax.axis_size("shot"))
-    out_ref, sum_ref = refs.take(2)
-    next_ref = refs.take()
+    now_ref, prev_ref, ha_ref, hb_ref, speed_ref, count_ref, d_next = refs.take(7)
+    out_ref, next_ref = refs.take(2)
     work = refs.take(3)
-    table_ref, sems, table_sem = refs.take(3)
-    fetch = pltpu.make_async_copy(table_hbm, table_ref, table_sem)
-    fetch.start()
+    sems = refs.take()
     _, side, _ = now_ref.shape
     prepare(work, now_ref, ha_ref, hb_ref, 0, band_weights(side))
 
@@ -327,8 +372,6 @@
         store_out(next_ref, out_ref, sems, part, parts).start()
 
     each_laplacian(work, now_ref, emit, finish, PARTS)
-    fetch.wait()
-    sum_tiles(table_ref, blocks, sum_ref)
     for part in range(PARTS):
         store_out(next_ref, out_ref, sems, part, PARTS).wait()
 
@@ -339,17 +382,26 @@
     )(*args)
 
 
-def u_call(step, last, wavelet, source, u, u_prev, halo, speed, w, corr, aperture, tile_slot, lat_dev, tile_side):
+def u_call(step, last, wavelet, source, u, u_prev, halo, speed, w, corr, local, aperture, tile_slot, lat_dev, tile_side):
     field = sds(u.shape)
     edge = sds((1, HALO) + u.shape[1:])
-    args = [source, wavelet, u, u_prev, *halo, speed, w] + ([corr] if step else [])
-    specs = [SMEM] + [VMEM] * (len(args) - 1)
-    scratch = work_space(*u.shape[:2])
+    args = [source, in_hbm(wavelet), u, u_prev, *halo, speed, w] + ([corr] if step else [])
+    specs = [SMEM, HBM] + [VMEM] * (len(args) - 2)
+    if not step:
+        args[7], specs[7] = in_hbm(w), HBM
+    ahead = local is not None
+    if ahead:
+        args, specs = args + list(local), specs + [VMEM] * 2
     n_shot, n_tiles = aperture.shape
     cells = tile_side * tile_side
     capacity = n_tiles // 4
+    rows, halos, lanes = work_space(*u.shape[:2])
+    scratch = [halos] + ([] if ahead else [rows, lanes])
+    scratch += [pltpu.SMEM(wavelet.shape, F32), pltpu.SemaphoreType.DMA((3,))]
+    if not step:
+        scratch += [pltpu.VMEM(u.shape, F32)]
     if last:
-        args += [aperture, tile_slot]
+        args += [in_hbm(aperture), in_hbm(tile_slot)]
         specs += [HBM, HBM]
         outs = [sds((1,) + u.shape), field] + [sds((capacity, u.shape[0], cells))] * n_shot
         kinds = [HBM] + [VMEM] * (1 + n_shot)
@@ -358,11 +410,10 @@
             pltpu.SMEM(tile_slot.shape, jnp.int32),
             *tile_scratch(n_shot, capacity, u.shape[0], cells, n_tiles),
             pltpu.SemaphoreType.DMA((PARTS,)),
-            pltpu.SemaphoreType.DMA((2,)),
         ]
     else:
         outs, kinds = [field] * 3 + [edge] * 2, [VMEM] * 5
-    body = functools.partial(u_kernel, step, last, (n_shot, lat_dev, tile_side))
+    body = functools.partial(u_kernel, step, last, ahead, (n_shot, lat_dev, tile_side))
     return stencil_call(body, specs, args, outs, kinds, scratch)
 
 
@@ -381,13 +432,14 @@
     return stencil_call(body, [VMEM] * 9, args, outs, [VMEM] * 4, work_space(*d.shape[:2]))
 
 
-def dw_call(d, d_prev, w, w_prev, d_halo, w_halo, speed, perturb, lap_u, count, outer):
+def dw_call(d, d_prev, w, w_prev, d_halo, w_halo, d_local, w_local, speed, perturb, lap_u, count, outer):
     field, edge = sds(d.shape), sds((1, HALO) + d.shape[1:])
     bare = outer is not None
-    args = [speed, d, d_prev, w, w_prev, perturb, lap_u, count, *d_halo, *w_halo] + ([outer] if bare else [])
+    args = [speed, d, d_prev, w, w_prev, perturb, lap_u, count, *d_halo, *w_halo, *d_local, *w_local]
+    args += [outer] if bare else []
     outs = [field, field] + [edge] * 4
     body = functools.partial(dw_kernel, bare)
-    return stencil_call(body, [VMEM] * len(args), args, outs, [VMEM] * 6, work_space(*d.shape[:2]) * 2)
+    return stencil_call(body, [VMEM] * len(args), args, outs, [VMEM] * 6, [halo_space(d.shape[1])] * 2)
 
 
 def last_d_call(step, d, d_prev, halo, speed, perturb, lap_u, cells, early):
@@ -408,19 +460,10 @@
     return stencil_call(body, specs, args, outs, [HBM, VMEM, VMEM], scratch)
 
 
-def last_w_call(w, w_prev, halo, speed, count, d_next, table, blocks, lat_dev):
-    _, depth, cells = blocks[0].shape
-    args = [w, w_prev, *halo, speed, count, d_next, table, *blocks]
-    specs = [VMEM] * len(args)
-    specs[7] = HBM
-    scratch = [pltpu.VMEM(w.shape, F32)] + work_space(*w.shape[:2]) + [
-        pltpu.SMEM(table.shape, jnp.int32),
-        pltpu.SemaphoreType.DMA((PARTS,)),
-        pltpu.SemaphoreType.DMA(()),
-    ]
-    outs = [sds((1,) + w.shape), sds((lat_dev, depth, cells))]
-    body = functools.partial(last_w_kernel, False)
-    return stencil_call(body, specs, args, outs, [HBM, VMEM], scratch)
+def last_w_call(w, w_prev, halo, speed, count, d_next):
+    args = [w, w_prev, *halo, speed, count, d_next]
+    scratch = [pltpu.VMEM(w.shape, F32)] + work_space(*w.shape[:2]) + [pltpu.SemaphoreType.DMA((PARTS,))]
+    return stencil_call(last_w_kernel, [VMEM] * len(args), args, [sds((1,) + w.shape)], [HBM], scratch)
 
 
 def count_kernel(cells_ref, count_ref, outer_ref):
@@ -502,27 +545,6 @@
     )(*args)
 
 
-def total_kernel(*refs):
-    *parts, out_ref = refs
-    total = parts[0][...]
-    for part in parts[1:]:
-        total = total + part[...]
-    for step in range(total.shape[0]):
-        out_ref[step] = total[step : step + 1]
-
-
-def total_call(parts):
-    steps, n = parts[0].shape
-    return pl.pallas_call(
-        total_kernel,
-        out_shape=sds((steps, 1, n)),
-        in_specs=[VMEM] * len(parts),
-        out_specs=VMEM,
-        compiler_params=params(4),
-        name="total",
-    )(*parts)
-
-
 def swap_segments(parts, segment):
     count = len(parts)
     lanes = count * segment
@@ -606,7 +628,7 @@
         ],
         compiler_params=params(8),
         name="pack",
-    )(aperture, tile_slot, model_tiles)
+    )(in_hbm(aperture), in_hbm(tile_slot), in_hbm(model_tiles))
     return blocks, table
 
 
@@ -690,10 +712,21 @@
     )(aperture, tile_slot, *blocks)
 
 
-def sum_tiles(table_ref, blocks, out_ref):
-    n_shot = len(blocks)
+def finish_kernel(n_shot, table_hbm, *refs):
+    refs = Refs(refs)
+    blocks = refs.take(n_shot)
+    parts = refs.refs[:-4]
+    sum_ref, record_ref, table_ref, sem = refs.refs[-4:]
+    fetch = pltpu.make_async_copy(table_hbm, table_ref, sem)
+    fetch.start()
     capacity = blocks[0].shape[0]
-    out_ref[...] = jnp.zeros(out_ref.shape, F32)
+    total = parts[0][...]
+    for part in parts[1:]:
+        total = total + part[...]
+    for step in range(total.shape[0]):
+        record_ref[step] = total[step : step + 1]
+    sum_ref[...] = jnp.zeros(sum_ref.shape, F32)
+    fetch.wait()
     for k in range(n_shot):
         base = partner_of(lax.axis_index("shot"), k, n_shot) * (capacity + 1)
         for r in range(capacity):
@@ -701,7 +734,21 @@
             @pl.when(r < table_ref[base + capacity])
             def _():
                 slot = table_ref[base + r]
-                out_ref[slot] = out_ref[slot] + blocks[k][r]
+                sum_ref[slot] = sum_ref[slot] + blocks[k][r]
+
+
+def finish_call(table, blocks, parts, lat_dev):
+    depth, cells = blocks[0].shape[1:]
+    steps, n = parts[0].shape
+    return pl.pallas_call(
+        functools.partial(finish_kernel, len(blocks)),
+        out_shape=[sds((lat_dev, depth, cells)), sds((steps, 1, n))],
+        in_specs=[HBM] + [VMEM] * (len(blocks) + len(parts)),
+        out_specs=[VMEM, VMEM],
+        scratch_shapes=[pltpu.SMEM(table.shape, jnp.int32), pltpu.SemaphoreType.DMA(())],
+        compiler_params=params(8),
+        name="finish",
+    )(table, *blocks, *parts)
 
 
 def swap(edges):
@@ -724,25 +771,34 @@
 def edges_kernel(groups, *refs):
     refs = Refs(refs)
     fields = [refs.take(n) for n in groups]
-    for group in fields:
+    copies = []
+    outs = [refs.take(2) for _ in groups]
+    sems = refs.take()
+    for group, pair in zip(fields, outs):
         depth = group[0].shape[1]
         low = jnp.where(place()[0] == 1, 0, depth - HALO)
-        for out_ref, at in zip(refs.take(2), (low, depth - HALO - low)):
+        for out_ref, at in zip(pair, (low, depth - HALO - low)):
             for index, field_ref in enumerate(group):
-                for z in range(HALO):
-                    out_ref[index, z] = field_ref[0, at + z]
+                copies.append(
+                    pltpu.make_async_copy(field_ref.at[0, pl.ds(at, HALO)], out_ref.at[index], sems.at[len(copies)])
+                )
+    for copy in copies:
+        copy.start()
+    for copy in copies:
+        copy.wait()
 
 
 def first_edges(groups):
     outs = []
     for group in groups:
         outs += [sds((len(group), HALO) + group[0].shape[2:])] * 2
-    fields = [field for group in groups for field in group]
+    fields = [in_hbm(field) for group in groups for field in group]
     edges = pl.pallas_call(
         functools.partial(edges_kernel, [len(group) for group in groups]),
         out_shape=outs,
-        in_specs=[VMEM] * len(fields),
+        in_specs=[HBM] * len(fields),
         out_specs=[VMEM] * len(outs),
+        scratch_shapes=[pltpu.SemaphoreType.DMA((2 * len(fields),))],
         compiler_params=params(8),
         name="edges",
     )(*fields)
@@ -772,13 +828,17 @@
     return got
 
 
-def slab_sum(part):
+def slab_parts(part):
     count = lax.axis_size("slab")
     parts = [part]
-    for k in range(1, count):
-        to = [s ^ k for s in range(count)] if count & (count - 1) == 0 else [(s + k) % count for s in range(count)]
-        parts.append(lax.ppermute(part, "slab", list(enumerate(to))))
-    return total_call(parts)
+    if count & (count - 1) == 0:
+        for bit in range(count.bit_length() - 1):
+            part = functools.reduce(jnp.add, parts)
+            parts = [part, lax.ppermute(part, "slab", [(s, s ^ (1 << bit)) for s in range(count)])]
+    else:
+        for k in range(1, count):
+            parts.append(lax.ppermute(part, "slab", [(s, (s + k) % count) for s in range(count)]))
+    return parts
 
 
 def per_device(
@@ -814,30 +874,34 @@
     count, outer = count_call(receiver_cells, depth, side)
     perturb = perturb_call(aperture, tile_slot, incoming, side, lat_dev, tile_side)
 
-    u_next, lap, corr, *edges = u_call(0, False, wavelet, source_cell, u, up, u_halo, speed, w, None, *tiling)
+    u_next, lap, corr, *edges = u_call(0, False, wavelet, source_cell, u, up, u_halo, speed, w_now, None, None, *tiling)
     u_halo = swap(edges)
     bare, *edges = w_bare_call(w, wp, dw_halo, 1, speed)
     w_halo = swap(edges)
     d_next, w_next, *edges = d_call(d, dp, dw_halo, 0, speed, perturb, lap, bare, count)
     d_halo = swap(edges)
-    traces = None
+    traces = u_local = None
     for step in range(1, steps - 1):
         traces = record_call(receiver_cells, traces, [d_next])
         u, up, d, dp, w, wp = u_next, u, d_next, d, w_next, w
-        u_next, lap, corr, *edges = u_call(step, False, wavelet, source_cell, u, up, u_halo, speed, w, corr, *tiling)
+        u_next, lap, corr, *edges = u_call(
+            step, False, wavelet, source_cell, u, up, u_halo, speed, w, corr, u_local, *tiling
+        )
         u_halo = swap(edges)
+        u_local, d_local, w_local = ahead_call([u_next, d, w])
         d_next, w_next, *edges = dw_call(
-            d, dp, w, wp, d_halo, w_halo, speed, perturb, lap, count, outer if step == 1 else None
+            d, dp, w, wp, d_halo, w_halo, d_local, w_local, speed, perturb, lap, count, outer if step == 1 else None
         )
         d_halo = swap(edges[:2])
         w_halo = swap(edges[2:])
     u, up, d, dp, w, wp = u_next, u, d_next, d, w_next, w
     step = steps - 1
-    u_final, lap, *returning = u_call(step, True, wavelet, source_cell, u, up, u_halo, speed, w, corr, *tiling)
+    u_final, lap, *returning = u_call(step, True, wavelet, source_cell, u, up, u_halo, speed, w, corr, u_local, *tiling)
     arrived = exchange(returning)
     d_final, d_next, traces = last_d_call(step, d, dp, d_halo, speed, perturb, lap, receiver_cells, traces)
-    traces = slab_sum(traces)
-    w_final, sensitivity = last_w_call(w, wp, w_halo, speed, count, d_next, table, arrived, lat_dev)
+    parts = slab_parts(traces)
+    (w_final,) = last_w_call(w, wp, w_halo, speed, count, d_next)
+    sensitivity, traces = finish_call(table, arrived, parts, lat_dev)
     return (sensitivity, u_final, d_final, w_final, jnp.transpose(traces, (1, 0, 2)))
 
 

time: 94.8 us -> 87.2 us (0.920)
  local copies, waits for them, and re-layouts: 6.07 us -> 0.08 us
  starting transfers between devices: 37.7 us -> 35.3 us
  Pallas kernels: 21 us -> 23.4 us
  waiting for transfers between devices: 28.1 us -> 26.6 us
    unnamed x34 -> x20, local copies, waits for them, and re-layouts: 6.07 us -> 0.08 us
    ppermute x14, starting transfers between devices: 15.4 us -> 13.2 us  [exchange(): got[k] = lax.ppermute(block, 'shot', moves) if moves else block]
    ppermute x16, waiting for transfers between devices: 10.6 us -> 8.55 us  [swap(): got.append(lax.ppermute(edge, ('shot', 'slab'), sorted(pairs.items())))]
    pallas_call x1 -> x2, Pallas kernels: 0.59 us -> 2.44 us  [the longest x1 1.62 us: finish_call(): pl.pallas_call(functools.partial(finish_kernel, len(blocks)), out_shape=[...]
    ppermute x14, waiting for transfers between devices: 16.3 us -> 18.1 us  [exchange(): got[k] = lax.ppermute(block, 'shot', moves) if moves else block]
    pallas_call x1, Pallas kernels: 0.1 us -> 1.39 us  [first_edges(): pl.pallas_call(functools.partial(edges_kernel, [len(group) for group in g...]
    ppermute x3 -> x2, waiting for transfers between devices: 1.19 us -> 0.01 us  [slab_parts(): lax.ppermute(part, 'slab', [(s, s ^ 1 << bit) for s in range(count)])]
    ppermute x3 -> x2, starting transfers between devices: 4.39 us -> 3.99 us  [slab_parts(): lax.ppermute(part, 'slab', [(s, s ^ 1 << bit) for s in range(count)])]
  transfers between devices with their start and end apart: 33 -> 32, of which waited for: 12 -> 11; matrix products, arithmetic and copies ran while one was open for 0% -> 0% of each run, Pallas kernels for 17% -> 23%
where the time goes in v1:
time: 87.2 us; the launch traced here: 86.9 us
  starting transfers between devices  35.3 us (40%)
  waiting for transfers between devices  26.6 us (31%)
  Pallas kernels  23.4 us (27%)
  between operations  1.56 us (2%)
    ppermute x16, starting transfers between devices, swap(): got.append(lax.ppermute(edge, ('shot', 'slab'), sorted(pairs.items())))  18.1 us
    ppermute x14, waiting for transfers between devices, exchange(): got[k] = lax.ppermute(block, 'shot', moves) if moves else block  18.1 us
    pallas_call x8, Pallas kernels, stencil_call(): pl.pallas_call(body, out_shape=outs, in_specs=in_specs, out_specs=kinds,...  14.2 us
    ppermute x14, starting transfers between devices, exchange(): got[k] = lax.ppermute(block, 'shot', moves) if moves else block  13.2 us
    ppermute x16, waiting for transfers between devices, swap(): got.append(lax.ppermute(edge, ('shot', 'slab'), sorted(pairs.items())))  8.55 us
    ppermute x2, starting transfers between devices, slab_parts(): lax.ppermute(part, 'slab', [(s, s ^ 1 << bit) for s in range(count)])  3.99 us
    pallas_call x1, Pallas kernels, pack_call(): pl.pallas_call(pack_kernel, out_shape=[sds((capacity, depth, cells))] * n...  1.85 us
  transfers between devices with their start and end apart: 32, of which 11 were waited for; matrix products, arithmetic and copies ran while one was open for 0% of the time, Pallas kernels for 23%

profile of v1, /device:TPU:0, one launch (start us, length us, event | category | flops | bytes accessed | tf_op | source)
XLA Modules:
  0.0 86.9 jit_solution(7537467920592410840)
XLA Ops:
  0.6 1.9 %pack.1 = (f32[4,8,1024]{2,1,0:T(8,128)S(1)}, f32[4,8,1024]{2,1,0:T(8,128)S(1)}, f32[4,8,1024]{2,1,0:T(8,128)S(1)}, f32[4,8,1024]{2,1,0:T(8,128)S(1)}, f32[4,8,1...) custom-call(s32[8,16]{1,0:T(8,128)} %refs_11_.1, ...), custom_call_target="tpu_custom_call" | custom-call | tf_op jit(solution)/shard_map/pack/pallas_call | solution.py:618
  4.5 2.7 %collective-permute-start = (f32[1,4,128,128]{3,2,1,0:T(8,128)S(1)}, f32[1,4,128,128]{3,2,1,0:T(8,128)S(1)}, u32[]{:S(2)}, u32[]{:S(2)}) collective-permute-start(f32[1,4,128,128]{3,2,1,0:T(8,128)S(1)} %get-tuple-element.65), channel_id=1, source_target_pairs={{0,1},{1,0},{2,3},{3,2},{4,5},{5,4},{6,7},{7,6},{8,9},{9,8},{10,11... | collective-permute-start | bytes 786440 | tf_op jit(solution)/shard_map/ppermute | solution.py:767
  7.3 3.0 %collective-permute-start.4 = (f32[2,4,128,128]{3,2,1,0:T(8,128)S(1)}, f32[2,4,128,128]{3,2,1,0:T(8,128)S(1)}, u32[]{:S(2)}, u32[]{:S(2)}) collective-permute-start(f32[2,4,128,128]{3,2,1,0:T(8,128)S(1)} %get-tuple-element.70), channel_id=1, source_target_pairs={{0,1},{1,0},{2,3},{3,2},{4,5},{5,4},{6,7},{7,6},{8,9},{9,8},{10,11... | collective-permute-start | bytes 1572872 | tf_op jit(solution)/shard_map/ppermute | solution.py:767
  11.9 4.4 %collective-permute-done.7.rest_2_ = f32[4,8,1024]{2,1,0:T(8,128)S(1)} collective-permute-done((f32[4,8,1024]{2,1,0:T(8,128)S(1)}, f32[4,8,1024]{2,1,0:T(8,128)S(1)}, u32[]{:S(2)}, u32[]{:S(2)}) %collective-permute-start.7) | collective-permute-done | bytes 131104 | tf_op jit(solution)/shard_map/ppermute | solution.py:827
  20.0 1.8 %shard_map.164 = (f32[8,128,128]{2,1,0:T(8,128)S(1)}, f32[8,128,128]{2,1,0:T(8,128)S(1)}, f32[8,128,128]{2,1,0:T(8,128)S(1)}, f32[1,4,128,128]{3,2,1,0:T(8,128)S(1)}, f32[1,4,128,128]{3,2,1,0:T(8,128)S(1)}) custom-call(s32[1]{0:T(128)S(6)} %copy.18.refs_0_, f32[1,3]{1,0:T(1,128)} %refs_1_.7, f32[8,128,128]{2,1,0:T(8,128)S(1)} %bitcast.18, ...), custom_call_target="tpu_custom_call" | custom-call | tf_op jit(solution)/shard_map/pallas_call | solution.py:380
  23.4 1.7 %collective-permute-start.11 = (f32[4,8,1024]{2,1,0:T(8,128)S(1)}, f32[4,8,1024]{2,1,0:T(8,128)S(1)}, u32[]{:S(2)}, u32[]{:S(2)}) collective-permute-start(f32[4,8,1024]{2,1,0:T(8,128)S(1)} %get-tuple-element.78), channel_id=1, source_target_pairs={{0,24},{4,28},{8,16},{12,20},{16,8},{20,12},{24,0},{28,4},{1,25},{... | collective-permute-start | bytes 393224 | tf_op jit(solution)/shard_map/ppermute | solution.py:827
  27.8 1.8 %collective-permute-done.11.rest_6_ = f32[4,8,1024]{2,1,0:T(8,128)S(1)} collective-permute-done((f32[4,8,1024]{2,1,0:T(8,128)S(1)}, f32[4,8,1024]{2,1,0:T(8,128)S(1)}, u32[]{:S(2)}, u32[]{:S(2)}) %collective-permute-start.11) | collective-permute-done | bytes 131104 | tf_op jit(solution)/shard_map/ppermute | solution.py:827
  29.6 2.7 %collective-permute-done.12.rest_7_ = f32[4,8,1024]{2,1,0:T(8,128)S(1)} collective-permute-done((f32[4,8,1024]{2,1,0:T(8,128)S(1)}, f32[4,8,1024]{2,1,0:T(8,128)S(1)}, u32[]{:S(2)}, u32[]{:S(2)}) %collective-permute-start.12) | collective-permute-done | bytes 131104 | tf_op jit(solution)/shard_map/ppermute | solution.py:827
  32.3 1.7 %perturb.1.perturb_ref.refs_5_ = f32[8,128,128]{2,1,0:T(8,128)S(1)} custom-call(s32[8,16]{1,0:T(8,128)S(1)} %copy-done.7, s32[64]{0:T(128)S(1)} %copy-done.9, f32[4,8,1024]{2,1,0:T(8,128)S(1)} %get-tuple-element.72.rest_0_, f32[4,8,1024]{2,1,0:T(8,128)S(1)} %collective-permute-done.6.rest_1_, f32[4,8,1024]{2,1,0:T(8,128)S(1)} %collective-permute-done.7.rest_2_, ...), custom_call_target="tpu_custom_call" | custom-call | tf_op jit(solution)/shard_map/perturb/pallas_call | solution.py:704
  38.1 1.6 %collective-permute-start.17 = (f32[1,4,128,128]{3,2,1,0:T(8,128)S(1)}, f32[1,4,128,128]{3,2,1,0:T(8,128)S(1)}, u32[]{:S(2)}, u32[]{:S(2)}) collective-permute-start(f32[1,4,128,128]{3,2,1,0:T(8,128)S(1)} %get-tuple-element.92), channel_id=1, source_target_pairs={{0,1},{1,0},{2,3},{3,2},{4,5},{5,4},{6,7},{7,6},{8,9},{9,8},{10,11... | collective-permute-start | bytes 786440 | tf_op jit(solution)/shard_map/ppermute | solution.py:767
  41.1 4.5 %collective-permute-start.13 = (f32[1,4,128,128]{3,2,1,0:T(8,128)S(1)}, f32[1,4,128,128]{3,2,1,0:T(8,128)S(1)}, u32[]{:S(2)}, u32[]{:S(2)}) collective-permute-start(f32[1,4,128,128]{3,2,1,0:T(8,128)S(1)} %get-tuple-element.86), channel_id=1, source_target_pairs={{0,1},{1,0},{2,3},{3,2},{4,5},{5,4},{6,7},{7,6},{8,9},{9,8},{10,11... | collective-permute-start | bytes 786440 | tf_op jit(solution)/shard_map/ppermute | solution.py:767
  47.0 4.8 %collective-permute-done.17.refs_10_ = f32[1,4,128,128]{3,2,1,0:T(8,128)S(1)} collective-permute-done((f32[1,4,128,128]{3,2,1,0:T(8,128)S(1)}, f32[1,4,128,128]{3,2,1,0:T(8,128)S(1)}, u32[]{:S(2)}, u32[]{:S(2)}) %collective-permute-start.17) | collective-permute-done | bytes 262176 | tf_op jit(solution)/shard_map/ppermute | solution.py:767
  51.8 1.7 %shard_map.169 = (f32[8,128,128]{2,1,0:T(8,128)S(1)}, f32[8,128,128]{2,1,0:T(8,128)S(1)}, f32[1,4,128,128]{3,2,1,0:T(8,128)S(1)}, f32[1,4,128,128]{3,2,1,0:T(8,1...) custom-call(f32[8,128,128]{2,1,0:T(8,128)S(1)} %bitcast.12, ...), custom_call_target="tpu_custom_call" | custom-call | tf_op jit(solution)/shard_map/pallas_call | solution.py:380
  53.5 3.6 %collective-permute-start.26 = (f32[1,4,128,128]{3,2,1,0:T(8,128)S(1)}, f32[1,4,128,128]{3,2,1,0:T(8,128)S(1)}, u32[]{:S(2)}, u32[]{:S(2)}) collective-permute-start(f32[1,4,128,128]{3,2,1,0:T(8,128)S(1)} %get-tuple-element.112), channel_id=1, source_target_pairs={{0,1},{1,0},{2,3},{3,2},{4,5},{5,4},{6,7},{7,6},{8,9},{9,8},{10,11... | collective-permute-start | bytes 786440 | tf_op jit(solution)/shard_map/ppermute | solution.py:767
  57.7 2.8 %shard_map.170 = (f32[1,8,128,128]{3,2,1,0:T(8,128)}, f32[8,128,128]{2,1,0:T(8,128)S(1)}, f32[4,8,1024]{2,1,0:T(8,128)S(1)}, f32[4,8,1024]{2,1,0:T(8,128)S(1)}, ...) custom-call(s32[1]{0:T(128)S(6)} %copy.18.refs_0_, ...), custom_call_target="tpu_custom_call" | custom-call | tf_op jit(solution)/shard_map/pallas_call | solution.py:380
  61.1 3.2 %collective-permute-done.26.refs_2_ = f32[1,4,128,128]{3,2,1,0:T(8,128)S(1)} collective-permute-done((f32[1,4,128,128]{3,2,1,0:T(8,128)S(1)}, f32[1,4,128,128]{3,2,1,0:T(8,128)S(1)}, u32[]{:S(2)}, u32[]{:S(2)}) %collective-permute-start.26) | collective-permute-done | bytes 262176 | tf_op jit(solution)/shard_map/ppermute | solution.py:767
  66.3 2.1 %shard_map.172 = (f32[1,8,128,128]{3,2,1,0:T(8,128)}, f32[8,128,128]{2,1,0:T(8,128)S(1)}, f32[3,256]{1,0:T(4,128)S(1)}) custom-call(f32[8,128,128]{2,1,0:T(8,128)S(1)} %get-tuple-element.111.refs_0_, f32[8,128,128]{2,1,0:T(8,128)S(1)} %get-tuple-element.88.refs_1_.rest_0_, f32[1,4,128,128]{3,2,1,0:T(8,128)S(1)} %collective-permute-done.26.refs_2_, ...), custom_call_target="tpu_custom_call" | custom-call | tf_op jit(solution)/shard_map/pallas_call | solution.py:380
  68.4 2.1 %collective-permute-start.28 = (f32[3,256]{1,0:T(4,128)S(1)}, f32[3,256]{1,0:T(4,128)S(1)}, u32[]{:S(2)}, u32[]{:S(2)}) collective-permute-start(f32[3,256]{1,0:T(4,128)S(1)} %get-tuple-element.115), channel_id=1, source_target_pairs={{0,1},{1,0},{2,3},{3,2},{4,5},{5,4},{6,7},{7,6},{8,9},{9,8},{10,11... | collective-permute-start | bytes 9224 | tf_op jit(solution)/shard_map/ppermute | solution.py:837
  71.2 1.8 %collective-permute-start.23 = (f32[4,8,1024]{2,1,0:T(8,128)S(1)}, f32[4,8,1024]{2,1,0:T(8,128)S(1)}, u32[]{:S(2)}, u32[]{:S(2)}) collective-permute-start(f32[4,8,1024]{2,1,0:T(8,128)S(1)} %get-tuple-element.108), channel_id=1, source_target_pairs={{0,20},{4,16},{8,28},{12,24},{16,4},{20,0},{24,12},{28,8},{1,21},{... | collective-permute-start | bytes 393224 | tf_op jit(solution)/shard_map/ppermute | solution.py:827
  74.9 1.9 %collective-permute-start.29 = (f32[3,256]{1,0:T(4,128)S(1)}, f32[3,256]{1,0:T(4,128)S(1)}, u32[]{:S(2)}, u32[]{:S(2)}) collective-permute-start(f32[3,256]{1,0:T(4,128)S(1)} %add.3.refs_8_), channel_id=1, source_target_pairs={{0,2},{1,3},{2,0},{3,1},{4,6},{5,7},{6,4},{7,5},{8,10},{9,11},{10,... | collective-permute-start | bytes 9224 | tf_op jit(solution)/shard_map/ppermute | solution.py:837
  76.8 1.9 %shard_map.173 = f32[1,8,128,128]{3,2,1,0:T(8,128)} custom-call(f32[8,128,128]{2,1,0:T(8,128)S(1)} %get-tuple-element.99.refs_7_.refs_0_, f32[8,128,128]{2,1,0:T(8,128)S(1)} %get-tuple-element.83.refs_7_.refs_2_.refs_3_.refs_1_, f32[1,4,128,128]{3,2,1,0:T(8,128)S(1)} %collective-permute-done.30.refs_2_, ...), custom_call_target="tpu_custom_call" | custom-call | tf_op jit(solution)/shard_map/pallas_call | solution.py:380
  78.7 3.6 %collective-permute-done.22.refs_4_ = f32[4,8,1024]{2,1,0:T(8,128)S(1)} collective-permute-done((f32[4,8,1024]{2,1,0:T(8,128)S(1)}, f32[4,8,1024]{2,1,0:T(8,128)S(1)}, u32[]{:S(2)}, u32[]{:S(2)}) %collective-permute-start.22) | collective-permute-done | bytes 131104 | tf_op jit(solution)/shard_map/ppermute | solution.py:827
  82.3 3.0 %collective-permute-done.23.refs_5_ = f32[4,8,1024]{2,1,0:T(8,128)S(1)} collective-permute-done((f32[4,8,1024]{2,1,0:T(8,128)S(1)}, f32[4,8,1024]{2,1,0:T(8,128)S(1)}, u32[]{:S(2)}, u32[]{:S(2)}) %collective-permute-start.23) | collective-permute-done | bytes 131104 | tf_op jit(solution)/shard_map/ppermute | solution.py:827
  85.3 1.6 %finish.1 = (f32[8,8,1024]{2,1,0:T(8,128)}, f32[3,1,256]{2,1,0:T(1,128)}) custom-call(s32[40]{0:T(128)S(1)} %get-tuple-element.64.table_hbm, f32[4,8,1024]{2,1,0:T(8,128)S(1)} %get-tuple-element.103.refs_0_, f32[4,8,1024]{2,1,0:T(8,128)S(1)} %collective-permute-done.19.refs_1_, f32[4,8,1024]{2,1,0:T(8,128)S(1)} %collective-permute-done.20.refs_2_, ...), custom_call_target="tpu_custom_call" | custom-call | tf_op jit(solution)/shard_map/finish/pallas_call | solution.py:743
  (76 shorter events, 23.5 us)
Async XLA Ops:
  2.5 7.9 %collective-permute-start.6 = (f32[4,8,1024]{2,1,0:T(8,128)S(1)}, f32[4,8,1024]{2,1,0:T(8,128)S(1)}, u32[]{:S(2)}, u32[]{:S(2)}) collective-permute-start(f32[4,8,1024]{2,1,0:T(8,128)S(1)} %get-tuple-element.73), channel_id=1, source_target_pairs={{0,4},{4,0},{8,12},{12,8},{16,20},{20,16},{24,28},{28,24},{1,5},{5... | collective-permute-start | bytes 393224 | tf_op jit(solution)/shard_map/ppermute | solution.py:827
  4.5 12.6 %collective-permute-start = (f32[1,4,128,128]{3,2,1,0:T(8,128)S(1)}, f32[1,4,128,128]{3,2,1,0:T(8,128)S(1)}, u32[]{:S(2)}, u32[]{:S(2)}) collective-permute-start(f32[1,4,128,128]{3,2,1,0:T(8,128)S(1)} %get-tuple-element.65), channel_id=1, source_target_pairs={{0,1},{1,0},{2,3},{3,2},{4,5},{5,4},{6,7},{7,6},{8,9},{9,8},{10,11... | collective-permute-start | bytes 786440 | tf_op jit(solution)/shard_map/ppermute | solution.py:767
  7.2 11.3 %collective-permute-start.1 = (f32[1,4,128,128]{3,2,1,0:T(8,128)S(1)}, f32[1,4,128,128]{3,2,1,0:T(8,128)S(1)}, u32[]{:S(2)}, u32[]{:S(2)}) collective-permute-start(f32[1,4,128,128]{3,2,1,0:T(8,128)S(1)} %get-tuple-element.66), channel_id=1, source_target_pairs={{0,4},{1,2},{2,1},{3,7},{4,0},{5,6},{6,5},{7,3},{8,12},{9,10},{10,... | collective-permute-start | bytes 786440 | tf_op jit(solution)/shard_map/ppermute | solution.py:767
  7.3 27.0 %collective-permute-start.4 = (f32[2,4,128,128]{3,2,1,0:T(8,128)S(1)}, f32[2,4,128,128]{3,2,1,0:T(8,128)S(1)}, u32[]{:S(2)}, u32[]{:S(2)}) collective-permute-start(f32[2,4,128,128]{3,2,1,0:T(8,128)S(1)} %get-tuple-element.70), channel_id=1, source_target_pairs={{0,1},{1,0},{2,3},{3,2},{4,5},{5,4},{6,7},{7,6},{8,9},{9,8},{10,11... | collective-permute-start | bytes 1572872 | tf_op jit(solution)/shard_map/ppermute | solution.py:767
  10.4 24.0 %collective-permute-start.5 = (f32[2,4,128,128]{3,2,1,0:T(8,128)S(1)}, f32[2,4,128,128]{3,2,1,0:T(8,128)S(1)}, u32[]{:S(2)}, u32[]{:S(2)}) collective-permute-start(f32[2,4,128,128]{3,2,1,0:T(8,128)S(1)} %get-tuple-element.71), channel_id=1, source_target_pairs={{0,4},{1,2},{2,1},{3,7},{4,0},{5,6},{6,5},{7,3},{8,12},{9,10},{10,... | collective-permute-start | bytes 1572872 | tf_op jit(solution)/shard_map/ppermute | solution.py:767
  17.1 6.4 %collective-permute-start.9 = (f32[4,8,1024]{2,1,0:T(8,128)S(1)}, f32[4,8,1024]{2,1,0:T(8,128)S(1)}, u32[]{:S(2)}, u32[]{:S(2)}) collective-permute-start(f32[4,8,1024]{2,1,0:T(8,128)S(1)} %get-tuple-element.76), channel_id=1, source_target_pairs={{0,16},{4,20},{8,24},{12,28},{16,0},{20,4},{24,8},{28,12},{1,17},{... | collective-permute-start | bytes 393224 | tf_op jit(solution)/shard_map/ppermute | solution.py:827
  18.6 7.4 %collective-permute-start.10 = (f32[4,8,1024]{2,1,0:T(8,128)S(1)}, f32[4,8,1024]{2,1,0:T(8,128)S(1)}, u32[]{:S(2)}, u32[]{:S(2)}) collective-permute-start(f32[4,8,1024]{2,1,0:T(8,128)S(1)} %get-tuple-element.77), channel_id=1, source_target_pairs={{0,20},{4,16},{8,28},{12,24},{16,4},{20,0},{24,12},{28,8},{1,21},{... | collective-permute-start | bytes 393224 | tf_op jit(solution)/shard_map/ppermute | solution.py:827
  22.1 17.6 %collective-permute-start.2 = (f32[1,4,128,128]{3,2,1,0:T(8,128)S(1)}, f32[1,4,128,128]{3,2,1,0:T(8,128)S(1)}, u32[]{:S(2)}, u32[]{:S(2)}) collective-permute-start(f32[1,4,128,128]{3,2,1,0:T(8,128)S(1)} %get-tuple-element.68), channel_id=1, source_target_pairs={{0,1},{1,0},{2,3},{3,2},{4,5},{5,4},{6,7},{7,6},{8,9},{9,8},{10,11... | collective-permute-start | bytes 786440 | tf_op jit(solution)/shard_map/ppermute | solution.py:767
  36.9 9.2 %collective-permute-start.15 = (f32[1,4,128,128]{3,2,1,0:T(8,128)S(1)}, f32[1,4,128,128]{3,2,1,0:T(8,128)S(1)}, u32[]{:S(2)}, u32[]{:S(2)}) collective-permute-start(f32[1,4,128,128]{3,2,1,0:T(8,128)S(1)} %get-tuple-element.90), channel_id=1, source_target_pairs={{0,1},{1,0},{2,3},{3,2},{4,5},{5,4},{6,7},{7,6},{8,9},{9,8},{10,11... | collective-permute-start | bytes 786440 | tf_op jit(solution)/shard_map/ppermute | solution.py:767
  38.1 8.9 %collective-permute-start.16 = (f32[1,4,128,128]{3,2,1,0:T(8,128)S(1)}, f32[1,4,128,128]{3,2,1,0:T(8,128)S(1)}, u32[]{:S(2)}, u32[]{:S(2)}) collective-permute-start(f32[1,4,128,128]{3,2,1,0:T(8,128)S(1)} %get-tuple-element.91), channel_id=1, source_target_pairs={{0,4},{1,2},{2,1},{3,7},{4,0},{5,6},{6,5},{7,3},{8,12},{9,10},{10,... | collective-permute-start | bytes 786440 | tf_op jit(solution)/shard_map/ppermute | solution.py:767
  38.1 13.7 %collective-permute-start.17 = (f32[1,4,128,128]{3,2,1,0:T(8,128)S(1)}, f32[1,4,128,128]{3,2,1,0:T(8,128)S(1)}, u32[]{:S(2)}, u32[]{:S(2)}) collective-permute-start(f32[1,4,128,128]{3,2,1,0:T(8,128)S(1)} %get-tuple-element.92), channel_id=1, source_target_pairs={{0,1},{1,0},{2,3},{3,2},{4,5},{5,4},{6,7},{7,6},{8,9},{9,8},{10,11... | collective-permute-start | bytes 786440 | tf_op jit(solution)/shard_map/ppermute | solution.py:767
  39.6 12.1 %collective-permute-start.18 = (f32[1,4,128,128]{3,2,1,0:T(8,128)S(1)}, f32[1,4,128,128]{3,2,1,0:T(8,128)S(1)}, u32[]{:S(2)}, u32[]{:S(2)}) collective-permute-start(f32[1,4,128,128]{3,2,1,0:T(8,128)S(1)} %get-tuple-element.93), channel_id=1, source_target_pairs={{0,4},{1,2},{2,1},{3,7},{4,0},{5,6},{6,5},{7,3},{8,12},{9,10},{10,... | collective-permute-start | bytes 786440 | tf_op jit(solution)/shard_map/ppermute | solution.py:767
  41.1 16.6 %collective-permute-start.13 = (f32[1,4,128,128]{3,2,1,0:T(8,128)S(1)}, f32[1,4,128,128]{3,2,1,0:T(8,128)S(1)}, u32[]{:S(2)}, u32[]{:S(2)}) collective-permute-start(f32[1,4,128,128]{3,2,1,0:T(8,128)S(1)} %get-tuple-element.86), channel_id=1, source_target_pairs={{0,1},{1,0},{2,3},{3,2},{4,5},{5,4},{6,7},{7,6},{8,9},{9,8},{10,11... | collective-permute-start | bytes 786440 | tf_op jit(solution)/shard_map/ppermute | solution.py:767
  46.2 11.5 %collective-permute-start.14 = (f32[1,4,128,128]{3,2,1,0:T(8,128)S(1)}, f32[1,4,128,128]{3,2,1,0:T(8,128)S(1)}, u32[]{:S(2)}, u32[]{:S(2)}) collective-permute-start(f32[1,4,128,128]{3,2,1,0:T(8,128)S(1)} %get-tuple-element.87), channel_id=1, source_target_pairs={{0,4},{1,2},{2,1},{3,7},{4,0},{5,6},{6,5},{7,3},{8,12},{9,10},{10,... | collective-permute-start | bytes 786440 | tf_op jit(solution)/shard_map/ppermute | solution.py:767
  53.5 10.7 %collective-permute-start.26 = (f32[1,4,128,128]{3,2,1,0:T(8,128)S(1)}, f32[1,4,128,128]{3,2,1,0:T(8,128)S(1)}, u32[]{:S(2)}, u32[]{:S(2)}) collective-permute-start(f32[1,4,128,128]{3,2,1,0:T(8,128)S(1)} %get-tuple-element.112), channel_id=1, source_target_pairs={{0,1},{1,0},{2,3},{3,2},{4,5},{5,4},{6,7},{7,6},{8,9},{9,8},{10,11... | collective-permute-start | bytes 786440 | tf_op jit(solution)/shard_map/ppermute | solution.py:767
  57.1 7.8 %collective-permute-start.27 = (f32[1,4,128,128]{3,2,1,0:T(8,128)S(1)}, f32[1,4,128,128]{3,2,1,0:T(8,128)S(1)}, u32[]{:S(2)}, u32[]{:S(2)}) collective-permute-start(f32[1,4,128,128]{3,2,1,0:T(8,128)S(1)} %get-tuple-element.113), channel_id=1, source_target_pairs={{0,4},{1,2},{2,1},{3,7},{4,0},{5,6},{6,5},{7,3},{8,12},{9,10},{10,... | collective-permute-start | bytes 786440 | tf_op jit(solution)/shard_map/ppermute | solution.py:767
  57.1 15.9 %collective-permute-start.30 = (f32[1,4,128,128]{3,2,1,0:T(8,128)S(1)}, f32[1,4,128,128]{3,2,1,0:T(8,128)S(1)}, u32[]{:S(2)}, u32[]{:S(2)}) collective-permute-start(f32[1,4,128,128]{3,2,1,0:T(8,128)S(1)} %get-tuple-element.119), channel_id=1, source_target_pairs={{0,1},{1,0},{2,3},{3,2},{4,5},{5,4},{6,7},{7,6},{8,9},{9,8},{10,11... | collective-permute-start | bytes 786440 | tf_op jit(solution)/shard_map/ppermute | solution.py:767
  60.5 7.9 %collective-permute-start.19 = (f32[4,8,1024]{2,1,0:T(8,128)S(1)}, f32[4,8,1024]{2,1,0:T(8,128)S(1)}, u32[]{:S(2)}, u32[]{:S(2)}) collective-permute-start(f32[4,8,1024]{2,1,0:T(8,128)S(1)} %get-tuple-element.104), channel_id=1, source_target_pairs={{0,4},{4,0},{8,12},{12,8},{16,20},{20,16},{24,28},{28,24},{1,5},{5... | collective-permute-start | bytes 393224 | tf_op jit(solution)/shard_map/ppermute | solution.py:827
  60.6 14.4 %collective-permute-start.31 = (f32[1,4,128,128]{3,2,1,0:T(8,128)S(1)}, f32[1,4,128,128]{3,2,1,0:T(8,128)S(1)}, u32[]{:S(2)}, u32[]{:S(2)}) collective-permute-start(f32[1,4,128,128]{3,2,1,0:T(8,128)S(1)} %get-tuple-element.120), channel_id=1, source_target_pairs={{0,4},{1,2},{2,1},{3,7},{4,0},{5,6},{6,5},{7,3},{8,12},{9,10},{10,... | collective-permute-start | bytes 786440 | tf_op jit(solution)/shard_map/ppermute | solution.py:767
  70.5 11.8 %collective-permute-start.22 = (f32[4,8,1024]{2,1,0:T(8,128)S(1)}, f32[4,8,1024]{2,1,0:T(8,128)S(1)}, u32[]{:S(2)}, u32[]{:S(2)}) collective-permute-start(f32[4,8,1024]{2,1,0:T(8,128)S(1)} %get-tuple-element.107), channel_id=1, source_target_pairs={{0,16},{4,20},{8,24},{12,28},{16,0},{20,4},{24,8},{28,12},{1,17},{... | collective-permute-start | bytes 393224 | tf_op jit(solution)/shard_map/ppermute | solution.py:827
  71.2 14.1 %collective-permute-start.23 = (f32[4,8,1024]{2,1,0:T(8,128)S(1)}, f32[4,8,1024]{2,1,0:T(8,128)S(1)}, u32[]{:S(2)}, u32[]{:S(2)}) collective-permute-start(f32[4,8,1024]{2,1,0:T(8,128)S(1)} %get-tuple-element.108), channel_id=1, source_target_pairs={{0,20},{4,16},{8,28},{12,24},{16,4},{20,0},{24,12},{28,8},{1,21},{... | collective-permute-start | bytes 393224 | tf_op jit(solution)/shard_map/ppermute | solution.py:827
  73.0 12.3 %collective-permute-start.24 = (f32[4,8,1024]{2,1,0:T(8,128)S(1)}, f32[4,8,1024]{2,1,0:T(8,128)S(1)}, u32[]{:S(2)}, u32[]{:S(2)}) collective-permute-start(f32[4,8,1024]{2,1,0:T(8,128)S(1)} %get-tuple-element.109), channel_id=1, source_target_pairs={{0,24},{4,28},{8,16},{12,20},{16,8},{20,12},{24,0},{28,4},{1,25},{... | collective-permute-start | bytes 393224 | tf_op jit(solution)/shard_map/ppermute | solution.py:827
  73.7 11.6 %collective-permute-start.25 = (f32[4,8,1024]{2,1,0:T(8,128)S(1)}, f32[4,8,1024]{2,1,0:T(8,128)S(1)}, u32[]{:S(2)}, u32[]{:S(2)}) collective-permute-start(f32[4,8,1024]{2,1,0:T(8,128)S(1)} %get-tuple-element.110), channel_id=1, source_target_pairs={{0,28},{4,24},{8,20},{12,16},{16,12},{20,8},{24,4},{28,0},{1,29},{... | collective-permute-start | bytes 393224 | tf_op jit(solution)/shard_map/ppermute | solution.py:827
  74.9 10.4 %collective-permute-start.29 = (f32[3,256]{1,0:T(4,128)S(1)}, f32[3,256]{1,0:T(4,128)S(1)}, u32[]{:S(2)}, u32[]{:S(2)}) collective-permute-start(f32[3,256]{1,0:T(4,128)S(1)} %add.3.refs_8_), channel_id=1, source_target_pairs={{0,2},{1,3},{2,0},{3,1},{4,6},{5,7},{6,4},{7,5},{8,10},{9,11},{10,... | collective-permute-start | bytes 9224 | tf_op jit(solution)/shard_map/ppermute | solution.py:837
  (18 other events, 128.5 us)

commit v2 on v1

--- a/solution.py
+++ b/solution.py
@@ -181,6 +181,21 @@
     return pltpu.make_async_copy(next_ref.at[:, rows], out_ref.at[0, :, rows], sems.at[step])
 
 
+def add_source(next_ref, source_ref, wavelet_ref, step, first, rows):
+    depth, side, _ = next_ref.shape
+    local = source_ref[0] - lax.axis_index("slab") * (depth * side * side)
+    mine = (local >= 0) & (local < depth * side * side)
+    cell = jnp.where(mine, local, 0)
+    z = quotient(cell, side * side)
+    x = remainder(quotient(cell, side), side)
+    lane = lax.broadcasted_iota(jnp.int32, (1, side), 1)
+
+    @pl.when(mine & (x >= first) & (x < first + rows))
+    def _():
+        add = jnp.where(lane == remainder(cell, side), wavelet_ref[0, step], 0.0)
+        next_ref[z, pl.ds(x, 1), :] = next_ref[z, pl.ds(x, 1), :] + add
+
+
 class Refs:
     def __init__(self, refs):
         self.refs = list(refs)
@@ -193,23 +208,27 @@
 
 def u_kernel(step, last, ahead, tiles, *refs):
     refs = Refs(refs)
-    source_ref, wavelet_hbm, now_ref, prev_ref, ha_ref, hb_ref, speed_ref, w_in = refs.take(8)
+    now_ref, ha_ref, hb_ref, w_in = refs.take(4)
+    if not last:
+        source_ref, wavelet_hbm, prev_ref, speed_ref = refs.take(4)
     corr_in = refs.take() if step else None
     local_work = refs.take(2) if ahead else None
     tables = refs.take(2) if last else []
     if last:
-        out_ref, lap_ref = refs.take(2)
+        lap_ref = refs.take()
         blocks = refs.take(tiles[0])
-        sends = []
-        next_ref, corr_ref = refs.take(2)
+        corr_ref = refs.take()
     else:
         next_ref, lap_ref, corr_ref = refs.take(3)
         sends = refs.take(2)
     halo_ref = refs.take()
     if not ahead:
         local_work = refs.take(2)
-    wavelet_ref, own_sems = refs.take(2)
-    copies = [pltpu.make_async_copy(wavelet_hbm, wavelet_ref, own_sems.at[0])]
+    own_sems = refs.take()
+    copies = []
+    if not last:
+        wavelet_ref = refs.take()
+        copies.append(pltpu.make_async_copy(wavelet_hbm, wavelet_ref, own_sems.at[0]))
     w_ref = w_in
     if not step:
         w_ref = refs.take()
@@ -219,12 +238,12 @@
             copies.append(pltpu.make_async_copy(w_in.at[0, part], w_ref.at[part], own_sems.at[1 + i]))
     if last:
         fetched = refs.take(2)
-        tiles_ref, seen_ref, place_ref, sems = refs.take(4)
+        tiles_ref, seen_ref, place_ref = refs.take(3)
         for i, (a, b) in enumerate(zip(tables, fetched)):
             copies.append(pltpu.make_async_copy(a, b, own_sems.at[1 + i]))
     for copy in copies:
         copy.start()
-    depth, side, _ = now_ref.shape
+    _, side, _ = now_ref.shape
     work = (local_work[0], halo_ref, local_work[1])
     if not ahead:
         prepare_local(*local_work, now_ref, band_weights(side))
@@ -236,34 +255,15 @@
         lap_ref[z, block, :] = lap
         part = lap * w_ref[z, block, :]
         corr_ref[z, block, :] = corr_in[z, block, :] + part if step else part
-        next_ref[z, block, :] = (2.0 * centre - prev_ref[z, block, :]) + speed_ref[z, block, :] * lap
-
-    local = source_ref[0] - lax.axis_index("slab") * (depth * side * side)
-    mine = (local >= 0) & (local < depth * side * side)
-    cell = jnp.where(mine, local, 0)
-    z = quotient(cell, side * side)
-    x = remainder(quotient(cell, side), side)
-    lane = lax.broadcasted_iota(jnp.int32, (1, side), 1)
-    add = jnp.where((lane == remainder(cell, side)) & mine, wavelet_ref[0, step], 0.0)
-
-    def finish(part, parts):
-        size = side // parts
-
-        @pl.when((x >= part * size) & (x < (part + 1) * size))
-        def _():
-            next_ref[z, pl.ds(x, 1), :] = next_ref[z, pl.ds(x, 1), :] + add
-
-        if last:
-            store_out(next_ref, out_ref, sems, part, parts).start()
-
-    parts = PARTS if last else 1
-    each_laplacian(work, now_ref, emit, finish, parts)
-    if sends:
-        copy_sends(next_ref, *sends, 0)
+        if not last:
+            next_ref[z, block, :] = (2.0 * centre - prev_ref[z, block, :]) + speed_ref[z, block, :] * lap
+
+    each_laplacian(work, now_ref, emit)
     if last:
         pack_back(*tiles[1:], *fetched, corr_ref, blocks, tiles_ref, seen_ref, place_ref)
-        for part in range(parts):
-            store_out(next_ref, out_ref, sems, part, parts).wait()
+    else:
+        add_source(next_ref, source_ref, wavelet_ref, step, 0, side)
+        copy_sends(next_ref, *sends, 0)
 
 
 def w_bare_kernel(index, now_ref, prev_ref, ha_ref, hb_ref, speed_ref, next_ref, *rest):
@@ -327,31 +327,45 @@
 def last_d_kernel(before, *refs):
     refs = Refs(refs)
     now_ref, prev_ref, ha_ref, hb_ref, speed_ref, perturb_ref, lap_u_ref, cells_hbm, cells_ref = refs.take(9)
+    u_ref, u_prev, source_ref, wavelet_hbm = refs.take(4)
     early_ref = refs.take() if before else None
-    out_ref, next_ref, record_ref = refs.take(3)
+    out_ref, next_ref, record_ref, u_out = refs.take(4)
+    u_next = refs.take()
     work = refs.take(3)
-    cells_smem, rows_ref, sems, table_sem = refs.take(4)
-    fetch = pltpu.make_async_copy(cells_hbm, cells_smem, table_sem)
-    fetch.start()
+    cells_smem, wavelet_ref, rows_ref, sems, table_sems = refs.take(5)
+    fetches = [
+        pltpu.make_async_copy(cells_hbm, cells_smem, table_sems.at[0]),
+        pltpu.make_async_copy(wavelet_hbm, wavelet_ref, table_sems.at[1]),
+    ]
+    for fetch in fetches:
+        fetch.start()
     _, side, _ = now_ref.shape
     prepare(work, now_ref, ha_ref, hb_ref, 0, band_weights(side))
+    for fetch in fetches:
+        fetch.wait()
+    last_step = wavelet_ref.shape[1] - 1
 
     def emit(z, block, centre, lap):
-        next_ref[z, block, :] = ((2.0 * centre - prev_ref[z, block, :]) + speed_ref[z, block, :] * lap) + (
-            perturb_ref[z, block, :] * lap_u_ref[z, block, :]
+        speed, lap_u = speed_ref[z, block, :], lap_u_ref[z, block, :]
+        next_ref[z, block, :] = ((2.0 * centre - prev_ref[z, block, :]) + speed * lap) + (
+            perturb_ref[z, block, :] * lap_u
         )
+        u_next[z, block, :] = (2.0 * u_ref[z, block, :] - u_prev[z, block, :]) + speed * lap_u
 
     def finish(part, parts):
-        store_out(next_ref, out_ref, sems, part, parts).start()
+        size = side // parts
+        add_source(u_next, source_ref, wavelet_ref, last_step, part * size, size)
+        store_out(next_ref, out_ref, sems.at[0], part, parts).start()
+        store_out(u_next, u_out, sems.at[1], part, parts).start()
 
     each_laplacian(work, now_ref, emit, finish, PARTS)
-    fetch.wait()
     if before:
         record_ref[pl.ds(0, before), :] = early_ref[...]
     fields = [now_ref, next_ref] if record_ref.shape[0] > before + 1 else [next_ref]
     gather_records(before, cells_smem, cells_ref, fields, record_ref, rows_ref)
     for part in range(PARTS):
-        store_out(next_ref, out_ref, sems, part, PARTS).wait()
+        store_out(next_ref, out_ref, sems.at[0], part, PARTS).wait()
+        store_out(u_next, u_out, sems.at[1], part, PARTS).wait()
 
 
 def last_w_kernel(*refs):
@@ -385,10 +399,13 @@
 def u_call(step, last, wavelet, source, u, u_prev, halo, speed, w, corr, local, aperture, tile_slot, lat_dev, tile_side):
     field = sds(u.shape)
     edge = sds((1, HALO) + u.shape[1:])
-    args = [source, in_hbm(wavelet), u, u_prev, *halo, speed, w] + ([corr] if step else [])
-    specs = [SMEM, HBM] + [VMEM] * (len(args) - 2)
+    args, specs = [u, *halo, w], [VMEM] * 4
     if not step:
-        args[7], specs[7] = in_hbm(w), HBM
+        args[3], specs[3] = in_hbm(w), HBM
+    if not last:
+        args, specs = args + [source, in_hbm(wavelet), u_prev, speed], specs + [SMEM, HBM, VMEM, VMEM]
+    if step:
+        args, specs = args + [corr], specs + [VMEM]
     ahead = local is not None
     if ahead:
         args, specs = args + list(local), specs + [VMEM] * 2
@@ -396,25 +413,24 @@
     cells = tile_side * tile_side
     capacity = n_tiles // 4
     rows, halos, lanes = work_space(*u.shape[:2])
-    scratch = [halos] + ([] if ahead else [rows, lanes])
-    scratch += [pltpu.SMEM(wavelet.shape, F32), pltpu.SemaphoreType.DMA((3,))]
+    scratch = [halos] + ([] if ahead else [rows, lanes]) + [pltpu.SemaphoreType.DMA((3,))]
+    if not last:
+        scratch += [pltpu.SMEM(wavelet.shape, F32)]
     if not step:
         scratch += [pltpu.VMEM(u.shape, F32)]
     if last:
         args += [in_hbm(aperture), in_hbm(tile_slot)]
         specs += [HBM, HBM]
-        outs = [sds((1,) + u.shape), field] + [sds((capacity, u.shape[0], cells))] * n_shot
-        kinds = [HBM] + [VMEM] * (1 + n_shot)
-        scratch = [pltpu.VMEM(u.shape, F32)] * 2 + scratch + [
+        outs = [field] + [sds((capacity, u.shape[0], cells))] * n_shot
+        scratch = [pltpu.VMEM(u.shape, F32)] + scratch + [
             pltpu.SMEM(aperture.shape, jnp.int32),
             pltpu.SMEM(tile_slot.shape, jnp.int32),
             *tile_scratch(n_shot, capacity, u.shape[0], cells, n_tiles),
-            pltpu.SemaphoreType.DMA((PARTS,)),
         ]
     else:
-        outs, kinds = [field] * 3 + [edge] * 2, [VMEM] * 5
+        outs = [field] * 3 + [edge] * 2
     body = functools.partial(u_kernel, step, last, ahead, (n_shot, lat_dev, tile_side))
-    return stencil_call(body, specs, args, outs, kinds, scratch)
+    return stencil_call(body, specs, args, outs, [VMEM] * len(outs), scratch)
 
 
 def w_bare_call(w, w_prev, halo, index, speed):
@@ -442,22 +458,25 @@
     return stencil_call(body, [VMEM] * len(args), args, outs, [VMEM] * 6, [halo_space(d.shape[1])] * 2)
 
 
-def last_d_call(step, d, d_prev, halo, speed, perturb, lap_u, cells, early):
+def last_d_call(step, d, d_prev, halo, speed, perturb, lap_u, cells, u, u_prev, source, wavelet, early):
     before = 0 if early is None else early.shape[0]
     n = cells.shape[1]
     fields = step + 1 - before
-    args = [d, d_prev, *halo, speed, perturb, lap_u, cells, cells] + ([early] if before else [])
+    args = [d, d_prev, *halo, speed, perturb, lap_u, in_hbm(cells), cells, u, u_prev, source, in_hbm(wavelet)]
     specs = [VMEM] * len(args)
-    specs[7] = HBM
-    scratch = work_space(*d.shape[:2]) + [
+    specs[7], specs[11], specs[12] = HBM, SMEM, HBM
+    if before:
+        args, specs = args + [early], specs + [VMEM]
+    scratch = [pltpu.VMEM(u.shape, F32)] + work_space(*d.shape[:2]) + [
         pltpu.SMEM(cells.shape, jnp.int32),
+        pltpu.SMEM(wavelet.shape, F32),
         pltpu.VMEM((fields, n, d.shape[-1]), F32),
-        pltpu.SemaphoreType.DMA((PARTS,)),
-        pltpu.SemaphoreType.DMA(()),
+        pltpu.SemaphoreType.DMA((2, PARTS)),
+        pltpu.SemaphoreType.DMA((2,)),
     ]
-    outs = [sds((1,) + d.shape), sds(d.shape), sds((step + 1, n))]
+    outs = [sds((1,) + d.shape), sds(d.shape), sds((step + 1, n)), sds((1,) + u.shape)]
     body = functools.partial(last_d_kernel, before)
-    return stencil_call(body, specs, args, outs, [HBM, VMEM, VMEM], scratch)
+    return stencil_call(body, specs, args, outs, [HBM, VMEM, VMEM, HBM], scratch)
 
 
 def last_w_call(w, w_prev, halo, speed, count, d_next):
@@ -675,7 +694,6 @@
     across = side // tile_side
     flat_ref = corr_ref.reshape(depth * side, side)
     places(aperture_ref, slot_ref, lat_dev, n_shot, capacity, seen_ref, place_ref)
-    tiles_ref[...] = jnp.zeros(tiles_ref.shape, F32)
 
     def tile_row(i, carry):
         for high in range(cells // side):
@@ -768,41 +786,33 @@
     return tuple(got)
 
 
-def edges_kernel(groups, *refs):
-    refs = Refs(refs)
-    fields = [refs.take(n) for n in groups]
+def edges_kernel(n, *refs):
+    fields, outs, sems = refs[:n], refs[n:-1], refs[-1]
+    depth = fields[0].shape[1]
+    low = jnp.where(place()[0] == 1, 0, depth - HALO)
     copies = []
-    outs = [refs.take(2) for _ in groups]
-    sems = refs.take()
-    for group, pair in zip(fields, outs):
-        depth = group[0].shape[1]
-        low = jnp.where(place()[0] == 1, 0, depth - HALO)
-        for out_ref, at in zip(pair, (low, depth - HALO - low)):
-            for index, field_ref in enumerate(group):
-                copies.append(
-                    pltpu.make_async_copy(field_ref.at[0, pl.ds(at, HALO)], out_ref.at[index], sems.at[len(copies)])
-                )
+    for out_ref, at in zip(outs, (low, depth - HALO - low)):
+        for index, field_ref in enumerate(fields):
+            copies.append(
+                pltpu.make_async_copy(field_ref.at[0, pl.ds(at, HALO)], out_ref.at[index], sems.at[len(copies)])
+            )
     for copy in copies:
         copy.start()
     for copy in copies:
         copy.wait()
 
 
-def first_edges(groups):
-    outs = []
-    for group in groups:
-        outs += [sds((len(group), HALO) + group[0].shape[2:])] * 2
-    fields = [in_hbm(field) for group in groups for field in group]
-    edges = pl.pallas_call(
-        functools.partial(edges_kernel, [len(group) for group in groups]),
-        out_shape=outs,
-        in_specs=[HBM] * len(fields),
-        out_specs=[VMEM] * len(outs),
-        scratch_shapes=[pltpu.SemaphoreType.DMA((2 * len(fields),))],
+def first_edges(fields):
+    n = len(fields)
+    edge = sds((n, HALO) + fields[0].shape[2:])
+    return pl.pallas_call(
+        functools.partial(edges_kernel, n),
+        out_shape=[edge, edge],
+        in_specs=[HBM] * n,
+        out_specs=[VMEM, VMEM],
+        scratch_shapes=[pltpu.SemaphoreType.DMA((2 * n,))],
         compiler_params=params(8),
-        name="edges",
-    )(*fields)
-    return [edges[2 * i : 2 * i + 2] for i in range(len(groups))]
+    )(*map(in_hbm, fields))
 
 
 def partners():
@@ -831,13 +841,9 @@
 def slab_parts(part):
     count = lax.axis_size("slab")
     parts = [part]
-    if count & (count - 1) == 0:
-        for bit in range(count.bit_length() - 1):
-            part = functools.reduce(jnp.add, parts)
-            parts = [part, lax.ppermute(part, "slab", [(s, s ^ (1 << bit)) for s in range(count)])]
-    else:
-        for k in range(1, count):
-            parts.append(lax.ppermute(part, "slab", [(s, (s + k) % count) for s in range(count)]))
+    for k in range(1, count):
+        to = [s ^ k for s in range(count)] if count & (count - 1) == 0 else [(s + k) % count for s in range(count)]
+        parts.append(lax.ppermute(part, "slab", list(enumerate(to))))
     return parts
 
 
@@ -866,9 +872,8 @@
     up, dp, wp = u_prev[0], du_prev[0], w_prev[0]
 
     tiling = (aperture, tile_slot, lat_dev, tile_side)
-    u_edges, dw_edges = first_edges([[u_now], [du_now, w_now]])
-    u_halo = swap(u_edges)
-    dw_halo = swap(dw_edges)
+    u_halo = swap(first_edges([u_now]))
+    dw_halo = swap(first_edges([du_now, w_now]))
     outgoing, table = pack_call(aperture, tile_slot, model_tiles, capacity)
     incoming = exchange(outgoing)
     count, outer = count_call(receiver_cells, depth, side)
@@ -896,9 +901,11 @@
         w_halo = swap(edges[2:])
     u, up, d, dp, w, wp = u_next, u, d_next, d, w_next, w
     step = steps - 1
-    u_final, lap, *returning = u_call(step, True, wavelet, source_cell, u, up, u_halo, speed, w, corr, u_local, *tiling)
+    lap, *returning = u_call(step, True, wavelet, source_cell, u, up, u_halo, speed, w, corr, u_local, *tiling)
     arrived = exchange(returning)
-    d_final, d_next, traces = last_d_call(step, d, dp, d_halo, speed, perturb, lap, receiver_cells, traces)
+    d_final, d_next, traces, u_final = last_d_call(
+        step, d, dp, d_halo, speed, perturb, lap, receiver_cells, u, up, source_cell, wavelet, traces
+    )
     parts = slab_parts(traces)
     (w_final,) = last_w_call(w, wp, w_halo, speed, count, d_next)
     sensitivity, traces = finish_call(table, arrived, parts, lat_dev)

time: 87.2 us -> 91.1 us (1.045)
  starting transfers between devices: 35.3 us -> 37.6 us
  Pallas kernels: 23.4 us -> 25.4 us
    ppermute x14, waiting for transfers between devices: 18.1 us -> 12.6 us  [exchange(): got[k] = lax.ppermute(block, 'shot', moves) if moves else block]
    ppermute x16, waiting for transfers between devices: 8.55 us -> 11.5 us  [swap(): got.append(lax.ppermute(edge, ('shot', 'slab'), sorted(pairs.items())))]
    ppermute x2 -> x3, waiting for transfers between devices: 0.01 us -> 2.11 us  [slab_parts(): parts.append(lax.ppermute(part, 'slab', list(enumerate(to))))]
    ppermute x14, starting transfers between devices: 13.2 us -> 14.7 us  [exchange(): got[k] = lax.ppermute(block, 'shot', moves) if moves else block]
    pallas_call x8, Pallas kernels: 14.2 us -> 15.3 us  [stencil_call(): pl.pallas_call(body, out_shape=outs, in_specs=in_specs, out_specs=kinds,...]
    pallas_call x1 -> x2, Pallas kernels: 1.39 us -> 2.28 us  [first_edges(): pl.pallas_call(functools.partial(edges_kernel, n), out_shape=[edge, edge]...]
    ppermute x2 -> x3, starting transfers between devices: 3.99 us -> 4.44 us  [slab_parts(): parts.append(lax.ppermute(part, 'slab', list(enumerate(to))))]
  transfers between devices with their start and end apart: 32 -> 33, of which waited for: 11 -> 14; matrix products, arithmetic and copies ran while one was open for 0% -> 0% of each run, Pallas kernels for 23% -> 21%
where the time goes in v2:
time: 91.1 us; the launch traced here: 90.8 us
  starting transfers between devices  37.6 us (41%)
  waiting for transfers between devices  26.2 us (29%)
  Pallas kernels  25.4 us (28%)
  between operations  1.6 us (2%)
    ppermute x16, starting transfers between devices, swap(): got.append(lax.ppermute(edge, ('shot', 'slab'), sorted(pairs.items())))  18.4 us
    pallas_call x8, Pallas kernels, stencil_call(): pl.pallas_call(body, out_shape=outs, in_specs=in_specs, out_specs=kinds,...  15.3 us
    ppermute x14, starting transfers between devices, exchange(): got[k] = lax.ppermute(block, 'shot', moves) if moves else block  14.7 us
    ppermute x14, waiting for transfers between devices, exchange(): got[k] = lax.ppermute(block, 'shot', moves) if moves else block  12.6 us
    ppermute x16, waiting for transfers between devices, swap(): got.append(lax.ppermute(edge, ('shot', 'slab'), sorted(pairs.items())))  11.5 us
    ppermute x3, starting transfers between devices, slab_parts(): parts.append(lax.ppermute(part, 'slab', list(enumerate(to))))  4.44 us
    pallas_call x2, Pallas kernels, first_edges(): pl.pallas_call(functools.partial(edges_kernel, n), out_shape=[edge, edge]...  2.28 us
    ppermute x3, waiting for transfers between devices, slab_parts(): parts.append(lax.ppermute(part, 'slab', list(enumerate(to))))  2.11 us
  transfers between devices with their start and end apart: 33, of which 14 were waited for; matrix products, arithmetic and copies ran while one was open for 0% of the time, Pallas kernels for 21%

profile of v2, /device:TPU:0, one launch (start us, length us, event | category | flops | bytes accessed | tf_op | source)
XLA Modules:
  0.0 90.8 jit_solution(11051333169599595910)
XLA Ops:
  0.6 1.9 %pack.1 = (f32[4,8,1024]{2,1,0:T(8,128)S(1)}, f32[4,8,1024]{2,1,0:T(8,128)S(1)}, f32[4,8,1024]{2,1,0:T(8,128)S(1)}, f32[4,8,1024]{2,1,0:T(8,128)S(1)}, f32[4,8,1...) custom-call(s32[8,16]{1,0:T(8,128)} %refs_7_.2, ...), custom_call_target="tpu_custom_call" | custom-call | tf_op jit(solution)/shard_map/pack/pallas_call | solution.py:637
  3.1 2.6 %collective-permute-start.7 = (f32[4,8,1024]{2,1,0:T(8,128)S(1)}, f32[4,8,1024]{2,1,0:T(8,128)S(1)}, u32[]{:S(2)}, u32[]{:S(2)}) collective-permute-start(f32[4,8,1024]{2,1,0:T(8,128)S(1)} %get-tuple-element.74), channel_id=1, source_target_pairs={{0,8},{4,12},{8,0},{12,4},{16,24},{20,28},{24,16},{28,20},{1,9},{5... | collective-permute-start | bytes 393224 | tf_op jit(solution)/shard_map/ppermute | solution.py:837
  11.7 1.9 %collective-permute-done.8.rest_3_ = f32[4,8,1024]{2,1,0:T(8,128)S(1)} collective-permute-done((f32[4,8,1024]{2,1,0:T(8,128)S(1)}, f32[4,8,1024]{2,1,0:T(8,128)S(1)}, u32[]{:S(2)}, u32[]{:S(2)}) %collective-permute-start.8) | collective-permute-done | bytes 131104 | tf_op jit(solution)/shard_map/ppermute | solution.py:837
  15.4 3.5 %collective-permute-start = (f32[1,4,128,128]{3,2,1,0:T(8,128)S(1)}, f32[1,4,128,128]{3,2,1,0:T(8,128)S(1)}, u32[]{:S(2)}, u32[]{:S(2)}) collective-permute-start(f32[1,4,128,128]{3,2,1,0:T(8,128)S(1)} %get-tuple-element.65), channel_id=1, source_target_pairs={{0,1},{1,0},{2,3},{3,2},{4,5},{5,4},{6,7},{7,6},{8,9},{9,8},{10,11... | collective-permute-start | bytes 786440 | tf_op jit(solution)/shard_map/ppermute | solution.py:785
  18.9 1.8 %collective-permute-done.11.rest_6_ = f32[4,8,1024]{2,1,0:T(8,128)S(1)} collective-permute-done((f32[4,8,1024]{2,1,0:T(8,128)S(1)}, f32[4,8,1024]{2,1,0:T(8,128)S(1)}, u32[]{:S(2)}, u32[]{:S(2)}) %collective-permute-start.11) | collective-permute-done | bytes 131104 | tf_op jit(solution)/shard_map/ppermute | solution.py:837
  20.7 1.7 %collective-permute-start.12 = (f32[4,8,1024]{2,1,0:T(8,128)S(1)}, f32[4,8,1024]{2,1,0:T(8,128)S(1)}, u32[]{:S(2)}, u32[]{:S(2)}) collective-permute-start(f32[4,8,1024]{2,1,0:T(8,128)S(1)} %get-tuple-element.79), channel_id=1, source_target_pairs={{0,28},{4,24},{8,20},{12,16},{16,12},{20,8},{24,4},{28,0},{1,29},{... | collective-permute-start | bytes 393224 | tf_op jit(solution)/shard_map/ppermute | solution.py:837
  23.5 3.7 %collective-permute-done.12.rest_7_ = f32[4,8,1024]{2,1,0:T(8,128)S(1)} collective-permute-done((f32[4,8,1024]{2,1,0:T(8,128)S(1)}, f32[4,8,1024]{2,1,0:T(8,128)S(1)}, u32[]{:S(2)}, u32[]{:S(2)}) %collective-permute-start.12) | collective-permute-done | bytes 131104 | tf_op jit(solution)/shard_map/ppermute | solution.py:837
  27.3 1.7 %perturb.1.perturb_ref.refs_5_ = f32[8,128,128]{2,1,0:T(8,128)S(1)} custom-call(s32[8,16]{1,0:T(8,128)S(1)} %copy-done.7, s32[64]{0:T(128)S(1)} %copy-done.9, f32[4,8,1024]{2,1,0:T(8,128)S(1)} %get-tuple-element.72.rest_0_, f32[4,8,1024]{2,1,0:T(8,128)S(1)} %collective-permute-done.6.rest_1_, f32[4,8,1024]{2,1,0:T(8,128)S(1)} %collective-permute-done.7.rest_2_, ...), custom_call_target="tpu_custom_call" | custom-call | tf_op jit(solution)/shard_map/perturb/pallas_call | solution.py:722
  29.1 1.9 %shard_map.165 = (f32[8,128,128]{2,1,0:T(8,128)S(1)}, f32[8,128,128]{2,1,0:T(8,128)S(1)}, f32[8,128,128]{2,1,0:T(8,128)S(1)}, f32[1,4,128,128]{3,2,1,0:T(8,128)S(1)}, f32[1,4,128,128]{3,2,1,0:T(8,128)S(1)}) custom-call(f32[8,128,128]{2,1,0:T(8,128)S(1)} %bitcast.17, f32[1,4,128,128]{3,2,1,0:T(8,128)S(1)} %collective-permute-done.refs_1_, ...), custom_call_target="tpu_custom_call" | custom-call | tf_op jit(solution)/shard_map/pallas_call | solution.py:394
  31.0 2.8 %collective-permute-start.2 = (f32[1,4,128,128]{3,2,1,0:T(8,128)S(1)}, f32[1,4,128,128]{3,2,1,0:T(8,128)S(1)}, u32[]{:S(2)}, u32[]{:S(2)}) collective-permute-start(f32[1,4,128,128]{3,2,1,0:T(8,128)S(1)} %get-tuple-element.68), channel_id=1, source_target_pairs={{0,1},{1,0},{2,3},{3,2},{4,5},{5,4},{6,7},{7,6},{8,9},{9,8},{10,11... | collective-permute-start | bytes 786440 | tf_op jit(solution)/shard_map/ppermute | solution.py:785
  37.5 2.0 %collective-permute-start.17 = (f32[1,4,128,128]{3,2,1,0:T(8,128)S(1)}, f32[1,4,128,128]{3,2,1,0:T(8,128)S(1)}, u32[]{:S(2)}, u32[]{:S(2)}) collective-permute-start(f32[1,4,128,128]{3,2,1,0:T(8,128)S(1)} %get-tuple-element.92), channel_id=1, source_target_pairs={{0,1},{1,0},{2,3},{3,2},{4,5},{5,4},{6,7},{7,6},{8,9},{9,8},{10,11... | collective-permute-start | bytes 786440 | tf_op jit(solution)/shard_map/ppermute | solution.py:785
  42.4 3.1 %collective-permute-start.13 = (f32[1,4,128,128]{3,2,1,0:T(8,128)S(1)}, f32[1,4,128,128]{3,2,1,0:T(8,128)S(1)}, u32[]{:S(2)}, u32[]{:S(2)}) collective-permute-start(f32[1,4,128,128]{3,2,1,0:T(8,128)S(1)} %get-tuple-element.86), channel_id=1, source_target_pairs={{0,1},{1,0},{2,3},{3,2},{4,5},{5,4},{6,7},{7,6},{8,9},{9,8},{10,11... | collective-permute-start | bytes 786440 | tf_op jit(solution)/shard_map/ppermute | solution.py:785
  47.4 4.8 %collective-permute-done.17.refs_10_ = f32[1,4,128,128]{3,2,1,0:T(8,128)S(1)} collective-permute-done((f32[1,4,128,128]{3,2,1,0:T(8,128)S(1)}, f32[1,4,128,128]{3,2,1,0:T(8,128)S(1)}, u32[]{:S(2)}, u32[]{:S(2)}) %collective-permute-start.17) | collective-permute-done | bytes 262176 | tf_op jit(solution)/shard_map/ppermute | solution.py:785
  52.2 1.7 %shard_map.171 = (f32[8,128,128]{2,1,0:T(8,128)S(1)}, f32[8,128,128]{2,1,0:T(8,128)S(1)}, f32[1,4,128,128]{3,2,1,0:T(8,128)S(1)}, f32[1,4,128,128]{3,2,1,0:T(8,1...) custom-call(f32[8,128,128]{2,1,0:T(8,128)S(1)} %bitcast.12, ...), custom_call_target="tpu_custom_call" | custom-call | tf_op jit(solution)/shard_map/pallas_call | solution.py:394
  53.9 3.3 %collective-permute-done.13.refs_1_ = f32[1,4,128,128]{3,2,1,0:T(8,128)S(1)} collective-permute-done((f32[1,4,128,128]{3,2,1,0:T(8,128)S(1)}, f32[1,4,128,128]{3,2,1,0:T(8,128)S(1)}, u32[]{:S(2)}, u32[]{:S(2)}) %collective-permute-start.13) | collective-permute-done | bytes 262176 | tf_op jit(solution)/shard_map/ppermute | solution.py:785
  57.2 2.5 %shard_map.172 = (f32[8,128,128]{2,1,0:T(8,128)S(1)}, f32[4,8,1024]{2,1,0:T(8,128)S(1)}, f32[4,8,1024]{2,1,0:T(8,128)S(1)}, f32[4,8,1024]{2,1,0:T(8,128)S(1)}, f...) custom-call(f32[8,128,128]{2,1,0:T(8,128)S(1)} %get-tuple-element.85, ...), custom_call_target="tpu_custom_call" | custom-call | tf_op jit(solution)/shard_map/pallas_call | solution.py:394
  61.7 1.8 %collective-permute-start.26 = (f32[1,4,128,128]{3,2,1,0:T(8,128)S(1)}, f32[1,4,128,128]{3,2,1,0:T(8,128)S(1)}, u32[]{:S(2)}, u32[]{:S(2)}) collective-permute-start(f32[1,4,128,128]{3,2,1,0:T(8,128)S(1)} %get-tuple-element.112), channel_id=1, source_target_pairs={{0,1},{1,0},{2,3},{3,2},{4,5},{5,4},{6,7},{7,6},{8,9},{9,8},{10,11... | collective-permute-start | bytes 786440 | tf_op jit(solution)/shard_map/ppermute | solution.py:785
  66.2 1.8 %collective-permute-start.31 = (f32[1,4,128,128]{3,2,1,0:T(8,128)S(1)}, f32[1,4,128,128]{3,2,1,0:T(8,128)S(1)}, u32[]{:S(2)}, u32[]{:S(2)}) collective-permute-start(f32[1,4,128,128]{3,2,1,0:T(8,128)S(1)} %get-tuple-element.119), channel_id=1, source_target_pairs={{0,1},{1,0},{2,3},{3,2},{4,5},{5,4},{6,7},{7,6},{8,9},{9,8},{10,11... | collective-permute-start | bytes 786440 | tf_op jit(solution)/shard_map/ppermute | solution.py:785
  70.8 2.4 %collective-permute-start.24 = (f32[4,8,1024]{2,1,0:T(8,128)S(1)}, f32[4,8,1024]{2,1,0:T(8,128)S(1)}, u32[]{:S(2)}, u32[]{:S(2)}) collective-permute-start(f32[4,8,1024]{2,1,0:T(8,128)S(1)} %get-tuple-element.109), channel_id=1, source_target_pairs={{0,24},{4,28},{8,16},{12,20},{16,8},{20,12},{24,0},{28,4},{1,25},{... | collective-permute-start | bytes 393224 | tf_op jit(solution)/shard_map/ppermute | solution.py:837
  74.5 3.5 %shard_map.174 = (f32[1,8,128,128]{3,2,1,0:T(8,128)}, f32[8,128,128]{2,1,0:T(8,128)S(1)}, f32[3,256]{1,0:T(4,128)S(1)}, f32[1,8,128,128]{3,2,1,0:T(8,128)}) custom-call(f32[8,128,128]{2,1,0:T(8,128)S(1)} %get-tuple-element.111.refs_0_, f32[8,128,128]{2,1,0:T(8,128)S(1)} %get-tuple-element.88.refs_1_.rest_0_, ...), custom_call_target="tpu_custom_call" | custom-call | tf_op jit(solution)/shard_map/pallas_call | solution.py:394
  78.0 2.7 %collective-permute-done.23.refs_5_ = f32[4,8,1024]{2,1,0:T(8,128)S(1)} collective-permute-done((f32[4,8,1024]{2,1,0:T(8,128)S(1)}, f32[4,8,1024]{2,1,0:T(8,128)S(1)}, u32[]{:S(2)}, u32[]{:S(2)}) %collective-permute-start.23) | collective-permute-done | bytes 131104 | tf_op jit(solution)/shard_map/ppermute | solution.py:837
  80.8 2.1 %collective-permute-start.28 = (f32[3,256]{1,0:T(4,128)S(1)}, f32[3,256]{1,0:T(4,128)S(1)}, u32[]{:S(2)}, u32[]{:S(2)}) collective-permute-start(f32[3,256]{1,0:T(4,128)S(1)} %get-tuple-element.115.refs_8_), channel_id=1, source_target_pairs={{0,1},{1,0},{2,3},{3,2},{4,5},{5,4},{6,7},{7,6},{8,9},{9,8},{10,11... | collective-permute-start | bytes 9224 | tf_op jit(solution)/shard_map/ppermute | solution.py:846
  85.2 1.9 %shard_map.175 = f32[1,8,128,128]{3,2,1,0:T(8,128)} custom-call(f32[8,128,128]{2,1,0:T(8,128)S(1)} %get-tuple-element.99.refs_3_.refs_0_, f32[8,128,128]{2,1,0:T(8,128)S(1)} %get-tuple-element.83.refs_3_.refs_2_.refs_1_, f32[1,4,128,128]{3,2,1,0:T(8,128)S(1)} %collective-permute-done.31.refs_2_, f32[1,4,128,128]{3,2,1,0:T(8,128)S(1)} %collective-permute-done.32.refs_3_, ...), custom_call_target="tpu_custom_call" | custom-call | tf_op jit(solution)/shard_map/pallas_call | solution.py:394
  87.3 1.9 %collective-permute-done.30.refs_11_ = f32[3,256]{1,0:T(4,128)S(1)} collective-permute-done((f32[3,256]{1,0:T(4,128)S(1)}, f32[3,256]{1,0:T(4,128)S(1)}, u32[]{:S(2)}, u32[]{:S(2)}) %collective-permute-start.30) | collective-permute-done | bytes 3104 | tf_op jit(solution)/shard_map/ppermute | solution.py:846
  (78 shorter events, 30.5 us)
Async XLA Ops:
  2.5 6.6 %collective-permute-start.6 = (f32[4,8,1024]{2,1,0:T(8,128)S(1)}, f32[4,8,1024]{2,1,0:T(8,128)S(1)}, u32[]{:S(2)}, u32[]{:S(2)}) collective-permute-start(f32[4,8,1024]{2,1,0:T(8,128)S(1)} %get-tuple-element.73), channel_id=1, source_target_pairs={{0,4},{4,0},{8,12},{12,8},{16,20},{20,16},{24,28},{28,24},{1,5},{5... | collective-permute-start | bytes 393224 | tf_op jit(solution)/shard_map/ppermute | solution.py:837
  3.1 7.6 %collective-permute-start.7 = (f32[4,8,1024]{2,1,0:T(8,128)S(1)}, f32[4,8,1024]{2,1,0:T(8,128)S(1)}, u32[]{:S(2)}, u32[]{:S(2)}) collective-permute-start(f32[4,8,1024]{2,1,0:T(8,128)S(1)} %get-tuple-element.74), channel_id=1, source_target_pairs={{0,8},{4,12},{8,0},{12,4},{16,24},{20,28},{24,16},{28,20},{1,9},{5... | collective-permute-start | bytes 393224 | tf_op jit(solution)/shard_map/ppermute | solution.py:837
  6.8 27.0 %collective-permute-start.4 = (f32[2,4,128,128]{3,2,1,0:T(8,128)S(1)}, f32[2,4,128,128]{3,2,1,0:T(8,128)S(1)}, u32[]{:S(2)}, u32[]{:S(2)}) collective-permute-start(f32[2,4,128,128]{3,2,1,0:T(8,128)S(1)} %get-tuple-element.70), channel_id=1, source_target_pairs={{0,1},{1,0},{2,3},{3,2},{4,5},{5,4},{6,7},{7,6},{8,9},{9,8},{10,11... | collective-permute-start | bytes 1572872 | tf_op jit(solution)/shard_map/ppermute | solution.py:785
  8.5 25.3 %collective-permute-start.5 = (f32[2,4,128,128]{3,2,1,0:T(8,128)S(1)}, f32[2,4,128,128]{3,2,1,0:T(8,128)S(1)}, u32[]{:S(2)}, u32[]{:S(2)}) collective-permute-start(f32[2,4,128,128]{3,2,1,0:T(8,128)S(1)} %get-tuple-element.71), channel_id=1, source_target_pairs={{0,4},{1,2},{2,1},{3,7},{4,0},{5,6},{6,5},{7,3},{8,12},{9,10},{10,... | collective-permute-start | bytes 1572872 | tf_op jit(solution)/shard_map/ppermute | solution.py:785
  10.7 8.2 %collective-permute-start.10 = (f32[4,8,1024]{2,1,0:T(8,128)S(1)}, f32[4,8,1024]{2,1,0:T(8,128)S(1)}, u32[]{:S(2)}, u32[]{:S(2)}) collective-permute-start(f32[4,8,1024]{2,1,0:T(8,128)S(1)} %get-tuple-element.77), channel_id=1, source_target_pairs={{0,20},{4,16},{8,28},{12,24},{16,4},{20,0},{24,12},{28,8},{1,21},{... | collective-permute-start | bytes 393224 | tf_op jit(solution)/shard_map/ppermute | solution.py:837
  13.6 7.1 %collective-permute-start.11 = (f32[4,8,1024]{2,1,0:T(8,128)S(1)}, f32[4,8,1024]{2,1,0:T(8,128)S(1)}, u32[]{:S(2)}, u32[]{:S(2)}) collective-permute-start(f32[4,8,1024]{2,1,0:T(8,128)S(1)} %get-tuple-element.78), channel_id=1, source_target_pairs={{0,24},{4,28},{8,16},{12,20},{16,8},{20,12},{24,0},{28,4},{1,25},{... | collective-permute-start | bytes 393224 | tf_op jit(solution)/shard_map/ppermute | solution.py:837
  15.4 13.6 %collective-permute-start = (f32[1,4,128,128]{3,2,1,0:T(8,128)S(1)}, f32[1,4,128,128]{3,2,1,0:T(8,128)S(1)}, u32[]{:S(2)}, u32[]{:S(2)}) collective-permute-start(f32[1,4,128,128]{3,2,1,0:T(8,128)S(1)} %get-tuple-element.65), channel_id=1, source_target_pairs={{0,1},{1,0},{2,3},{3,2},{4,5},{5,4},{6,7},{7,6},{8,9},{9,8},{10,11... | collective-permute-start | bytes 786440 | tf_op jit(solution)/shard_map/ppermute | solution.py:785
  18.9 10.1 %collective-permute-start.1 = (f32[1,4,128,128]{3,2,1,0:T(8,128)S(1)}, f32[1,4,128,128]{3,2,1,0:T(8,128)S(1)}, u32[]{:S(2)}, u32[]{:S(2)}) collective-permute-start(f32[1,4,128,128]{3,2,1,0:T(8,128)S(1)} %get-tuple-element.66), channel_id=1, source_target_pairs={{0,4},{1,2},{2,1},{3,7},{4,0},{5,6},{6,5},{7,3},{8,12},{9,10},{10,... | collective-permute-start | bytes 786440 | tf_op jit(solution)/shard_map/ppermute | solution.py:785
  31.0 10.0 %collective-permute-start.2 = (f32[1,4,128,128]{3,2,1,0:T(8,128)S(1)}, f32[1,4,128,128]{3,2,1,0:T(8,128)S(1)}, u32[]{:S(2)}, u32[]{:S(2)}) collective-permute-start(f32[1,4,128,128]{3,2,1,0:T(8,128)S(1)} %get-tuple-element.68), channel_id=1, source_target_pairs={{0,1},{1,0},{2,3},{3,2},{4,5},{5,4},{6,7},{7,6},{8,9},{9,8},{10,11... | collective-permute-start | bytes 786440 | tf_op jit(solution)/shard_map/ppermute | solution.py:785
  33.8 7.2 %collective-permute-start.3 = (f32[1,4,128,128]{3,2,1,0:T(8,128)S(1)}, f32[1,4,128,128]{3,2,1,0:T(8,128)S(1)}, u32[]{:S(2)}, u32[]{:S(2)}) collective-permute-start(f32[1,4,128,128]{3,2,1,0:T(8,128)S(1)} %get-tuple-element.69), channel_id=1, source_target_pairs={{0,4},{1,2},{2,1},{3,7},{4,0},{5,6},{6,5},{7,3},{8,12},{9,10},{10,... | collective-permute-start | bytes 786440 | tf_op jit(solution)/shard_map/ppermute | solution.py:785
  36.4 10.2 %collective-permute-start.15 = (f32[1,4,128,128]{3,2,1,0:T(8,128)S(1)}, f32[1,4,128,128]{3,2,1,0:T(8,128)S(1)}, u32[]{:S(2)}, u32[]{:S(2)}) collective-permute-start(f32[1,4,128,128]{3,2,1,0:T(8,128)S(1)} %get-tuple-element.90), channel_id=1, source_target_pairs={{0,1},{1,0},{2,3},{3,2},{4,5},{5,4},{6,7},{7,6},{8,9},{9,8},{10,11... | collective-permute-start | bytes 786440 | tf_op jit(solution)/shard_map/ppermute | solution.py:785
  37.5 9.9 %collective-permute-start.16 = (f32[1,4,128,128]{3,2,1,0:T(8,128)S(1)}, f32[1,4,128,128]{3,2,1,0:T(8,128)S(1)}, u32[]{:S(2)}, u32[]{:S(2)}) collective-permute-start(f32[1,4,128,128]{3,2,1,0:T(8,128)S(1)} %get-tuple-element.91), channel_id=1, source_target_pairs={{0,4},{1,2},{2,1},{3,7},{4,0},{5,6},{6,5},{7,3},{8,12},{9,10},{10,... | collective-permute-start | bytes 786440 | tf_op jit(solution)/shard_map/ppermute | solution.py:785
  37.5 14.7 %collective-permute-start.17 = (f32[1,4,128,128]{3,2,1,0:T(8,128)S(1)}, f32[1,4,128,128]{3,2,1,0:T(8,128)S(1)}, u32[]{:S(2)}, u32[]{:S(2)}) collective-permute-start(f32[1,4,128,128]{3,2,1,0:T(8,128)S(1)} %get-tuple-element.92), channel_id=1, source_target_pairs={{0,1},{1,0},{2,3},{3,2},{4,5},{5,4},{6,7},{7,6},{8,9},{9,8},{10,11... | collective-permute-start | bytes 786440 | tf_op jit(solution)/shard_map/ppermute | solution.py:785
  41.0 11.2 %collective-permute-start.18 = (f32[1,4,128,128]{3,2,1,0:T(8,128)S(1)}, f32[1,4,128,128]{3,2,1,0:T(8,128)S(1)}, u32[]{:S(2)}, u32[]{:S(2)}) collective-permute-start(f32[1,4,128,128]{3,2,1,0:T(8,128)S(1)} %get-tuple-element.93), channel_id=1, source_target_pairs={{0,4},{1,2},{2,1},{3,7},{4,0},{5,6},{6,5},{7,3},{8,12},{9,10},{10,... | collective-permute-start | bytes 786440 | tf_op jit(solution)/shard_map/ppermute | solution.py:785
  42.4 14.8 %collective-permute-start.13 = (f32[1,4,128,128]{3,2,1,0:T(8,128)S(1)}, f32[1,4,128,128]{3,2,1,0:T(8,128)S(1)}, u32[]{:S(2)}, u32[]{:S(2)}) collective-permute-start(f32[1,4,128,128]{3,2,1,0:T(8,128)S(1)} %get-tuple-element.86), channel_id=1, source_target_pairs={{0,1},{1,0},{2,3},{3,2},{4,5},{5,4},{6,7},{7,6},{8,9},{9,8},{10,11... | collective-permute-start | bytes 786440 | tf_op jit(solution)/shard_map/ppermute | solution.py:785
  46.6 10.7 %collective-permute-start.14 = (f32[1,4,128,128]{3,2,1,0:T(8,128)S(1)}, f32[1,4,128,128]{3,2,1,0:T(8,128)S(1)}, u32[]{:S(2)}, u32[]{:S(2)}) collective-permute-start(f32[1,4,128,128]{3,2,1,0:T(8,128)S(1)} %get-tuple-element.87), channel_id=1, source_target_pairs={{0,4},{1,2},{2,1},{3,7},{4,0},{5,6},{6,5},{7,3},{8,12},{9,10},{10,... | collective-permute-start | bytes 786440 | tf_op jit(solution)/shard_map/ppermute | solution.py:785
  61.1 7.0 %collective-permute-start.21 = (f32[4,8,1024]{2,1,0:T(8,128)S(1)}, f32[4,8,1024]{2,1,0:T(8,128)S(1)}, u32[]{:S(2)}, u32[]{:S(2)}) collective-permute-start(f32[4,8,1024]{2,1,0:T(8,128)S(1)} %get-tuple-element.106), channel_id=1, source_target_pairs={{0,12},{4,8},{8,4},{12,0},{16,28},{20,24},{24,20},{28,16},{1,13},{... | collective-permute-start | bytes 393224 | tf_op jit(solution)/shard_map/ppermute | solution.py:837
  61.7 9.2 %collective-permute-start.26 = (f32[1,4,128,128]{3,2,1,0:T(8,128)S(1)}, f32[1,4,128,128]{3,2,1,0:T(8,128)S(1)}, u32[]{:S(2)}, u32[]{:S(2)}) collective-permute-start(f32[1,4,128,128]{3,2,1,0:T(8,128)S(1)} %get-tuple-element.112), channel_id=1, source_target_pairs={{0,1},{1,0},{2,3},{3,2},{4,5},{5,4},{6,7},{7,6},{8,9},{9,8},{10,11... | collective-permute-start | bytes 786440 | tf_op jit(solution)/shard_map/ppermute | solution.py:785
  63.5 9.7 %collective-permute-start.27 = (f32[1,4,128,128]{3,2,1,0:T(8,128)S(1)}, f32[1,4,128,128]{3,2,1,0:T(8,128)S(1)}, u32[]{:S(2)}, u32[]{:S(2)}) collective-permute-start(f32[1,4,128,128]{3,2,1,0:T(8,128)S(1)} %get-tuple-element.113), channel_id=1, source_target_pairs={{0,4},{1,2},{2,1},{3,7},{4,0},{5,6},{6,5},{7,3},{8,12},{9,10},{10,... | collective-permute-start | bytes 786440 | tf_op jit(solution)/shard_map/ppermute | solution.py:785
  66.2 16.6 %collective-permute-start.31 = (f32[1,4,128,128]{3,2,1,0:T(8,128)S(1)}, f32[1,4,128,128]{3,2,1,0:T(8,128)S(1)}, u32[]{:S(2)}, u32[]{:S(2)}) collective-permute-start(f32[1,4,128,128]{3,2,1,0:T(8,128)S(1)} %get-tuple-element.119), channel_id=1, source_target_pairs={{0,1},{1,0},{2,3},{3,2},{4,5},{5,4},{6,7},{7,6},{8,9},{9,8},{10,11... | collective-permute-start | bytes 786440 | tf_op jit(solution)/shard_map/ppermute | solution.py:785
  68.1 15.8 %collective-permute-start.32 = (f32[1,4,128,128]{3,2,1,0:T(8,128)S(1)}, f32[1,4,128,128]{3,2,1,0:T(8,128)S(1)}, u32[]{:S(2)}, u32[]{:S(2)}) collective-permute-start(f32[1,4,128,128]{3,2,1,0:T(8,128)S(1)} %get-tuple-element.120), channel_id=1, source_target_pairs={{0,4},{1,2},{2,1},{3,7},{4,0},{5,6},{6,5},{7,3},{8,12},{9,10},{10,... | collective-permute-start | bytes 786440 | tf_op jit(solution)/shard_map/ppermute | solution.py:785
  69.4 11.4 %collective-permute-start.23 = (f32[4,8,1024]{2,1,0:T(8,128)S(1)}, f32[4,8,1024]{2,1,0:T(8,128)S(1)}, u32[]{:S(2)}, u32[]{:S(2)}) collective-permute-start(f32[4,8,1024]{2,1,0:T(8,128)S(1)} %get-tuple-element.108), channel_id=1, source_target_pairs={{0,20},{4,16},{8,28},{12,24},{16,4},{20,0},{24,12},{28,8},{1,21},{... | collective-permute-start | bytes 393224 | tf_op jit(solution)/shard_map/ppermute | solution.py:837
  70.8 16.2 %collective-permute-start.24 = (f32[4,8,1024]{2,1,0:T(8,128)S(1)}, f32[4,8,1024]{2,1,0:T(8,128)S(1)}, u32[]{:S(2)}, u32[]{:S(2)}) collective-permute-start(f32[4,8,1024]{2,1,0:T(8,128)S(1)} %get-tuple-element.109), channel_id=1, source_target_pairs={{0,24},{4,28},{8,16},{12,20},{16,8},{20,12},{24,0},{28,4},{1,25},{... | collective-permute-start | bytes 393224 | tf_op jit(solution)/shard_map/ppermute | solution.py:837
  73.2 13.9 %collective-permute-start.25 = (f32[4,8,1024]{2,1,0:T(8,128)S(1)}, f32[4,8,1024]{2,1,0:T(8,128)S(1)}, u32[]{:S(2)}, u32[]{:S(2)}) collective-permute-start(f32[4,8,1024]{2,1,0:T(8,128)S(1)} %get-tuple-element.110), channel_id=1, source_target_pairs={{0,28},{4,24},{8,20},{12,16},{16,12},{20,8},{24,4},{28,0},{1,29},{... | collective-permute-start | bytes 393224 | tf_op jit(solution)/shard_map/ppermute | solution.py:837
  (19 other events, 92.1 us)

commit v3 on v2

--- a/solution.py
+++ b/solution.py
@@ -225,10 +225,10 @@
     if not ahead:
         local_work = refs.take(2)
     own_sems = refs.take()
-    copies = []
+    copies, late = [], []
     if not last:
         wavelet_ref = refs.take()
-        copies.append(pltpu.make_async_copy(wavelet_hbm, wavelet_ref, own_sems.at[0]))
+        late.append(pltpu.make_async_copy(wavelet_hbm, wavelet_ref, own_sems.at[0]))
     w_ref = w_in
     if not step:
         w_ref = refs.take()
@@ -240,8 +240,8 @@
         fetched = refs.take(2)
         tiles_ref, seen_ref, place_ref = refs.take(3)
         for i, (a, b) in enumerate(zip(tables, fetched)):
-            copies.append(pltpu.make_async_copy(a, b, own_sems.at[1 + i]))
-    for copy in copies:
+            late.append(pltpu.make_async_copy(a, b, own_sems.at[1 + i]))
+    for copy in copies + late:
         copy.start()
     _, side, _ = now_ref.shape
     work = (local_work[0], halo_ref, local_work[1])
@@ -259,6 +259,8 @@
             next_ref[z, block, :] = (2.0 * centre - prev_ref[z, block, :]) + speed_ref[z, block, :] * lap
 
     each_laplacian(work, now_ref, emit)
+    for copy in late:
+        copy.wait()
     if last:
         pack_back(*tiles[1:], *fetched, corr_ref, blocks, tiles_ref, seen_ref, place_ref)
     else:
@@ -326,68 +328,67 @@
 
 def last_d_kernel(before, *refs):
     refs = Refs(refs)
-    now_ref, prev_ref, ha_ref, hb_ref, speed_ref, perturb_ref, lap_u_ref, cells_hbm, cells_ref = refs.take(9)
-    u_ref, u_prev, source_ref, wavelet_hbm = refs.take(4)
+    now_ref, prev_ref, ha_ref, hb_ref, speed_ref, perturb_ref, lap_u_ref, cells_ref, rows_hbm = refs.take(9)
     early_ref = refs.take() if before else None
-    out_ref, next_ref, record_ref, u_out = refs.take(4)
-    u_next = refs.take()
+    out_ref, next_ref, record_ref = refs.take(3)
     work = refs.take(3)
-    cells_smem, wavelet_ref, rows_ref, sems, table_sems = refs.take(5)
-    fetches = [
-        pltpu.make_async_copy(cells_hbm, cells_smem, table_sems.at[0]),
-        pltpu.make_async_copy(wavelet_hbm, wavelet_ref, table_sems.at[1]),
-    ]
-    for fetch in fetches:
-        fetch.start()
+    rows_smem, rows_ref, sems, table_sem = refs.take(4)
+    fetch = pltpu.make_async_copy(rows_hbm, rows_smem, table_sem)
+    fetch.start()
     _, side, _ = now_ref.shape
     prepare(work, now_ref, ha_ref, hb_ref, 0, band_weights(side))
-    for fetch in fetches:
-        fetch.wait()
+
+    def emit(z, block, centre, lap):
+        next_ref[z, block, :] = ((2.0 * centre - prev_ref[z, block, :]) + speed_ref[z, block, :] * lap) + (
+            perturb_ref[z, block, :] * lap_u_ref[z, block, :]
+        )
+
+    def finish(part, parts):
+        store_out(next_ref, out_ref, sems, part, parts).start()
+
+    each_laplacian(work, now_ref, emit, finish, PARTS)
+    fetch.wait()
+    if before:
+        record_ref[pl.ds(0, before), :] = early_ref[...]
+    fields = [now_ref, next_ref] if record_ref.shape[0] > before + 1 else [next_ref]
+    gather_records(before, lambda r: rows_smem[0, r], cells_ref, fields, record_ref, rows_ref)
+    for part in range(PARTS):
+        store_out(next_ref, out_ref, sems, part, PARTS).wait()
+
+
+def last_w_kernel(*refs):
+    refs = Refs(refs)
+    now_ref, prev_ref, ha_ref, hb_ref, speed_ref, count_ref, d_next = refs.take(7)
+    u_ref, u_prev, lap_u_ref, source_ref, wavelet_hbm = refs.take(5)
+    out_ref, u_out = refs.take(2)
+    next_ref, u_next = refs.take(2)
+    work = refs.take(3)
+    wavelet_ref, sems, table_sem = refs.take(3)
+    fetch = pltpu.make_async_copy(wavelet_hbm, wavelet_ref, table_sem)
+    fetch.start()
+    _, side, _ = now_ref.shape
+    prepare(work, now_ref, ha_ref, hb_ref, 0, band_weights(side))
     last_step = wavelet_ref.shape[1] - 1
 
     def emit(z, block, centre, lap):
-        speed, lap_u = speed_ref[z, block, :], lap_u_ref[z, block, :]
+        speed = speed_ref[z, block, :]
         next_ref[z, block, :] = ((2.0 * centre - prev_ref[z, block, :]) + speed * lap) + (
-            perturb_ref[z, block, :] * lap_u
+            count_ref[z, block, :] * d_next[z, block, :]
         )
-        u_next[z, block, :] = (2.0 * u_ref[z, block, :] - u_prev[z, block, :]) + speed * lap_u
+        u_next[z, block, :] = (2.0 * u_ref[z, block, :] - u_prev[z, block, :]) + speed * lap_u_ref[z, block, :]
 
     def finish(part, parts):
         size = side // parts
+        if part == 0:
+            fetch.wait()
         add_source(u_next, source_ref, wavelet_ref, last_step, part * size, size)
         store_out(next_ref, out_ref, sems.at[0], part, parts).start()
         store_out(u_next, u_out, sems.at[1], part, parts).start()
 
     each_laplacian(work, now_ref, emit, finish, PARTS)
-    if before:
-        record_ref[pl.ds(0, before), :] = early_ref[...]
-    fields = [now_ref, next_ref] if record_ref.shape[0] > before + 1 else [next_ref]
-    gather_records(before, cells_smem, cells_ref, fields, record_ref, rows_ref)
     for part in range(PARTS):
         store_out(next_ref, out_ref, sems.at[0], part, PARTS).wait()
         store_out(u_next, u_out, sems.at[1], part, PARTS).wait()
-
-
-def last_w_kernel(*refs):
-    refs = Refs(refs)
-    now_ref, prev_ref, ha_ref, hb_ref, speed_ref, count_ref, d_next = refs.take(7)
-    out_ref, next_ref = refs.take(2)
-    work = refs.take(3)
-    sems = refs.take()
-    _, side, _ = now_ref.shape
-    prepare(work, now_ref, ha_ref, hb_ref, 0, band_weights(side))
-
-    def emit(z, block, centre, lap):
-        next_ref[z, block, :] = ((2.0 * centre - prev_ref[z, block, :]) + speed_ref[z, block, :] * lap) + (
-            count_ref[z, block, :] * d_next[z, block, :]
-        )
-
-    def finish(part, parts):
-        store_out(next_ref, out_ref, sems, part, parts).start()
-
-    each_laplacian(work, now_ref, emit, finish, PARTS)
-    for part in range(PARTS):
-        store_out(next_ref, out_ref, sems, part, PARTS).wait()
 
 
 def stencil_call(body, in_specs, args, outs, kinds, scratch):
@@ -458,31 +459,35 @@
     return stencil_call(body, [VMEM] * len(args), args, outs, [VMEM] * 6, [halo_space(d.shape[1])] * 2)
 
 
-def last_d_call(step, d, d_prev, halo, speed, perturb, lap_u, cells, u, u_prev, source, wavelet, early):
+def last_d_call(step, d, d_prev, halo, speed, perturb, lap_u, cells, rows, early):
     before = 0 if early is None else early.shape[0]
     n = cells.shape[1]
     fields = step + 1 - before
-    args = [d, d_prev, *halo, speed, perturb, lap_u, in_hbm(cells), cells, u, u_prev, source, in_hbm(wavelet)]
-    specs = [VMEM] * len(args)
-    specs[7], specs[11], specs[12] = HBM, SMEM, HBM
+    args = [d, d_prev, *halo, speed, perturb, lap_u, cells, rows]
+    specs = [VMEM] * 8 + [HBM]
     if before:
         args, specs = args + [early], specs + [VMEM]
-    scratch = [pltpu.VMEM(u.shape, F32)] + work_space(*d.shape[:2]) + [
+    scratch = work_space(*d.shape[:2]) + [
         pltpu.SMEM(cells.shape, jnp.int32),
+        pltpu.VMEM((fields, n, d.shape[-1]), F32),
+        pltpu.SemaphoreType.DMA((PARTS,)),
+        pltpu.SemaphoreType.DMA(()),
+    ]
+    outs = [sds((1,) + d.shape), sds(d.shape), sds((step + 1, n))]
+    body = functools.partial(last_d_kernel, before)
+    return stencil_call(body, specs, args, outs, [HBM, VMEM, VMEM], scratch)
+
+
+def last_w_call(w, w_prev, halo, speed, count, d_next, u, u_prev, lap_u, source, wavelet):
+    args = [w, w_prev, *halo, speed, count, d_next, u, u_prev, lap_u, source, in_hbm(wavelet)]
+    specs = [VMEM] * 10 + [SMEM, HBM]
+    scratch = [pltpu.VMEM(w.shape, F32)] * 2 + work_space(*w.shape[:2]) + [
         pltpu.SMEM(wavelet.shape, F32),
-        pltpu.VMEM((fields, n, d.shape[-1]), F32),
         pltpu.SemaphoreType.DMA((2, PARTS)),
-        pltpu.SemaphoreType.DMA((2,)),
+        pltpu.SemaphoreType.DMA(()),
     ]
-    outs = [sds((1,) + d.shape), sds(d.shape), sds((step + 1, n)), sds((1,) + u.shape)]
-    body = functools.partial(last_d_kernel, before)
-    return stencil_call(body, specs, args, outs, [HBM, VMEM, VMEM, HBM], scratch)
-
-
-def last_w_call(w, w_prev, halo, speed, count, d_next):
-    args = [w, w_prev, *halo, speed, count, d_next]
-    scratch = [pltpu.VMEM(w.shape, F32)] + work_space(*w.shape[:2]) + [pltpu.SemaphoreType.DMA((PARTS,))]
-    return stencil_call(last_w_kernel, [VMEM] * len(args), args, [sds((1,) + w.shape)], [HBM], scratch)
+    outs = [sds((1,) + w.shape)] * 2
+    return stencil_call(last_w_kernel, specs, args, outs, [HBM] * 2, scratch)
 
 
 def count_kernel(cells_ref, count_ref, outer_ref):
@@ -515,12 +520,11 @@
     )(cells)
 
 
-def gather_records(before, cells_smem, cells_ref, fields, out_ref, rows_ref):
+def gather_records(before, row_of, cells_ref, fields, out_ref, rows_ref):
     depth, side, _ = fields[0].shape
     n = cells_ref.shape[1]
     total = depth * side * side
-    start = lax.axis_index("slab") * total
-    local = cells_ref[...] - start
+    local = cells_ref[...] - lax.axis_index("slab") * total
     mine = (local >= 0) & (local < total)
     lane_of = jnp.where(mine, remainder(jnp.maximum(local, 0), side), -1)
     lanes = lax.broadcasted_iota(jnp.int32, (side, n), 0)
@@ -528,8 +532,7 @@
     flat = [field_ref.reshape(depth * side, side) for field_ref in fields]
 
     def gather(r, carry):
-        cell = jnp.clip(cells_smem[0, r] - start, 0, total - 1)
-        row = quotient(cell, side)
+        row = row_of(r)
         for step, field_ref in enumerate(flat):
             rows_ref[step, pl.ds(r, 1), :] = field_ref[pl.ds(row, 1), :]
         return carry
@@ -543,10 +546,19 @@
 def record_kernel(before, cells_smem, cells_ref, *rest):
     if before:
         early_ref, rest = rest[0], rest[1:]
-    *fields, out_ref, rows_ref = rest
+    *fields, out_ref, table_ref, rows_ref = rest
     if before:
         out_ref[pl.ds(0, before), :] = early_ref[...]
-    gather_records(before, cells_smem, cells_ref, fields, out_ref, rows_ref)
+    depth, side, _ = fields[0].shape
+    total = depth * side * side
+    start = lax.axis_index("slab") * total
+
+    def row_of(r):
+        row = quotient(jnp.clip(cells_smem[0, r] - start, 0, total - 1), side)
+        table_ref[0, r] = row
+        return row
+
+    gather_records(before, row_of, cells_ref, fields, out_ref, rows_ref)
 
 
 def record_call(cells, early, fields):
@@ -556,9 +568,9 @@
     args = [cells, cells] + ([early] if before else []) + list(fields)
     return pl.pallas_call(
         functools.partial(record_kernel, before),
-        out_shape=sds((before + len(fields), n)),
+        out_shape=[sds((before + len(fields), n)), sds(cells.shape, jnp.int32)],
         in_specs=[SMEM] + [VMEM] * (len(args) - 1),
-        out_specs=VMEM,
+        out_specs=[VMEM, SMEM],
         scratch_shapes=[pltpu.VMEM((len(fields), n, side), F32)],
         compiler_params=params(8),
     )(*args)
@@ -666,16 +678,24 @@
     lax.fori_loop(0, aperture_ref.shape[1], tile, 0)
 
 
-def perturb_kernel(lat_dev, tile_side, aperture_ref, slot_ref, *rest):
-    *blocks, out_ref, tiles_ref, seen_ref, place_ref = rest
+def perturb_kernel(lat_dev, tile_side, aperture_hbm, slot_hbm, *rest):
+    *blocks, out_ref, tiles_ref, seen_ref, place_ref, aperture_ref, slot_ref, sems = rest
+    copies = [
+        pltpu.make_async_copy(aperture_hbm, aperture_ref, sems.at[0]),
+        pltpu.make_async_copy(slot_hbm, slot_ref, sems.at[1]),
+    ]
+    for copy in copies:
+        copy.start()
     n_shot = len(blocks)
     capacity, depth, cells = blocks[0].shape
     side = out_ref.shape[1]
     across = side // tile_side
     flat_ref = out_ref.reshape(depth * side, side)
-    places(aperture_ref, slot_ref, lat_dev, n_shot, capacity, seen_ref, place_ref)
     for k in range(n_shot):
         tiles_ref[pl.ds(k * capacity, capacity)] = blocks[k][...]
+    for copy in copies:
+        copy.wait()
+    places(aperture_ref, slot_ref, lat_dev, n_shot, capacity, seen_ref, place_ref)
 
     def tile_row(i, carry):
         for high in range(cells // side):
@@ -722,12 +742,17 @@
     return pl.pallas_call(
         functools.partial(perturb_kernel, lat_dev, tile_side),
         out_shape=sds((depth, side, side)),
-        in_specs=[SMEM, SMEM] + [VMEM] * len(blocks),
+        in_specs=[HBM, HBM] + [VMEM] * len(blocks),
         out_specs=VMEM,
-        scratch_shapes=tile_scratch(len(blocks), capacity, depth, cells, aperture.shape[1]),
+        scratch_shapes=[
+            *tile_scratch(len(blocks), capacity, depth, cells, aperture.shape[1]),
+            pltpu.SMEM(aperture.shape, jnp.int32),
+            pltpu.SMEM(tile_slot.shape, jnp.int32),
+            pltpu.SemaphoreType.DMA((2,)),
+        ],
         compiler_params=params(8),
         name="perturb",
-    )(aperture, tile_slot, *blocks)
+    )(in_hbm(aperture), in_hbm(tile_slot), *blocks)
 
 
 def finish_kernel(n_shot, table_hbm, *refs):
@@ -841,7 +866,7 @@
 def slab_parts(part):
     count = lax.axis_size("slab")
     parts = [part]
-    for k in range(1, count):
+    for k in range(count - 1, 0, -1):
         to = [s ^ k for s in range(count)] if count & (count - 1) == 0 else [(s + k) % count for s in range(count)]
         parts.append(lax.ppermute(part, "slab", list(enumerate(to))))
     return parts
@@ -887,7 +912,7 @@
     d_halo = swap(edges)
     traces = u_local = None
     for step in range(1, steps - 1):
-        traces = record_call(receiver_cells, traces, [d_next])
+        traces, receiver_rows = record_call(receiver_cells, traces, [d_next])
         u, up, d, dp, w, wp = u_next, u, d_next, d, w_next, w
         u_next, lap, corr, *edges = u_call(
             step, False, wavelet, source_cell, u, up, u_halo, speed, w, corr, u_local, *tiling
@@ -903,11 +928,11 @@
     step = steps - 1
     lap, *returning = u_call(step, True, wavelet, source_cell, u, up, u_halo, speed, w, corr, u_local, *tiling)
     arrived = exchange(returning)
-    d_final, d_next, traces, u_final = last_d_call(
-        step, d, dp, d_halo, speed, perturb, lap, receiver_cells, u, up, source_cell, wavelet, traces
+    d_final, d_next, traces = last_d_call(
+        step, d, dp, d_halo, speed, perturb, lap, receiver_cells, receiver_rows, traces
     )
     parts = slab_parts(traces)
-    (w_final,) = last_w_call(w, wp, w_halo, speed, count, d_next)
+    w_final, u_final = last_w_call(w, wp, w_halo, speed, count, d_next, u, up, lap, source_cell, wavelet)
     sensitivity, traces = finish_call(table, arrived, parts, lat_dev)
     return (sensitivity, u_final, d_final, w_final, jnp.transpose(traces, (1, 0, 2)))
 

time: 91.1 us -> 89.4 us (0.981)
  Pallas kernels: 25.4 us -> 24.2 us
    pallas_call x8, Pallas kernels: 15.3 us -> 13.3 us  [stencil_call(): pl.pallas_call(body, out_shape=outs, in_specs=in_specs, out_specs=kinds,...]
    ppermute x3, waiting for transfers between devices: 2.11 us -> 0.49 us  [slab_parts(): parts.append(lax.ppermute(part, 'slab', list(enumerate(to))))]
    ppermute x14, waiting for transfers between devices: 12.6 us -> 13.6 us  [exchange(): got[k] = lax.ppermute(block, 'shot', moves) if moves else block]
where the time goes in v3:
time: 89.4 us; the launch traced here: 89.1 us
  starting transfers between devices  37.5 us (42%)
  waiting for transfers between devices  25.7 us (29%)
  Pallas kernels  24.2 us (27%)
  between operations  1.58 us (2%)
    ppermute x16, starting transfers between devices, swap(): got.append(lax.ppermute(edge, ('shot', 'slab'), sorted(pairs.items())))  18.4 us
    ppermute x14, starting transfers between devices, exchange(): got[k] = lax.ppermute(block, 'shot', moves) if moves else block  14.7 us
    ppermute x14, waiting for transfers between devices, exchange(): got[k] = lax.ppermute(block, 'shot', moves) if moves else block  13.6 us
    pallas_call x8, Pallas kernels, stencil_call(): pl.pallas_call(body, out_shape=outs, in_specs=in_specs, out_specs=kinds,...  13.3 us
    ppermute x16, waiting for transfers between devices, swap(): got.append(lax.ppermute(edge, ('shot', 'slab'), sorted(pairs.items())))  11.6 us
    ppermute x3, starting transfers between devices, slab_parts(): parts.append(lax.ppermute(part, 'slab', list(enumerate(to))))  4.39 us
    pallas_call x2, Pallas kernels, first_edges(): pl.pallas_call(functools.partial(edges_kernel, n), out_shape=[edge, edge]...  2.27 us
    pallas_call x1, Pallas kernels, perturb_call(): pl.pallas_call(functools.partial(perturb_kernel, lat_dev, tile_side), out...  1.95 us
  transfers between devices with their start and end apart: 33, of which 14 were waited for; matrix products, arithmetic and copies ran while one was open for 0% of the time, Pallas kernels for 21%

profile of v3, /device:TPU:0, one launch (start us, length us, event | category | flops | bytes accessed | tf_op | source)
XLA Modules:
  0.0 89.1 jit_solution(16268245710525413141)
XLA Ops:
  0.6 1.9 %pack.1 = (f32[4,8,1024]{2,1,0:T(8,128)S(1)}, f32[4,8,1024]{2,1,0:T(8,128)S(1)}, f32[4,8,1024]{2,1,0:T(8,128)S(1)}, f32[4,8,1024]{2,1,0:T(8,128)S(1)}, f32[4,8,1...) custom-call(s32[8,16]{1,0:T(8,128)} %refs_7_.2, ...), custom_call_target="tpu_custom_call" | custom-call | tf_op jit(solution)/shard_map/pack/pallas_call | solution.py:649
  3.1 2.6 %collective-permute-start.7 = (f32[4,8,1024]{2,1,0:T(8,128)S(1)}, f32[4,8,1024]{2,1,0:T(8,128)S(1)}, u32[]{:S(2)}, u32[]{:S(2)}) collective-permute-start(f32[4,8,1024]{2,1,0:T(8,128)S(1)} %get-tuple-element.77), channel_id=1, source_target_pairs={{0,8},{4,12},{8,0},{12,4},{16,24},{20,28},{24,16},{28,20},{1,9},{5... | collective-permute-start | bytes 393224 | tf_op jit(solution)/shard_map/ppermute | solution.py:862
  11.7 1.9 %collective-permute-done.8.rest_3_ = f32[4,8,1024]{2,1,0:T(8,128)S(1)} collective-permute-done((f32[4,8,1024]{2,1,0:T(8,128)S(1)}, f32[4,8,1024]{2,1,0:T(8,128)S(1)}, u32[]{:S(2)}, u32[]{:S(2)}) %collective-permute-start.8) | collective-permute-done | bytes 131104 | tf_op jit(solution)/shard_map/ppermute | solution.py:862
  15.4 3.5 %collective-permute-start = (f32[1,4,128,128]{3,2,1,0:T(8,128)S(1)}, f32[1,4,128,128]{3,2,1,0:T(8,128)S(1)}, u32[]{:S(2)}, u32[]{:S(2)}) collective-permute-start(f32[1,4,128,128]{3,2,1,0:T(8,128)S(1)} %get-tuple-element.68), channel_id=1, source_target_pairs={{0,1},{1,0},{2,3},{3,2},{4,5},{5,4},{6,7},{7,6},{8,9},{9,8},{10,11... | collective-permute-start | bytes 786440 | tf_op jit(solution)/shard_map/ppermute | solution.py:810
  18.9 1.8 %collective-permute-done.11.rest_6_ = f32[4,8,1024]{2,1,0:T(8,128)S(1)} collective-permute-done((f32[4,8,1024]{2,1,0:T(8,128)S(1)}, f32[4,8,1024]{2,1,0:T(8,128)S(1)}, u32[]{:S(2)}, u32[]{:S(2)}) %collective-permute-start.11) | collective-permute-done | bytes 131104 | tf_op jit(solution)/shard_map/ppermute | solution.py:862
  20.7 1.7 %collective-permute-start.12 = (f32[4,8,1024]{2,1,0:T(8,128)S(1)}, f32[4,8,1024]{2,1,0:T(8,128)S(1)}, u32[]{:S(2)}, u32[]{:S(2)}) collective-permute-start(f32[4,8,1024]{2,1,0:T(8,128)S(1)} %get-tuple-element.82), channel_id=1, source_target_pairs={{0,28},{4,24},{8,20},{12,16},{16,12},{20,8},{24,4},{28,0},{1,29},{... | collective-permute-start | bytes 393224 | tf_op jit(solution)/shard_map/ppermute | solution.py:862
  23.5 3.7 %collective-permute-done.12.rest_7_ = f32[4,8,1024]{2,1,0:T(8,128)S(1)} collective-permute-done((f32[4,8,1024]{2,1,0:T(8,128)S(1)}, f32[4,8,1024]{2,1,0:T(8,128)S(1)}, u32[]{:S(2)}, u32[]{:S(2)}) %collective-permute-start.12) | collective-permute-done | bytes 131104 | tf_op jit(solution)/shard_map/ppermute | solution.py:862
  27.3 2.0 %perturb.1.perturb_ref.refs_5_ = f32[8,128,128]{2,1,0:T(8,128)S(1)} custom-call(s32[8,16]{1,0:T(8,128)} %refs_7_.2, s32[64]{0:T(128)} %refs_8_.1, f32[4,8,1024]{2,1,0:T(8,128)S(1)} %get-tuple-element.75.rest_0_, f32[4,8,1024]{2,1,0:T(8,128)S(1)} %collective-permute-done.6.rest_1_, f32[4,8,1024]{2,1,0:T(8,128)S(1)} %collective-permute-done.7.rest_2_, ...), custom_call_target="tpu_custom_call" | custom-call | tf_op jit(solution)/shard_map/perturb/pallas_call | solution.py:742
  29.3 1.9 %shard_map.165 = (f32[8,128,128]{2,1,0:T(8,128)S(1)}, f32[8,128,128]{2,1,0:T(8,128)S(1)}, f32[8,128,128]{2,1,0:T(8,128)S(1)}, f32[1,4,128,128]{3,2,1,0:T(8,128)S(1)}, f32[1,4,128,128]{3,2,1,0:T(8,128)S(1)}) custom-call(f32[8,128,128]{2,1,0:T(8,128)S(1)} %bitcast.17, f32[1,4,128,128]{3,2,1,0:T(8,128)S(1)} %collective-permute-done.refs_1_, ...), custom_call_target="tpu_custom_call" | custom-call | tf_op jit(solution)/shard_map/pallas_call | solution.py:395
  31.2 2.8 %collective-permute-start.2 = (f32[1,4,128,128]{3,2,1,0:T(8,128)S(1)}, f32[1,4,128,128]{3,2,1,0:T(8,128)S(1)}, u32[]{:S(2)}, u32[]{:S(2)}) collective-permute-start(f32[1,4,128,128]{3,2,1,0:T(8,128)S(1)} %get-tuple-element.71), channel_id=1, source_target_pairs={{0,1},{1,0},{2,3},{3,2},{4,5},{5,4},{6,7},{7,6},{8,9},{9,8},{10,11... | collective-permute-start | bytes 786440 | tf_op jit(solution)/shard_map/ppermute | solution.py:810
  37.7 2.0 %collective-permute-start.17 = (f32[1,4,128,128]{3,2,1,0:T(8,128)S(1)}, f32[1,4,128,128]{3,2,1,0:T(8,128)S(1)}, u32[]{:S(2)}, u32[]{:S(2)}) collective-permute-start(f32[1,4,128,128]{3,2,1,0:T(8,128)S(1)} %get-tuple-element.95), channel_id=1, source_target_pairs={{0,1},{1,0},{2,3},{3,2},{4,5},{5,4},{6,7},{7,6},{8,9},{9,8},{10,11... | collective-permute-start | bytes 786440 | tf_op jit(solution)/shard_map/ppermute | solution.py:810
  42.5 3.1 %collective-permute-start.13 = (f32[1,4,128,128]{3,2,1,0:T(8,128)S(1)}, f32[1,4,128,128]{3,2,1,0:T(8,128)S(1)}, u32[]{:S(2)}, u32[]{:S(2)}) collective-permute-start(f32[1,4,128,128]{3,2,1,0:T(8,128)S(1)} %get-tuple-element.89), channel_id=1, source_target_pairs={{0,1},{1,0},{2,3},{3,2},{4,5},{5,4},{6,7},{7,6},{8,9},{9,8},{10,11... | collective-permute-start | bytes 786440 | tf_op jit(solution)/shard_map/ppermute | solution.py:810
  47.6 4.8 %collective-permute-done.17.refs_10_ = f32[1,4,128,128]{3,2,1,0:T(8,128)S(1)} collective-permute-done((f32[1,4,128,128]{3,2,1,0:T(8,128)S(1)}, f32[1,4,128,128]{3,2,1,0:T(8,128)S(1)}, u32[]{:S(2)}, u32[]{:S(2)}) %collective-permute-start.17) | collective-permute-done | bytes 262176 | tf_op jit(solution)/shard_map/ppermute | solution.py:810
  52.4 1.7 %shard_map.171 = (f32[8,128,128]{2,1,0:T(8,128)S(1)}, f32[8,128,128]{2,1,0:T(8,128)S(1)}, f32[1,4,128,128]{3,2,1,0:T(8,128)S(1)}, f32[1,4,128,128]{3,2,1,0:T(8,1...) custom-call(f32[8,128,128]{2,1,0:T(8,128)S(1)} %bitcast.12, ...), custom_call_target="tpu_custom_call" | custom-call | tf_op jit(solution)/shard_map/pallas_call | solution.py:395
  54.1 3.3 %collective-permute-done.13.refs_1_ = f32[1,4,128,128]{3,2,1,0:T(8,128)S(1)} collective-permute-done((f32[1,4,128,128]{3,2,1,0:T(8,128)S(1)}, f32[1,4,128,128]{3,2,1,0:T(8,128)S(1)}, u32[]{:S(2)}, u32[]{:S(2)}) %collective-permute-start.13) | collective-permute-done | bytes 262176 | tf_op jit(solution)/shard_map/ppermute | solution.py:810
  57.5 1.9 %shard_map.172 = (f32[8,128,128]{2,1,0:T(8,128)S(1)}, f32[4,8,1024]{2,1,0:T(8,128)S(1)}, f32[4,8,1024]{2,1,0:T(8,128)S(1)}, f32[4,8,1024]{2,1,0:T(8,128)S(1)}, f...) custom-call(f32[8,128,128]{2,1,0:T(8,128)S(1)} %get-tuple-element.88, ...), custom_call_target="tpu_custom_call" | custom-call | tf_op jit(solution)/shard_map/pallas_call | solution.py:395
  61.3 1.8 %collective-permute-start.26 = (f32[1,4,128,128]{3,2,1,0:T(8,128)S(1)}, f32[1,4,128,128]{3,2,1,0:T(8,128)S(1)}, u32[]{:S(2)}, u32[]{:S(2)}) collective-permute-start(f32[1,4,128,128]{3,2,1,0:T(8,128)S(1)} %get-tuple-element.115), channel_id=1, source_target_pairs={{0,1},{1,0},{2,3},{3,2},{4,5},{5,4},{6,7},{7,6},{8,9},{9,8},{10,11... | collective-permute-start | bytes 786440 | tf_op jit(solution)/shard_map/ppermute | solution.py:810
  65.9 1.8 %collective-permute-start.31 = (f32[1,4,128,128]{3,2,1,0:T(8,128)S(1)}, f32[1,4,128,128]{3,2,1,0:T(8,128)S(1)}, u32[]{:S(2)}, u32[]{:S(2)}) collective-permute-start(f32[1,4,128,128]{3,2,1,0:T(8,128)S(1)} %get-tuple-element.122), channel_id=1, source_target_pairs={{0,1},{1,0},{2,3},{3,2},{4,5},{5,4},{6,7},{7,6},{8,9},{9,8},{10,11... | collective-permute-start | bytes 786440 | tf_op jit(solution)/shard_map/ppermute | solution.py:810
  70.5 2.4 %collective-permute-start.24 = (f32[4,8,1024]{2,1,0:T(8,128)S(1)}, f32[4,8,1024]{2,1,0:T(8,128)S(1)}, u32[]{:S(2)}, u32[]{:S(2)}) collective-permute-start(f32[4,8,1024]{2,1,0:T(8,128)S(1)} %get-tuple-element.112), channel_id=1, source_target_pairs={{0,24},{4,28},{8,16},{12,20},{16,8},{20,12},{24,0},{28,4},{1,25},{... | collective-permute-start | bytes 393224 | tf_op jit(solution)/shard_map/ppermute | solution.py:862
  72.8 1.9 %shard_map.173 = (f32[1,256]{1,0:T(1,128)S(1)}, s32[1,256]{1,0:T(1,128)S(1)}) custom-call(s32[1,256]{1,0:T(1,128)S(1)} %copy-done.7, s32[1,256]{1,0:T(1,128)S(1)} %copy-done.7, f32[8,128,128]{2,1,0:T(8,128)S(1)} %get-tuple-element.91.refs_1_.rest_0_), custom_call_target="tpu_custom_call" | custom-call | tf_op jit(solution)/shard_map/pallas_call | solution.py:569
  74.8 1.9 %shard_map.174 = (f32[1,8,128,128]{3,2,1,0:T(8,128)}, f32[8,128,128]{2,1,0:T(8,128)S(1)}, f32[3,256]{1,0:T(4,128)S(1)}) custom-call(f32[8,128,128]{2,1,0:T(8,128)S(1)} %get-tuple-element.114.refs_0_, f32[8,128,128]{2,1,0:T(8,128)S(1)} %get-tuple-element.91.refs_1_.rest_0_, f32[1,4,128,128]{3,2,1,0:T(8,128)S(1)} %collective-permute-done.26.refs_2_, ...), custom_call_target="tpu_custom_call" | custom-call | tf_op jit(solution)/shard_map/pallas_call | solution.py:395
  76.7 3.7 %collective-permute-done.23.refs_5_ = f32[4,8,1024]{2,1,0:T(8,128)S(1)} collective-permute-done((f32[4,8,1024]{2,1,0:T(8,128)S(1)}, f32[4,8,1024]{2,1,0:T(8,128)S(1)}, u32[]{:S(2)}, u32[]{:S(2)}) %collective-permute-start.23) | collective-permute-done | bytes 131104 | tf_op jit(solution)/shard_map/ppermute | solution.py:862
  80.4 2.5 %collective-permute-start.28 = (f32[3,256]{1,0:T(4,128)S(1)}, f32[3,256]{1,0:T(4,128)S(1)}, u32[]{:S(2)}, u32[]{:S(2)}) collective-permute-start(f32[3,256]{1,0:T(4,128)S(1)} %get-tuple-element.120.refs_8_), channel_id=1, source_target_pairs={{0,3},{1,2},{2,1},{3,0},{4,7},{5,6},{6,5},{7,4},{8,11},{9,10},{10,... | collective-permute-start | bytes 9224 | tf_op jit(solution)/shard_map/ppermute | solution.py:871
  84.8 2.2 %shard_map.175 = (f32[1,8,128,128]{3,2,1,0:T(8,128)}, f32[1,8,128,128]{3,2,1,0:T(8,128)}) custom-call(f32[8,128,128]{2,1,0:T(8,128)S(1)} %get-tuple-element.102.refs_3_.refs_0_, f32[8,128,128]{2,1,0:T(8,128)S(1)} %get-tuple-element.86.refs_3_.refs_2_.refs_1_, f32[1,4,128,128]{3,2,1,0:T(8,128)S(1)} %collective-permute-done.31.refs_2_, ...), custom_call_target="tpu_custom_call" | custom-call | tf_op jit(solution)/shard_map/pallas_call | solution.py:395
  (74 shorter events, 28.9 us)
Async XLA Ops:
  3.1 7.6 %collective-permute-start.7 = (f32[4,8,1024]{2,1,0:T(8,128)S(1)}, f32[4,8,1024]{2,1,0:T(8,128)S(1)}, u32[]{:S(2)}, u32[]{:S(2)}) collective-permute-start(f32[4,8,1024]{2,1,0:T(8,128)S(1)} %get-tuple-element.77), channel_id=1, source_target_pairs={{0,8},{4,12},{8,0},{12,4},{16,24},{20,28},{24,16},{28,20},{1,9},{5... | collective-permute-start | bytes 393224 | tf_op jit(solution)/shard_map/ppermute | solution.py:862
  6.8 27.2 %collective-permute-start.4 = (f32[2,4,128,128]{3,2,1,0:T(8,128)S(1)}, f32[2,4,128,128]{3,2,1,0:T(8,128)S(1)}, u32[]{:S(2)}, u32[]{:S(2)}) collective-permute-start(f32[2,4,128,128]{3,2,1,0:T(8,128)S(1)} %get-tuple-element.73), channel_id=1, source_target_pairs={{0,1},{1,0},{2,3},{3,2},{4,5},{5,4},{6,7},{7,6},{8,9},{9,8},{10,11... | collective-permute-start | bytes 1572872 | tf_op jit(solution)/shard_map/ppermute | solution.py:810
  8.5 25.6 %collective-permute-start.5 = (f32[2,4,128,128]{3,2,1,0:T(8,128)S(1)}, f32[2,4,128,128]{3,2,1,0:T(8,128)S(1)}, u32[]{:S(2)}, u32[]{:S(2)}) collective-permute-start(f32[2,4,128,128]{3,2,1,0:T(8,128)S(1)} %get-tuple-element.74), channel_id=1, source_target_pairs={{0,4},{1,2},{2,1},{3,7},{4,0},{5,6},{6,5},{7,3},{8,12},{9,10},{10,... | collective-permute-start | bytes 1572872 | tf_op jit(solution)/shard_map/ppermute | solution.py:810
  10.7 8.2 %collective-permute-start.10 = (f32[4,8,1024]{2,1,0:T(8,128)S(1)}, f32[4,8,1024]{2,1,0:T(8,128)S(1)}, u32[]{:S(2)}, u32[]{:S(2)}) collective-permute-start(f32[4,8,1024]{2,1,0:T(8,128)S(1)} %get-tuple-element.80), channel_id=1, source_target_pairs={{0,20},{4,16},{8,28},{12,24},{16,4},{20,0},{24,12},{28,8},{1,21},{... | collective-permute-start | bytes 393224 | tf_op jit(solution)/shard_map/ppermute | solution.py:862
  13.6 7.1 %collective-permute-start.11 = (f32[4,8,1024]{2,1,0:T(8,128)S(1)}, f32[4,8,1024]{2,1,0:T(8,128)S(1)}, u32[]{:S(2)}, u32[]{:S(2)}) collective-permute-start(f32[4,8,1024]{2,1,0:T(8,128)S(1)} %get-tuple-element.81), channel_id=1, source_target_pairs={{0,24},{4,28},{8,16},{12,20},{16,8},{20,12},{24,0},{28,4},{1,25},{... | collective-permute-start | bytes 393224 | tf_op jit(solution)/shard_map/ppermute | solution.py:862
  15.4 13.8 %collective-permute-start = (f32[1,4,128,128]{3,2,1,0:T(8,128)S(1)}, f32[1,4,128,128]{3,2,1,0:T(8,128)S(1)}, u32[]{:S(2)}, u32[]{:S(2)}) collective-permute-start(f32[1,4,128,128]{3,2,1,0:T(8,128)S(1)} %get-tuple-element.68), channel_id=1, source_target_pairs={{0,1},{1,0},{2,3},{3,2},{4,5},{5,4},{6,7},{7,6},{8,9},{9,8},{10,11... | collective-permute-start | bytes 786440 | tf_op jit(solution)/shard_map/ppermute | solution.py:810
  18.9 10.4 %collective-permute-start.1 = (f32[1,4,128,128]{3,2,1,0:T(8,128)S(1)}, f32[1,4,128,128]{3,2,1,0:T(8,128)S(1)}, u32[]{:S(2)}, u32[]{:S(2)}) collective-permute-start(f32[1,4,128,128]{3,2,1,0:T(8,128)S(1)} %get-tuple-element.69), channel_id=1, source_target_pairs={{0,4},{1,2},{2,1},{3,7},{4,0},{5,6},{6,5},{7,3},{8,12},{9,10},{10,... | collective-permute-start | bytes 786440 | tf_op jit(solution)/shard_map/ppermute | solution.py:810
  31.2 10.0 %collective-permute-start.2 = (f32[1,4,128,128]{3,2,1,0:T(8,128)S(1)}, f32[1,4,128,128]{3,2,1,0:T(8,128)S(1)}, u32[]{:S(2)}, u32[]{:S(2)}) collective-permute-start(f32[1,4,128,128]{3,2,1,0:T(8,128)S(1)} %get-tuple-element.71), channel_id=1, source_target_pairs={{0,1},{1,0},{2,3},{3,2},{4,5},{5,4},{6,7},{7,6},{8,9},{9,8},{10,11... | collective-permute-start | bytes 786440 | tf_op jit(solution)/shard_map/ppermute | solution.py:810
  34.0 7.2 %collective-permute-start.3 = (f32[1,4,128,128]{3,2,1,0:T(8,128)S(1)}, f32[1,4,128,128]{3,2,1,0:T(8,128)S(1)}, u32[]{:S(2)}, u32[]{:S(2)}) collective-permute-start(f32[1,4,128,128]{3,2,1,0:T(8,128)S(1)} %get-tuple-element.72), channel_id=1, source_target_pairs={{0,4},{1,2},{2,1},{3,7},{4,0},{5,6},{6,5},{7,3},{8,12},{9,10},{10,... | collective-permute-start | bytes 786440 | tf_op jit(solution)/shard_map/ppermute | solution.py:810
  36.6 10.2 %collective-permute-start.15 = (f32[1,4,128,128]{3,2,1,0:T(8,128)S(1)}, f32[1,4,128,128]{3,2,1,0:T(8,128)S(1)}, u32[]{:S(2)}, u32[]{:S(2)}) collective-permute-start(f32[1,4,128,128]{3,2,1,0:T(8,128)S(1)} %get-tuple-element.93), channel_id=1, source_target_pairs={{0,1},{1,0},{2,3},{3,2},{4,5},{5,4},{6,7},{7,6},{8,9},{9,8},{10,11... | collective-permute-start | bytes 786440 | tf_op jit(solution)/shard_map/ppermute | solution.py:810
  37.7 9.9 %collective-permute-start.16 = (f32[1,4,128,128]{3,2,1,0:T(8,128)S(1)}, f32[1,4,128,128]{3,2,1,0:T(8,128)S(1)}, u32[]{:S(2)}, u32[]{:S(2)}) collective-permute-start(f32[1,4,128,128]{3,2,1,0:T(8,128)S(1)} %get-tuple-element.94), channel_id=1, source_target_pairs={{0,4},{1,2},{2,1},{3,7},{4,0},{5,6},{6,5},{7,3},{8,12},{9,10},{10,... | collective-permute-start | bytes 786440 | tf_op jit(solution)/shard_map/ppermute | solution.py:810
  37.7 14.7 %collective-permute-start.17 = (f32[1,4,128,128]{3,2,1,0:T(8,128)S(1)}, f32[1,4,128,128]{3,2,1,0:T(8,128)S(1)}, u32[]{:S(2)}, u32[]{:S(2)}) collective-permute-start(f32[1,4,128,128]{3,2,1,0:T(8,128)S(1)} %get-tuple-element.95), channel_id=1, source_target_pairs={{0,1},{1,0},{2,3},{3,2},{4,5},{5,4},{6,7},{7,6},{8,9},{9,8},{10,11... | collective-permute-start | bytes 786440 | tf_op jit(solution)/shard_map/ppermute | solution.py:810
  41.2 11.2 %collective-permute-start.18 = (f32[1,4,128,128]{3,2,1,0:T(8,128)S(1)}, f32[1,4,128,128]{3,2,1,0:T(8,128)S(1)}, u32[]{:S(2)}, u32[]{:S(2)}) collective-permute-start(f32[1,4,128,128]{3,2,1,0:T(8,128)S(1)} %get-tuple-element.96), channel_id=1, source_target_pairs={{0,4},{1,2},{2,1},{3,7},{4,0},{5,6},{6,5},{7,3},{8,12},{9,10},{10,... | collective-permute-start | bytes 786440 | tf_op jit(solution)/shard_map/ppermute | solution.py:810
  42.5 15.0 %collective-permute-start.13 = (f32[1,4,128,128]{3,2,1,0:T(8,128)S(1)}, f32[1,4,128,128]{3,2,1,0:T(8,128)S(1)}, u32[]{:S(2)}, u32[]{:S(2)}) collective-permute-start(f32[1,4,128,128]{3,2,1,0:T(8,128)S(1)} %get-tuple-element.89), channel_id=1, source_target_pairs={{0,1},{1,0},{2,3},{3,2},{4,5},{5,4},{6,7},{7,6},{8,9},{9,8},{10,11... | collective-permute-start | bytes 786440 | tf_op jit(solution)/shard_map/ppermute | solution.py:810
  46.8 10.7 %collective-permute-start.14 = (f32[1,4,128,128]{3,2,1,0:T(8,128)S(1)}, f32[1,4,128,128]{3,2,1,0:T(8,128)S(1)}, u32[]{:S(2)}, u32[]{:S(2)}) collective-permute-start(f32[1,4,128,128]{3,2,1,0:T(8,128)S(1)} %get-tuple-element.90), channel_id=1, source_target_pairs={{0,4},{1,2},{2,1},{3,7},{4,0},{5,6},{6,5},{7,3},{8,12},{9,10},{10,... | collective-permute-start | bytes 786440 | tf_op jit(solution)/shard_map/ppermute | solution.py:810
  60.7 7.0 %collective-permute-start.21 = (f32[4,8,1024]{2,1,0:T(8,128)S(1)}, f32[4,8,1024]{2,1,0:T(8,128)S(1)}, u32[]{:S(2)}, u32[]{:S(2)}) collective-permute-start(f32[4,8,1024]{2,1,0:T(8,128)S(1)} %get-tuple-element.109), channel_id=1, source_target_pairs={{0,12},{4,8},{8,4},{12,0},{16,28},{20,24},{24,20},{28,16},{1,13},{... | collective-permute-start | bytes 393224 | tf_op jit(solution)/shard_map/ppermute | solution.py:862
  61.3 9.2 %collective-permute-start.26 = (f32[1,4,128,128]{3,2,1,0:T(8,128)S(1)}, f32[1,4,128,128]{3,2,1,0:T(8,128)S(1)}, u32[]{:S(2)}, u32[]{:S(2)}) collective-permute-start(f32[1,4,128,128]{3,2,1,0:T(8,128)S(1)} %get-tuple-element.115), channel_id=1, source_target_pairs={{0,1},{1,0},{2,3},{3,2},{4,5},{5,4},{6,7},{7,6},{8,9},{9,8},{10,11... | collective-permute-start | bytes 786440 | tf_op jit(solution)/shard_map/ppermute | solution.py:810
  63.1 9.7 %collective-permute-start.27 = (f32[1,4,128,128]{3,2,1,0:T(8,128)S(1)}, f32[1,4,128,128]{3,2,1,0:T(8,128)S(1)}, u32[]{:S(2)}, u32[]{:S(2)}) collective-permute-start(f32[1,4,128,128]{3,2,1,0:T(8,128)S(1)} %get-tuple-element.116), channel_id=1, source_target_pairs={{0,4},{1,2},{2,1},{3,7},{4,0},{5,6},{6,5},{7,3},{8,12},{9,10},{10,... | collective-permute-start | bytes 786440 | tf_op jit(solution)/shard_map/ppermute | solution.py:810
  65.9 17.0 %collective-permute-start.31 = (f32[1,4,128,128]{3,2,1,0:T(8,128)S(1)}, f32[1,4,128,128]{3,2,1,0:T(8,128)S(1)}, u32[]{:S(2)}, u32[]{:S(2)}) collective-permute-start(f32[1,4,128,128]{3,2,1,0:T(8,128)S(1)} %get-tuple-element.122), channel_id=1, source_target_pairs={{0,1},{1,0},{2,3},{3,2},{4,5},{5,4},{6,7},{7,6},{8,9},{9,8},{10,11... | collective-permute-start | bytes 786440 | tf_op jit(solution)/shard_map/ppermute | solution.py:810
  67.7 16.2 %collective-permute-start.32 = (f32[1,4,128,128]{3,2,1,0:T(8,128)S(1)}, f32[1,4,128,128]{3,2,1,0:T(8,128)S(1)}, u32[]{:S(2)}, u32[]{:S(2)}) collective-permute-start(f32[1,4,128,128]{3,2,1,0:T(8,128)S(1)} %get-tuple-element.123), channel_id=1, source_target_pairs={{0,4},{1,2},{2,1},{3,7},{4,0},{5,6},{6,5},{7,3},{8,12},{9,10},{10,... | collective-permute-start | bytes 786440 | tf_op jit(solution)/shard_map/ppermute | solution.py:810
  69.0 11.4 %collective-permute-start.23 = (f32[4,8,1024]{2,1,0:T(8,128)S(1)}, f32[4,8,1024]{2,1,0:T(8,128)S(1)}, u32[]{:S(2)}, u32[]{:S(2)}) collective-permute-start(f32[4,8,1024]{2,1,0:T(8,128)S(1)} %get-tuple-element.111), channel_id=1, source_target_pairs={{0,20},{4,16},{8,28},{12,24},{16,4},{20,0},{24,12},{28,8},{1,21},{... | collective-permute-start | bytes 393224 | tf_op jit(solution)/shard_map/ppermute | solution.py:862
  70.5 16.5 %collective-permute-start.24 = (f32[4,8,1024]{2,1,0:T(8,128)S(1)}, f32[4,8,1024]{2,1,0:T(8,128)S(1)}, u32[]{:S(2)}, u32[]{:S(2)}) collective-permute-start(f32[4,8,1024]{2,1,0:T(8,128)S(1)} %get-tuple-element.112), channel_id=1, source_target_pairs={{0,24},{4,28},{8,16},{12,20},{16,8},{20,12},{24,0},{28,4},{1,25},{... | collective-permute-start | bytes 393224 | tf_op jit(solution)/shard_map/ppermute | solution.py:862
  72.8 14.2 %collective-permute-start.25 = (f32[4,8,1024]{2,1,0:T(8,128)S(1)}, f32[4,8,1024]{2,1,0:T(8,128)S(1)}, u32[]{:S(2)}, u32[]{:S(2)}) collective-permute-start(f32[4,8,1024]{2,1,0:T(8,128)S(1)} %get-tuple-element.113), channel_id=1, source_target_pairs={{0,28},{4,24},{8,20},{12,16},{16,12},{20,8},{24,4},{28,0},{1,29},{... | collective-permute-start | bytes 393224 | tf_op jit(solution)/shard_map/ppermute | solution.py:862
  80.4 6.6 %collective-permute-start.28 = (f32[3,256]{1,0:T(4,128)S(1)}, f32[3,256]{1,0:T(4,128)S(1)}, u32[]{:S(2)}, u32[]{:S(2)}) collective-permute-start(f32[3,256]{1,0:T(4,128)S(1)} %get-tuple-element.120.refs_8_), channel_id=1, source_target_pairs={{0,3},{1,2},{2,1},{3,0},{4,7},{5,6},{6,5},{7,4},{8,11},{9,10},{10,... | collective-permute-start | bytes 9224 | tf_op jit(solution)/shard_map/ppermute | solution.py:871
  (17 other events, 69.0 us)

commit v4 on v3

--- a/solution.py
+++ b/solution.py
@@ -148,22 +148,65 @@
 
 
 def ahead_kernel(n, *refs):
-    weights = band_weights(refs[0].shape[-1])
-    for i in range(n):
-        prepare_local(refs[n + 2 * i], refs[n + 2 * i + 1], refs[i], weights)
+    fields, outs, (rows_ref, lanes_ref) = refs[:n], refs[n:-2], refs[-2:]
+    depth, side, _ = fields[0].shape
+    weights = band_weights(side)
+    for now_ref, out_ref in zip(fields, outs):
+        prepare_local(rows_ref, lanes_ref, now_ref, weights)
+
+        def block(g, carry, now_ref=now_ref, out_ref=out_ref):
+            start = pl.multiple_of(g * SUB, SUB)
+            rows = pl.ds(start, SUB)
+            column = [now_ref[z, rows, :] for z in range(depth)]
+            for z in range(depth):
+                total = (3.0 * COEFFS[0]) * column[z] + (1.0 / SCALE) * lanes_ref[z, rows, :]
+                for k in range(1, HALO + 1):
+                    ring = (
+                        rows_ref[z, pl.ds(start + (SUB + k), SUB), :] + rows_ref[z, pl.ds(start + (SUB - k), SUB), :]
+                    )
+                    if z + k < depth:
+                        ring = ring + column[z + k]
+                    if z - k >= 0:
+                        ring = ring + column[z - k]
+                    total = total + COEFFS[k] * ring
+                out_ref[z, rows, :] = total
+            return carry
+
+        lax.fori_loop(0, side // SUB, block, 0)
 
 
 def ahead_call(fields):
     depth, side, _ = fields[0].shape
-    outs = [sds((depth, side + 2 * SUB, side)), sds((depth, side, side))] * len(fields)
-    res = pl.pallas_call(
+    outs = [sds((depth, side, side))] * len(fields)
+    rows, _, lanes = work_space(depth, side)
+    return pl.pallas_call(
         functools.partial(ahead_kernel, len(fields)),
         out_shape=outs,
         in_specs=[VMEM] * len(fields),
         out_specs=[VMEM] * len(outs),
+        scratch_shapes=[rows, lanes],
         compiler_params=params(16),
     )(*fields)
-    return [res[2 * i : 2 * i + 2] for i in range(len(fields))]
+
+
+def each_remainder(halo_ref, local_ref, now_ref, emit):
+    depth, side, _ = now_ref.shape
+
+    def block(g, carry):
+        rows = pl.ds(pl.multiple_of(g * SUB, SUB), SUB)
+        below = [halo_ref[0, z, rows, :] for z in range(HALO)]
+        above = [halo_ref[1, z, rows, :] for z in range(HALO)]
+        for z in range(depth):
+            total = local_ref[z, rows, :]
+            for k in range(1, HALO + 1):
+                if z - k < 0:
+                    total = total + COEFFS[k] * below[HALO + z - k]
+                if z + k >= depth:
+                    total = total + COEFFS[k] * above[z + k - depth]
+            emit(z, rows, now_ref[z, rows, :], total)
+        return carry
+
+    lax.fori_loop(0, side // SUB, block, 0)
 
 
 def copy_sends(next_ref, first_ref, second_ref, index):
@@ -212,7 +255,7 @@
     if not last:
         source_ref, wavelet_hbm, prev_ref, speed_ref = refs.take(4)
     corr_in = refs.take() if step else None
-    local_work = refs.take(2) if ahead else None
+    local_ref = refs.take() if ahead else None
     tables = refs.take(2) if last else []
     if last:
         lap_ref = refs.take()
@@ -223,7 +266,7 @@
         sends = refs.take(2)
     halo_ref = refs.take()
     if not ahead:
-        local_work = refs.take(2)
+        rows_ref, lanes_ref = refs.take(2)
     own_sems = refs.take()
     copies, late = [], []
     if not last:
@@ -244,9 +287,8 @@
     for copy in copies + late:
         copy.start()
     _, side, _ = now_ref.shape
-    work = (local_work[0], halo_ref, local_work[1])
     if not ahead:
-        prepare_local(*local_work, now_ref, band_weights(side))
+        prepare_local(rows_ref, lanes_ref, now_ref, band_weights(side))
     prepare_halo(halo_ref, ha_ref, hb_ref, 0)
     for copy in copies:
         copy.wait()
@@ -258,7 +300,10 @@
         if not last:
             next_ref[z, block, :] = (2.0 * centre - prev_ref[z, block, :]) + speed_ref[z, block, :] * lap
 
-    each_laplacian(work, now_ref, emit)
+    if ahead:
+        each_remainder(halo_ref, local_ref, now_ref, emit)
+    else:
+        each_laplacian((rows_ref, halo_ref, lanes_ref), now_ref, emit)
     for copy in late:
         copy.wait()
     if last:
@@ -301,14 +346,13 @@
     refs = Refs(refs)
     speed_ref, d_ref, d_prev, w_ref, w_prev, perturb_ref, lap_u_ref, count_ref = refs.take(8)
     d_halo, w_halo = refs.take(2), refs.take(2)
-    d_local, w_local = refs.take(2), refs.take(2)
+    d_local, w_local = refs.take(2)
     outer_ref = refs.take() if bare else None
     d_next, w_next = refs.take(2)
     d_sends, w_sends = refs.take(2), refs.take(2)
     d_halos, w_halos = refs.take(2)
     prepare_halo(d_halos, *d_halo, 0)
     prepare_halo(w_halos, *w_halo, 0, (outer_ref, d_halos) if bare else None)
-    d_work, w_work = (d_local[0], d_halos, d_local[1]), (w_local[0], w_halos, w_local[1])
 
     def emit_d(z, block, centre, lap):
         d_next[z, block, :] = ((2.0 * centre - d_prev[z, block, :]) + speed_ref[z, block, :] * lap) + (
@@ -320,9 +364,9 @@
             count_ref[z, block, :] * d_next[z, block, :]
         )
 
-    each_laplacian(d_work, d_ref, emit_d)
+    each_remainder(d_halos, d_local, d_ref, emit_d)
     copy_sends(d_next, *d_sends, 0)
-    each_laplacian(w_work, w_ref, emit_w)
+    each_remainder(w_halos, w_local, w_ref, emit_w)
     copy_sends(w_next, *w_sends, 0)
 
 
@@ -409,7 +453,7 @@
         args, specs = args + [corr], specs + [VMEM]
     ahead = local is not None
     if ahead:
-        args, specs = args + list(local), specs + [VMEM] * 2
+        args, specs = args + [local], specs + [VMEM]
     n_shot, n_tiles = aperture.shape
     cells = tile_side * tile_side
     capacity = n_tiles // 4
@@ -452,7 +496,7 @@
 def dw_call(d, d_prev, w, w_prev, d_halo, w_halo, d_local, w_local, speed, perturb, lap_u, count, outer):
     field, edge = sds(d.shape), sds((1, HALO) + d.shape[1:])
     bare = outer is not None
-    args = [speed, d, d_prev, w, w_prev, perturb, lap_u, count, *d_halo, *w_halo, *d_local, *w_local]
+    args = [speed, d, d_prev, w, w_prev, perturb, lap_u, count, *d_halo, *w_halo, d_local, w_local]
     args += [outer] if bare else []
     outs = [field, field] + [edge] * 4
     body = functools.partial(dw_kernel, bare)

time: 89.4 us -> 89.4 us (level)
  Pallas kernels: 24.2 us -> 26 us
  waiting for transfers between devices: 25.7 us -> 24 us
    pallas_call x1, Pallas kernels: 0.83 us -> 2.94 us  [ahead_call(): pl.pallas_call(functools.partial(ahead_kernel, len(fields)), out_shape=ou...]
    ppermute x16, waiting for transfers between devices: 11.6 us -> 9.86 us  [swap(): got.append(lax.ppermute(edge, ('shot', 'slab'), sorted(pairs.items())))]
  transfers between devices with their start and end apart: 33 -> 33, of which waited for: 14 -> 14; matrix products, arithmetic and copies ran while one was open for 0% -> 0% of each run, Pallas kernels for 21% -> 23%
where the time goes in v4:
time: 89.4 us; the launch traced here: 89.1 us
  starting transfers between devices  37.5 us (42%)
  Pallas kernels  26 us (29%)
  waiting for transfers between devices  24 us (27%)
  between operations  1.58 us (2%)
    ppermute x16, starting transfers between devices, swap(): got.append(lax.ppermute(edge, ('shot', 'slab'), sorted(pairs.items())))  18.4 us
    ppermute x14, starting transfers between devices, exchange(): got[k] = lax.ppermute(block, 'shot', moves) if moves else block  14.7 us
    ppermute x14, waiting for transfers between devices, exchange(): got[k] = lax.ppermute(block, 'shot', moves) if moves else block  13.6 us
    pallas_call x8, Pallas kernels, stencil_call(): pl.pallas_call(body, out_shape=outs, in_specs=in_specs, out_specs=kinds,...  13 us
    ppermute x16, waiting for transfers between devices, swap(): got.append(lax.ppermute(edge, ('shot', 'slab'), sorted(pairs.items())))  9.86 us
    ppermute x3, starting transfers between devices, slab_parts(): parts.append(lax.ppermute(part, 'slab', list(enumerate(to))))  4.39 us
    pallas_call x1, Pallas kernels, ahead_call(): pl.pallas_call(functools.partial(ahead_kernel, len(fields)), out_shape=ou...  2.94 us
    pallas_call x2, Pallas kernels, first_edges(): pl.pallas_call(functools.partial(edges_kernel, n), out_shape=[edge, edge]...  2.27 us
  transfers between devices with their start and end apart: 33, of which 14 were waited for; matrix products, arithmetic and copies ran while one was open for 0% of the time, Pallas kernels for 23%

profile of v4, /device:TPU:0, one launch (start us, length us, event | category | flops | bytes accessed | tf_op | source)
XLA Modules:
  0.0 89.1 jit_solution(11937223322572572419)
XLA Ops:
  0.6 1.9 %pack.1 = (f32[4,8,1024]{2,1,0:T(8,128)S(1)}, f32[4,8,1024]{2,1,0:T(8,128)S(1)}, f32[4,8,1024]{2,1,0:T(8,128)S(1)}, f32[4,8,1024]{2,1,0:T(8,128)S(1)}, f32[4,8,1...) custom-call(s32[8,16]{1,0:T(8,128)} %refs_6_.1, ...), custom_call_target="tpu_custom_call" | custom-call | tf_op jit(solution)/shard_map/pack/pallas_call | solution.py:693
  3.1 2.6 %collective-permute-start.7 = (f32[4,8,1024]{2,1,0:T(8,128)S(1)}, f32[4,8,1024]{2,1,0:T(8,128)S(1)}, u32[]{:S(2)}, u32[]{:S(2)}) collective-permute-start(f32[4,8,1024]{2,1,0:T(8,128)S(1)} %get-tuple-element.74), channel_id=1, source_target_pairs={{0,8},{4,12},{8,0},{12,4},{16,24},{20,28},{24,16},{28,20},{1,9},{5... | collective-permute-start | bytes 393224 | tf_op jit(solution)/shard_map/ppermute | solution.py:906
  11.7 1.9 %collective-permute-done.8.rest_3_ = f32[4,8,1024]{2,1,0:T(8,128)S(1)} collective-permute-done((f32[4,8,1024]{2,1,0:T(8,128)S(1)}, f32[4,8,1024]{2,1,0:T(8,128)S(1)}, u32[]{:S(2)}, u32[]{:S(2)}) %collective-permute-start.8) | collective-permute-done | bytes 131104 | tf_op jit(solution)/shard_map/ppermute | solution.py:906
  15.4 3.5 %collective-permute-start = (f32[1,4,128,128]{3,2,1,0:T(8,128)S(1)}, f32[1,4,128,128]{3,2,1,0:T(8,128)S(1)}, u32[]{:S(2)}, u32[]{:S(2)}) collective-permute-start(f32[1,4,128,128]{3,2,1,0:T(8,128)S(1)} %get-tuple-element.65), channel_id=1, source_target_pairs={{0,1},{1,0},{2,3},{3,2},{4,5},{5,4},{6,7},{7,6},{8,9},{9,8},{10,11... | collective-permute-start | bytes 786440 | tf_op jit(solution)/shard_map/ppermute | solution.py:854
  18.9 1.8 %collective-permute-done.11.rest_6_ = f32[4,8,1024]{2,1,0:T(8,128)S(1)} collective-permute-done((f32[4,8,1024]{2,1,0:T(8,128)S(1)}, f32[4,8,1024]{2,1,0:T(8,128)S(1)}, u32[]{:S(2)}, u32[]{:S(2)}) %collective-permute-start.11) | collective-permute-done | bytes 131104 | tf_op jit(solution)/shard_map/ppermute | solution.py:906
  20.7 1.7 %collective-permute-start.12 = (f32[4,8,1024]{2,1,0:T(8,128)S(1)}, f32[4,8,1024]{2,1,0:T(8,128)S(1)}, u32[]{:S(2)}, u32[]{:S(2)}) collective-permute-start(f32[4,8,1024]{2,1,0:T(8,128)S(1)} %get-tuple-element.79), channel_id=1, source_target_pairs={{0,28},{4,24},{8,20},{12,16},{16,12},{20,8},{24,4},{28,0},{1,29},{... | collective-permute-start | bytes 393224 | tf_op jit(solution)/shard_map/ppermute | solution.py:906
  23.5 3.7 %collective-permute-done.12.rest_7_ = f32[4,8,1024]{2,1,0:T(8,128)S(1)} collective-permute-done((f32[4,8,1024]{2,1,0:T(8,128)S(1)}, f32[4,8,1024]{2,1,0:T(8,128)S(1)}, u32[]{:S(2)}, u32[]{:S(2)}) %collective-permute-start.12) | collective-permute-done | bytes 131104 | tf_op jit(solution)/shard_map/ppermute | solution.py:906
  27.3 2.0 %perturb.1.perturb_ref.refs_5_ = f32[8,128,128]{2,1,0:T(8,128)S(1)} custom-call(s32[8,16]{1,0:T(8,128)} %refs_6_.1, s32[64]{0:T(128)} %refs_7_.2, f32[4,8,1024]{2,1,0:T(8,128)S(1)} %get-tuple-element.72.rest_0_, f32[4,8,1024]{2,1,0:T(8,128)S(1)} %collective-permute-done.6.rest_1_, f32[4,8,1024]{2,1,0:T(8,128)S(1)} %collective-permute-done.7.rest_2_, ...), custom_call_target="tpu_custom_call" | custom-call | tf_op jit(solution)/shard_map/perturb/pallas_call | solution.py:786
  29.3 1.9 %shard_map.165 = (f32[8,128,128]{2,1,0:T(8,128)S(1)}, f32[8,128,128]{2,1,0:T(8,128)S(1)}, f32[8,128,128]{2,1,0:T(8,128)S(1)}, f32[1,4,128,128]{3,2,1,0:T(8,128)S(1)}, f32[1,4,128,128]{3,2,1,0:T(8,128)S(1)}) custom-call(f32[8,128,128]{2,1,0:T(8,128)S(1)} %bitcast.17, f32[1,4,128,128]{3,2,1,0:T(8,128)S(1)} %collective-permute-done.refs_1_, ...), custom_call_target="tpu_custom_call" | custom-call | tf_op jit(solution)/shard_map/pallas_call | solution.py:439
  31.2 2.8 %collective-permute-start.2 = (f32[1,4,128,128]{3,2,1,0:T(8,128)S(1)}, f32[1,4,128,128]{3,2,1,0:T(8,128)S(1)}, u32[]{:S(2)}, u32[]{:S(2)}) collective-permute-start(f32[1,4,128,128]{3,2,1,0:T(8,128)S(1)} %get-tuple-element.68), channel_id=1, source_target_pairs={{0,1},{1,0},{2,3},{3,2},{4,5},{5,4},{6,7},{7,6},{8,9},{9,8},{10,11... | collective-permute-start | bytes 786440 | tf_op jit(solution)/shard_map/ppermute | solution.py:854
  37.7 2.0 %collective-permute-start.17 = (f32[1,4,128,128]{3,2,1,0:T(8,128)S(1)}, f32[1,4,128,128]{3,2,1,0:T(8,128)S(1)}, u32[]{:S(2)}, u32[]{:S(2)}) collective-permute-start(f32[1,4,128,128]{3,2,1,0:T(8,128)S(1)} %get-tuple-element.92), channel_id=1, source_target_pairs={{0,1},{1,0},{2,3},{3,2},{4,5},{5,4},{6,7},{7,6},{8,9},{9,8},{10,11... | collective-permute-start | bytes 786440 | tf_op jit(solution)/shard_map/ppermute | solution.py:854
  42.5 3.1 %collective-permute-start.13 = (f32[1,4,128,128]{3,2,1,0:T(8,128)S(1)}, f32[1,4,128,128]{3,2,1,0:T(8,128)S(1)}, u32[]{:S(2)}, u32[]{:S(2)}) collective-permute-start(f32[1,4,128,128]{3,2,1,0:T(8,128)S(1)} %get-tuple-element.86), channel_id=1, source_target_pairs={{0,1},{1,0},{2,3},{3,2},{4,5},{5,4},{6,7},{7,6},{8,9},{9,8},{10,11... | collective-permute-start | bytes 786440 | tf_op jit(solution)/shard_map/ppermute | solution.py:854
  46.8 2.9 %shard_map.170 = (f32[8,128,128]{2,1,0:T(8,128)S(1)}, f32[8,128,128]{2,1,0:T(8,128)S(1)}, f32[8,128,128]{2,1,0:T(8,128)S(1)}) custom-call(f32[8,128,128]{2,1,0:T(8,128)S(1)} %get-tuple-element.85.refs_0_.refs_7_, f32[8,128,128]{2,1,0:T(8,128)S(1)} %get-tuple-element.88.refs_1_.rest_0_, f32[8,128,128]{2,1,0:T(8,128)S(1)} %get-tuple-element.83.refs_3_.refs_2_.refs_1_), custom_call_target="tpu_custom_call" | custom-call | tf_op jit(solution)/shard_map/pallas_call | solution.py:182
  49.7 2.7 %collective-permute-done.17.refs_10_ = f32[1,4,128,128]{3,2,1,0:T(8,128)S(1)} collective-permute-done((f32[1,4,128,128]{3,2,1,0:T(8,128)S(1)}, f32[1,4,128,128]{3,2,1,0:T(8,128)S(1)}, u32[]{:S(2)}, u32[]{:S(2)}) %collective-permute-start.17) | collective-permute-done | bytes 262176 | tf_op jit(solution)/shard_map/ppermute | solution.py:854
  53.8 3.7 %collective-permute-done.13.refs_1_ = f32[1,4,128,128]{3,2,1,0:T(8,128)S(1)} collective-permute-done((f32[1,4,128,128]{3,2,1,0:T(8,128)S(1)}, f32[1,4,128,128]{3,2,1,0:T(8,128)S(1)}, u32[]{:S(2)}, u32[]{:S(2)}) %collective-permute-start.13) | collective-permute-done | bytes 262176 | tf_op jit(solution)/shard_map/ppermute | solution.py:854
  57.5 1.9 %shard_map.172 = (f32[8,128,128]{2,1,0:T(8,128)S(1)}, f32[4,8,1024]{2,1,0:T(8,128)S(1)}, f32[4,8,1024]{2,1,0:T(8,128)S(1)}, f32[4,8,1024]{2,1,0:T(8,128)S(1)}, f...) custom-call(f32[8,128,128]{2,1,0:T(8,128)S(1)} %get-tuple-element.85, ...), custom_call_target="tpu_custom_call" | custom-call | tf_op jit(solution)/shard_map/pallas_call | solution.py:439
  61.3 1.8 %collective-permute-start.26 = (f32[1,4,128,128]{3,2,1,0:T(8,128)S(1)}, f32[1,4,128,128]{3,2,1,0:T(8,128)S(1)}, u32[]{:S(2)}, u32[]{:S(2)}) collective-permute-start(f32[1,4,128,128]{3,2,1,0:T(8,128)S(1)} %get-tuple-element.109), channel_id=1, source_target_pairs={{0,1},{1,0},{2,3},{3,2},{4,5},{5,4},{6,7},{7,6},{8,9},{9,8},{10,11... | collective-permute-start | bytes 786440 | tf_op jit(solution)/shard_map/ppermute | solution.py:854
  65.9 1.8 %collective-permute-start.31 = (f32[1,4,128,128]{3,2,1,0:T(8,128)S(1)}, f32[1,4,128,128]{3,2,1,0:T(8,128)S(1)}, u32[]{:S(2)}, u32[]{:S(2)}) collective-permute-start(f32[1,4,128,128]{3,2,1,0:T(8,128)S(1)} %get-tuple-element.116), channel_id=1, source_target_pairs={{0,1},{1,0},{2,3},{3,2},{4,5},{5,4},{6,7},{7,6},{8,9},{9,8},{10,11... | collective-permute-start | bytes 786440 | tf_op jit(solution)/shard_map/ppermute | solution.py:854
  70.5 2.4 %collective-permute-start.24 = (f32[4,8,1024]{2,1,0:T(8,128)S(1)}, f32[4,8,1024]{2,1,0:T(8,128)S(1)}, u32[]{:S(2)}, u32[]{:S(2)}) collective-permute-start(f32[4,8,1024]{2,1,0:T(8,128)S(1)} %get-tuple-element.106), channel_id=1, source_target_pairs={{0,24},{4,28},{8,16},{12,20},{16,8},{20,12},{24,0},{28,4},{1,25},{... | collective-permute-start | bytes 393224 | tf_op jit(solution)/shard_map/ppermute | solution.py:906
  72.8 1.9 %shard_map.173 = (f32[1,256]{1,0:T(1,128)S(1)}, s32[1,256]{1,0:T(1,128)S(1)}) custom-call(s32[1,256]{1,0:T(1,128)S(1)} %copy-done.7, s32[1,256]{1,0:T(1,128)S(1)} %copy-done.7, f32[8,128,128]{2,1,0:T(8,128)S(1)} %get-tuple-element.88.refs_1_.rest_0_), custom_call_target="tpu_custom_call" | custom-call | tf_op jit(solution)/shard_map/pallas_call | solution.py:613
  74.8 1.9 %shard_map.174 = (f32[1,8,128,128]{3,2,1,0:T(8,128)}, f32[8,128,128]{2,1,0:T(8,128)S(1)}, f32[3,256]{1,0:T(4,128)S(1)}) custom-call(f32[8,128,128]{2,1,0:T(8,128)S(1)} %get-tuple-element.108.refs_0_, f32[8,128,128]{2,1,0:T(8,128)S(1)} %get-tuple-element.88.refs_1_.rest_0_, f32[1,4,128,128]{3,2,1,0:T(8,128)S(1)} %collective-permute-done.26.refs_2_, ...), custom_call_target="tpu_custom_call" | custom-call | tf_op jit(solution)/shard_map/pallas_call | solution.py:439
  76.7 3.7 %collective-permute-done.23.refs_5_ = f32[4,8,1024]{2,1,0:T(8,128)S(1)} collective-permute-done((f32[4,8,1024]{2,1,0:T(8,128)S(1)}, f32[4,8,1024]{2,1,0:T(8,128)S(1)}, u32[]{:S(2)}, u32[]{:S(2)}) %collective-permute-start.23) | collective-permute-done | bytes 131104 | tf_op jit(solution)/shard_map/ppermute | solution.py:906
  80.4 2.5 %collective-permute-start.28 = (f32[3,256]{1,0:T(4,128)S(1)}, f32[3,256]{1,0:T(4,128)S(1)}, u32[]{:S(2)}, u32[]{:S(2)}) collective-permute-start(f32[3,256]{1,0:T(4,128)S(1)} %get-tuple-element.114.refs_8_), channel_id=1, source_target_pairs={{0,3},{1,2},{2,1},{3,0},{4,7},{5,6},{6,5},{7,4},{8,11},{9,10},{10,... | collective-permute-start | bytes 9224 | tf_op jit(solution)/shard_map/ppermute | solution.py:915
  84.8 2.2 %shard_map.175 = (f32[1,8,128,128]{3,2,1,0:T(8,128)}, f32[1,8,128,128]{3,2,1,0:T(8,128)}) custom-call(f32[8,128,128]{2,1,0:T(8,128)S(1)} %get-tuple-element.97.refs_3_.refs_0_, f32[8,128,128]{2,1,0:T(8,128)S(1)} %get-tuple-element.83.refs_3_.refs_2_.refs_1_, f32[1,4,128,128]{3,2,1,0:T(8,128)S(1)} %collective-permute-done.31.refs_2_, ...), custom_call_target="tpu_custom_call" | custom-call | tf_op jit(solution)/shard_map/pallas_call | solution.py:439
  (74 shorter events, 29.5 us)
Async XLA Ops:
  3.1 7.6 %collective-permute-start.7 = (f32[4,8,1024]{2,1,0:T(8,128)S(1)}, f32[4,8,1024]{2,1,0:T(8,128)S(1)}, u32[]{:S(2)}, u32[]{:S(2)}) collective-permute-start(f32[4,8,1024]{2,1,0:T(8,128)S(1)} %get-tuple-element.74), channel_id=1, source_target_pairs={{0,8},{4,12},{8,0},{12,4},{16,24},{20,28},{24,16},{28,20},{1,9},{5... | collective-permute-start | bytes 393224 | tf_op jit(solution)/shard_map/ppermute | solution.py:906
  6.8 27.2 %collective-permute-start.4 = (f32[2,4,128,128]{3,2,1,0:T(8,128)S(1)}, f32[2,4,128,128]{3,2,1,0:T(8,128)S(1)}, u32[]{:S(2)}, u32[]{:S(2)}) collective-permute-start(f32[2,4,128,128]{3,2,1,0:T(8,128)S(1)} %get-tuple-element.70), channel_id=1, source_target_pairs={{0,1},{1,0},{2,3},{3,2},{4,5},{5,4},{6,7},{7,6},{8,9},{9,8},{10,11... | collective-permute-start | bytes 1572872 | tf_op jit(solution)/shard_map/ppermute | solution.py:854
  8.5 25.6 %collective-permute-start.5 = (f32[2,4,128,128]{3,2,1,0:T(8,128)S(1)}, f32[2,4,128,128]{3,2,1,0:T(8,128)S(1)}, u32[]{:S(2)}, u32[]{:S(2)}) collective-permute-start(f32[2,4,128,128]{3,2,1,0:T(8,128)S(1)} %get-tuple-element.71), channel_id=1, source_target_pairs={{0,4},{1,2},{2,1},{3,7},{4,0},{5,6},{6,5},{7,3},{8,12},{9,10},{10,... | collective-permute-start | bytes 1572872 | tf_op jit(solution)/shard_map/ppermute | solution.py:854
  10.7 8.2 %collective-permute-start.10 = (f32[4,8,1024]{2,1,0:T(8,128)S(1)}, f32[4,8,1024]{2,1,0:T(8,128)S(1)}, u32[]{:S(2)}, u32[]{:S(2)}) collective-permute-start(f32[4,8,1024]{2,1,0:T(8,128)S(1)} %get-tuple-element.77), channel_id=1, source_target_pairs={{0,20},{4,16},{8,28},{12,24},{16,4},{20,0},{24,12},{28,8},{1,21},{... | collective-permute-start | bytes 393224 | tf_op jit(solution)/shard_map/ppermute | solution.py:906
  13.6 7.1 %collective-permute-start.11 = (f32[4,8,1024]{2,1,0:T(8,128)S(1)}, f32[4,8,1024]{2,1,0:T(8,128)S(1)}, u32[]{:S(2)}, u32[]{:S(2)}) collective-permute-start(f32[4,8,1024]{2,1,0:T(8,128)S(1)} %get-tuple-element.78), channel_id=1, source_target_pairs={{0,24},{4,28},{8,16},{12,20},{16,8},{20,12},{24,0},{28,4},{1,25},{... | collective-permute-start | bytes 393224 | tf_op jit(solution)/shard_map/ppermute | solution.py:906
  15.4 13.8 %collective-permute-start = (f32[1,4,128,128]{3,2,1,0:T(8,128)S(1)}, f32[1,4,128,128]{3,2,1,0:T(8,128)S(1)}, u32[]{:S(2)}, u32[]{:S(2)}) collective-permute-start(f32[1,4,128,128]{3,2,1,0:T(8,128)S(1)} %get-tuple-element.65), channel_id=1, source_target_pairs={{0,1},{1,0},{2,3},{3,2},{4,5},{5,4},{6,7},{7,6},{8,9},{9,8},{10,11... | collective-permute-start | bytes 786440 | tf_op jit(solution)/shard_map/ppermute | solution.py:854
  18.9 10.4 %collective-permute-start.1 = (f32[1,4,128,128]{3,2,1,0:T(8,128)S(1)}, f32[1,4,128,128]{3,2,1,0:T(8,128)S(1)}, u32[]{:S(2)}, u32[]{:S(2)}) collective-permute-start(f32[1,4,128,128]{3,2,1,0:T(8,128)S(1)} %get-tuple-element.66), channel_id=1, source_target_pairs={{0,4},{1,2},{2,1},{3,7},{4,0},{5,6},{6,5},{7,3},{8,12},{9,10},{10,... | collective-permute-start | bytes 786440 | tf_op jit(solution)/shard_map/ppermute | solution.py:854
  31.2 10.0 %collective-permute-start.2 = (f32[1,4,128,128]{3,2,1,0:T(8,128)S(1)}, f32[1,4,128,128]{3,2,1,0:T(8,128)S(1)}, u32[]{:S(2)}, u32[]{:S(2)}) collective-permute-start(f32[1,4,128,128]{3,2,1,0:T(8,128)S(1)} %get-tuple-element.68), channel_id=1, source_target_pairs={{0,1},{1,0},{2,3},{3,2},{4,5},{5,4},{6,7},{7,6},{8,9},{9,8},{10,11... | collective-permute-start | bytes 786440 | tf_op jit(solution)/shard_map/ppermute | solution.py:854
  34.0 7.2 %collective-permute-start.3 = (f32[1,4,128,128]{3,2,1,0:T(8,128)S(1)}, f32[1,4,128,128]{3,2,1,0:T(8,128)S(1)}, u32[]{:S(2)}, u32[]{:S(2)}) collective-permute-start(f32[1,4,128,128]{3,2,1,0:T(8,128)S(1)} %get-tuple-element.69), channel_id=1, source_target_pairs={{0,4},{1,2},{2,1},{3,7},{4,0},{5,6},{6,5},{7,3},{8,12},{9,10},{10,... | collective-permute-start | bytes 786440 | tf_op jit(solution)/shard_map/ppermute | solution.py:854
  36.6 10.2 %collective-permute-start.15 = (f32[1,4,128,128]{3,2,1,0:T(8,128)S(1)}, f32[1,4,128,128]{3,2,1,0:T(8,128)S(1)}, u32[]{:S(2)}, u32[]{:S(2)}) collective-permute-start(f32[1,4,128,128]{3,2,1,0:T(8,128)S(1)} %get-tuple-element.90), channel_id=1, source_target_pairs={{0,1},{1,0},{2,3},{3,2},{4,5},{5,4},{6,7},{7,6},{8,9},{9,8},{10,11... | collective-permute-start | bytes 786440 | tf_op jit(solution)/shard_map/ppermute | solution.py:854
  37.7 12.0 %collective-permute-start.16 = (f32[1,4,128,128]{3,2,1,0:T(8,128)S(1)}, f32[1,4,128,128]{3,2,1,0:T(8,128)S(1)}, u32[]{:S(2)}, u32[]{:S(2)}) collective-permute-start(f32[1,4,128,128]{3,2,1,0:T(8,128)S(1)} %get-tuple-element.91), channel_id=1, source_target_pairs={{0,4},{1,2},{2,1},{3,7},{4,0},{5,6},{6,5},{7,3},{8,12},{9,10},{10,... | collective-permute-start | bytes 786440 | tf_op jit(solution)/shard_map/ppermute | solution.py:854
  37.7 14.7 %collective-permute-start.17 = (f32[1,4,128,128]{3,2,1,0:T(8,128)S(1)}, f32[1,4,128,128]{3,2,1,0:T(8,128)S(1)}, u32[]{:S(2)}, u32[]{:S(2)}) collective-permute-start(f32[1,4,128,128]{3,2,1,0:T(8,128)S(1)} %get-tuple-element.92), channel_id=1, source_target_pairs={{0,1},{1,0},{2,3},{3,2},{4,5},{5,4},{6,7},{7,6},{8,9},{9,8},{10,11... | collective-permute-start | bytes 786440 | tf_op jit(solution)/shard_map/ppermute | solution.py:854
  41.2 11.2 %collective-permute-start.18 = (f32[1,4,128,128]{3,2,1,0:T(8,128)S(1)}, f32[1,4,128,128]{3,2,1,0:T(8,128)S(1)}, u32[]{:S(2)}, u32[]{:S(2)}) collective-permute-start(f32[1,4,128,128]{3,2,1,0:T(8,128)S(1)} %get-tuple-element.93), channel_id=1, source_target_pairs={{0,4},{1,2},{2,1},{3,7},{4,0},{5,6},{6,5},{7,3},{8,12},{9,10},{10,... | collective-permute-start | bytes 786440 | tf_op jit(solution)/shard_map/ppermute | solution.py:854
  42.5 15.0 %collective-permute-start.13 = (f32[1,4,128,128]{3,2,1,0:T(8,128)S(1)}, f32[1,4,128,128]{3,2,1,0:T(8,128)S(1)}, u32[]{:S(2)}, u32[]{:S(2)}) collective-permute-start(f32[1,4,128,128]{3,2,1,0:T(8,128)S(1)} %get-tuple-element.86), channel_id=1, source_target_pairs={{0,1},{1,0},{2,3},{3,2},{4,5},{5,4},{6,7},{7,6},{8,9},{9,8},{10,11... | collective-permute-start | bytes 786440 | tf_op jit(solution)/shard_map/ppermute | solution.py:854
  46.8 10.7 %collective-permute-start.14 = (f32[1,4,128,128]{3,2,1,0:T(8,128)S(1)}, f32[1,4,128,128]{3,2,1,0:T(8,128)S(1)}, u32[]{:S(2)}, u32[]{:S(2)}) collective-permute-start(f32[1,4,128,128]{3,2,1,0:T(8,128)S(1)} %get-tuple-element.87), channel_id=1, source_target_pairs={{0,4},{1,2},{2,1},{3,7},{4,0},{5,6},{6,5},{7,3},{8,12},{9,10},{10,... | collective-permute-start | bytes 786440 | tf_op jit(solution)/shard_map/ppermute | solution.py:854
  60.7 7.0 %collective-permute-start.21 = (f32[4,8,1024]{2,1,0:T(8,128)S(1)}, f32[4,8,1024]{2,1,0:T(8,128)S(1)}, u32[]{:S(2)}, u32[]{:S(2)}) collective-permute-start(f32[4,8,1024]{2,1,0:T(8,128)S(1)} %get-tuple-element.103), channel_id=1, source_target_pairs={{0,12},{4,8},{8,4},{12,0},{16,28},{20,24},{24,20},{28,16},{1,13},{... | collective-permute-start | bytes 393224 | tf_op jit(solution)/shard_map/ppermute | solution.py:906
  61.3 9.2 %collective-permute-start.26 = (f32[1,4,128,128]{3,2,1,0:T(8,128)S(1)}, f32[1,4,128,128]{3,2,1,0:T(8,128)S(1)}, u32[]{:S(2)}, u32[]{:S(2)}) collective-permute-start(f32[1,4,128,128]{3,2,1,0:T(8,128)S(1)} %get-tuple-element.109), channel_id=1, source_target_pairs={{0,1},{1,0},{2,3},{3,2},{4,5},{5,4},{6,7},{7,6},{8,9},{9,8},{10,11... | collective-permute-start | bytes 786440 | tf_op jit(solution)/shard_map/ppermute | solution.py:854
  63.1 9.7 %collective-permute-start.27 = (f32[1,4,128,128]{3,2,1,0:T(8,128)S(1)}, f32[1,4,128,128]{3,2,1,0:T(8,128)S(1)}, u32[]{:S(2)}, u32[]{:S(2)}) collective-permute-start(f32[1,4,128,128]{3,2,1,0:T(8,128)S(1)} %get-tuple-element.110), channel_id=1, source_target_pairs={{0,4},{1,2},{2,1},{3,7},{4,0},{5,6},{6,5},{7,3},{8,12},{9,10},{10,... | collective-permute-start | bytes 786440 | tf_op jit(solution)/shard_map/ppermute | solution.py:854
  65.9 17.0 %collective-permute-start.31 = (f32[1,4,128,128]{3,2,1,0:T(8,128)S(1)}, f32[1,4,128,128]{3,2,1,0:T(8,128)S(1)}, u32[]{:S(2)}, u32[]{:S(2)}) collective-permute-start(f32[1,4,128,128]{3,2,1,0:T(8,128)S(1)} %get-tuple-element.116), channel_id=1, source_target_pairs={{0,1},{1,0},{2,3},{3,2},{4,5},{5,4},{6,7},{7,6},{8,9},{9,8},{10,11... | collective-permute-start | bytes 786440 | tf_op jit(solution)/shard_map/ppermute | solution.py:854
  67.7 16.2 %collective-permute-start.32 = (f32[1,4,128,128]{3,2,1,0:T(8,128)S(1)}, f32[1,4,128,128]{3,2,1,0:T(8,128)S(1)}, u32[]{:S(2)}, u32[]{:S(2)}) collective-permute-start(f32[1,4,128,128]{3,2,1,0:T(8,128)S(1)} %get-tuple-element.117), channel_id=1, source_target_pairs={{0,4},{1,2},{2,1},{3,7},{4,0},{5,6},{6,5},{7,3},{8,12},{9,10},{10,... | collective-permute-start | bytes 786440 | tf_op jit(solution)/shard_map/ppermute | solution.py:854
  69.0 11.4 %collective-permute-start.23 = (f32[4,8,1024]{2,1,0:T(8,128)S(1)}, f32[4,8,1024]{2,1,0:T(8,128)S(1)}, u32[]{:S(2)}, u32[]{:S(2)}) collective-permute-start(f32[4,8,1024]{2,1,0:T(8,128)S(1)} %get-tuple-element.105), channel_id=1, source_target_pairs={{0,20},{4,16},{8,28},{12,24},{16,4},{20,0},{24,12},{28,8},{1,21},{... | collective-permute-start | bytes 393224 | tf_op jit(solution)/shard_map/ppermute | solution.py:906
  70.5 16.5 %collective-permute-start.24 = (f32[4,8,1024]{2,1,0:T(8,128)S(1)}, f32[4,8,1024]{2,1,0:T(8,128)S(1)}, u32[]{:S(2)}, u32[]{:S(2)}) collective-permute-start(f32[4,8,1024]{2,1,0:T(8,128)S(1)} %get-tuple-element.106), channel_id=1, source_target_pairs={{0,24},{4,28},{8,16},{12,20},{16,8},{20,12},{24,0},{28,4},{1,25},{... | collective-permute-start | bytes 393224 | tf_op jit(solution)/shard_map/ppermute | solution.py:906
  72.8 14.2 %collective-permute-start.25 = (f32[4,8,1024]{2,1,0:T(8,128)S(1)}, f32[4,8,1024]{2,1,0:T(8,128)S(1)}, u32[]{:S(2)}, u32[]{:S(2)}) collective-permute-start(f32[4,8,1024]{2,1,0:T(8,128)S(1)} %get-tuple-element.107), channel_id=1, source_target_pairs={{0,28},{4,24},{8,20},{12,16},{16,12},{20,8},{24,4},{28,0},{1,29},{... | collective-permute-start | bytes 393224 | tf_op jit(solution)/shard_map/ppermute | solution.py:906
  80.4 6.6 %collective-permute-start.28 = (f32[3,256]{1,0:T(4,128)S(1)}, f32[3,256]{1,0:T(4,128)S(1)}, u32[]{:S(2)}, u32[]{:S(2)}) collective-permute-start(f32[3,256]{1,0:T(4,128)S(1)} %get-tuple-element.114.refs_8_), channel_id=1, source_target_pairs={{0,3},{1,2},{2,1},{3,0},{4,7},{5,6},{6,5},{7,4},{8,11},{9,10},{10,... | collective-permute-start | bytes 9224 | tf_op jit(solution)/shard_map/ppermute | solution.py:915
  (17 other events, 69.0 us)

commit v5 on v4

--- a/solution.py
+++ b/solution.py
@@ -256,7 +256,7 @@
         source_ref, wavelet_hbm, prev_ref, speed_ref = refs.take(4)
     corr_in = refs.take() if step else None
     local_ref = refs.take() if ahead else None
-    tables = refs.take(2) if last else []
+    place_row = refs.take() if last else None
     if last:
         lap_ref = refs.take()
         blocks = refs.take(tiles[0])
@@ -280,10 +280,7 @@
             part = pl.ds(i * half, half)
             copies.append(pltpu.make_async_copy(w_in.at[0, part], w_ref.at[part], own_sems.at[1 + i]))
     if last:
-        fetched = refs.take(2)
-        tiles_ref, seen_ref, place_ref = refs.take(3)
-        for i, (a, b) in enumerate(zip(tables, fetched)):
-            late.append(pltpu.make_async_copy(a, b, own_sems.at[1 + i]))
+        tiles_ref, place_ref = refs.take(2)
     for copy in copies + late:
         copy.start()
     _, side, _ = now_ref.shape
@@ -307,7 +304,7 @@
     for copy in late:
         copy.wait()
     if last:
-        pack_back(*tiles[1:], *fetched, corr_ref, blocks, tiles_ref, seen_ref, place_ref)
+        pack_back(tiles[1], place_row, corr_ref, blocks, tiles_ref, place_ref)
     else:
         add_source(next_ref, source_ref, wavelet_ref, step, 0, side)
         copy_sends(next_ref, *sends, 0)
@@ -441,7 +438,7 @@
     )(*args)
 
 
-def u_call(step, last, wavelet, source, u, u_prev, halo, speed, w, corr, local, aperture, tile_slot, lat_dev, tile_side):
+def u_call(step, last, wavelet, source, u, u_prev, halo, speed, w, corr, local, place, n_shot, n_tiles, tile_side):
     field = sds(u.shape)
     edge = sds((1, HALO) + u.shape[1:])
     args, specs = [u, *halo, w], [VMEM] * 4
@@ -454,7 +451,6 @@
     ahead = local is not None
     if ahead:
         args, specs = args + [local], specs + [VMEM]
-    n_shot, n_tiles = aperture.shape
     cells = tile_side * tile_side
     capacity = n_tiles // 4
     rows, halos, lanes = work_space(*u.shape[:2])
@@ -464,17 +460,12 @@
     if not step:
         scratch += [pltpu.VMEM(u.shape, F32)]
     if last:
-        args += [in_hbm(aperture), in_hbm(tile_slot)]
-        specs += [HBM, HBM]
+        args, specs = args + [place], specs + [VMEM]
         outs = [field] + [sds((capacity, u.shape[0], cells))] * n_shot
-        scratch = [pltpu.VMEM(u.shape, F32)] + scratch + [
-            pltpu.SMEM(aperture.shape, jnp.int32),
-            pltpu.SMEM(tile_slot.shape, jnp.int32),
-            *tile_scratch(n_shot, capacity, u.shape[0], cells, n_tiles),
-        ]
+        scratch = [pltpu.VMEM(u.shape, F32)] + scratch + tile_scratch(n_shot, capacity, u.shape[0], cells, n_tiles)
     else:
         outs = [field] * 3 + [edge] * 2
-    body = functools.partial(u_kernel, step, last, ahead, (n_shot, lat_dev, tile_side))
+    body = functools.partial(u_kernel, step, last, ahead, (n_shot, tile_side))
     return stencil_call(body, specs, args, outs, [VMEM] * len(outs), scratch)
 
 
@@ -649,8 +640,25 @@
     return lax.rem(me + other, count)
 
 
+LANES = 128
+
+
+def to_row(values):
+    lane = lax.broadcasted_iota(jnp.int32, (1, LANES), 1)
+    row = jnp.zeros((1, LANES), jnp.int32)
+    for i, value in enumerate(values):
+        row = jnp.where(lane == i, value, row)
+    return row
+
+
+def from_row(row_ref, scalars_ref):
+    row = row_ref[...]
+    for i in range(scalars_ref.shape[0]):
+        scalars_ref[i] = row[0, i]
+
+
 def pack_kernel(aperture_hbm, slot_hbm, tiles_hbm, *rest):
-    *outs, table_ref, aperture_ref, slot_ref, tiles_ref, sems = rest
+    *outs, table_row, place_row, table_ref, aperture_ref, slot_ref, tiles_ref, seen_ref, place_ref, sems = rest
     pairs = ((aperture_hbm, aperture_ref), (slot_hbm, slot_ref), (tiles_hbm, tiles_ref))
     copies = [pltpu.make_async_copy(a, b, sems.at[i]) for i, (a, b) in enumerate(pairs)]
     for copy in copies:
@@ -680,6 +688,9 @@
         return carry
 
     lax.fori_loop(0, n_shot, shot, 0)
+    places(aperture_ref, slot_ref, lat_dev, n_shot, capacity, seen_ref, place_ref)
+    table_row[...] = to_row([table_ref[i] for i in range(table_ref.shape[0])])
+    place_row[...] = to_row([place_ref[i] for i in range(place_ref.shape[0])])
     copies[2].wait()
     for k in range(n_shot):
         base = partner_of(me, k, n_shot) * (capacity + 1)
@@ -690,21 +701,25 @@
 def pack_call(aperture, tile_slot, model_tiles, capacity):
     n_shot = aperture.shape[0]
     _, depth, cells = model_tiles.shape
-    *blocks, table = pl.pallas_call(
+    row = sds((1, LANES), jnp.int32)
+    *blocks, table, place = pl.pallas_call(
         pack_kernel,
-        out_shape=[sds((capacity, depth, cells))] * n_shot + [sds((n_shot * (capacity + 1),), jnp.int32)],
+        out_shape=[sds((capacity, depth, cells))] * n_shot + [row, row],
         in_specs=[HBM, HBM, HBM],
-        out_specs=[VMEM] * n_shot + [SMEM],
+        out_specs=[VMEM] * (n_shot + 2),
         scratch_shapes=[
+            pltpu.SMEM((n_shot * (capacity + 1),), jnp.int32),
             pltpu.SMEM(aperture.shape, jnp.int32),
             pltpu.SMEM(tile_slot.shape, jnp.int32),
             pltpu.VMEM(model_tiles.shape, F32),
+            pltpu.SMEM((n_shot,), jnp.int32),
+            pltpu.SMEM((aperture.shape[1],), jnp.int32),
             pltpu.SemaphoreType.DMA((3,)),
         ],
         compiler_params=params(8),
         name="pack",
     )(in_hbm(aperture), in_hbm(tile_slot), in_hbm(model_tiles))
-    return blocks, table
+    return blocks, table, place
 
 
 def places(aperture_ref, slot_ref, lat_dev, n_shot, capacity, seen_ref, place_ref):
@@ -722,24 +737,16 @@
     lax.fori_loop(0, aperture_ref.shape[1], tile, 0)
 
 
-def perturb_kernel(lat_dev, tile_side, aperture_hbm, slot_hbm, *rest):
-    *blocks, out_ref, tiles_ref, seen_ref, place_ref, aperture_ref, slot_ref, sems = rest
-    copies = [
-        pltpu.make_async_copy(aperture_hbm, aperture_ref, sems.at[0]),
-        pltpu.make_async_copy(slot_hbm, slot_ref, sems.at[1]),
-    ]
-    for copy in copies:
-        copy.start()
+def perturb_kernel(tile_side, place_row, *rest):
+    *blocks, out_ref, tiles_ref, place_ref = rest
     n_shot = len(blocks)
     capacity, depth, cells = blocks[0].shape
     side = out_ref.shape[1]
     across = side // tile_side
     flat_ref = out_ref.reshape(depth * side, side)
+    from_row(place_row, place_ref)
     for k in range(n_shot):
         tiles_ref[pl.ds(k * capacity, capacity)] = blocks[k][...]
-    for copy in copies:
-        copy.wait()
-    places(aperture_ref, slot_ref, lat_dev, n_shot, capacity, seen_ref, place_ref)
 
     def tile_row(i, carry):
         for high in range(cells // side):
@@ -751,13 +758,13 @@
     lax.fori_loop(0, across, tile_row, 0)
 
 
-def pack_back(lat_dev, tile_side, aperture_ref, slot_ref, corr_ref, blocks, tiles_ref, seen_ref, place_ref):
+def pack_back(tile_side, place_row, corr_ref, blocks, tiles_ref, place_ref):
     n_shot = len(blocks)
     capacity, depth, cells = blocks[0].shape
     side = corr_ref.shape[1]
     across = side // tile_side
     flat_ref = corr_ref.reshape(depth * side, side)
-    places(aperture_ref, slot_ref, lat_dev, n_shot, capacity, seen_ref, place_ref)
+    from_row(place_row, place_ref)
 
     def tile_row(i, carry):
         for high in range(cells // side):
@@ -774,38 +781,28 @@
 
 
 def tile_scratch(n_shot, capacity, depth, cells, n_tiles):
-    return [
-        pltpu.VMEM((n_shot * capacity, depth, cells), F32),
-        pltpu.SMEM((n_shot,), jnp.int32),
-        pltpu.SMEM((n_tiles,), jnp.int32),
-    ]
-
-
-def perturb_call(aperture, tile_slot, blocks, side, lat_dev, tile_side):
+    return [pltpu.VMEM((n_shot * capacity, depth, cells), F32), pltpu.SMEM((n_tiles,), jnp.int32)]
+
+
+def perturb_call(place, blocks, side, tile_side, n_tiles):
     capacity, depth, cells = blocks[0].shape
     return pl.pallas_call(
-        functools.partial(perturb_kernel, lat_dev, tile_side),
+        functools.partial(perturb_kernel, tile_side),
         out_shape=sds((depth, side, side)),
-        in_specs=[HBM, HBM] + [VMEM] * len(blocks),
+        in_specs=[VMEM] * (1 + len(blocks)),
         out_specs=VMEM,
-        scratch_shapes=[
-            *tile_scratch(len(blocks), capacity, depth, cells, aperture.shape[1]),
-            pltpu.SMEM(aperture.shape, jnp.int32),
-            pltpu.SMEM(tile_slot.shape, jnp.int32),
-            pltpu.SemaphoreType.DMA((2,)),
-        ],
+        scratch_shapes=tile_scratch(len(blocks), capacity, depth, cells, n_tiles),
         compiler_params=params(8),
         name="perturb",
-    )(in_hbm(aperture), in_hbm(tile_slot), *blocks)
-
-
-def finish_kernel(n_shot, table_hbm, *refs):
+    )(place, *blocks)
+
+
+def finish_kernel(n_shot, table_row, *refs):
     refs = Refs(refs)
     blocks = refs.take(n_shot)
-    parts = refs.refs[:-4]
-    sum_ref, record_ref, table_ref, sem = refs.refs[-4:]
-    fetch = pltpu.make_async_copy(table_hbm, table_ref, sem)
-    fetch.start()
+    parts = refs.refs[:-3]
+    sum_ref, record_ref, table_ref = refs.refs[-3:]
+    from_row(table_row, table_ref)
     capacity = blocks[0].shape[0]
     total = parts[0][...]
     for part in parts[1:]:
@@ -813,7 +810,6 @@
     for step in range(total.shape[0]):
         record_ref[step] = total[step : step + 1]
     sum_ref[...] = jnp.zeros(sum_ref.shape, F32)
-    fetch.wait()
     for k in range(n_shot):
         base = partner_of(lax.axis_index("shot"), k, n_shot) * (capacity + 1)
         for r in range(capacity):
@@ -830,9 +826,9 @@
     return pl.pallas_call(
         functools.partial(finish_kernel, len(blocks)),
         out_shape=[sds((lat_dev, depth, cells)), sds((steps, 1, n))],
-        in_specs=[HBM] + [VMEM] * (len(blocks) + len(parts)),
+        in_specs=[VMEM] * (1 + len(blocks) + len(parts)),
         out_specs=[VMEM, VMEM],
-        scratch_shapes=[pltpu.SMEM(table.shape, jnp.int32), pltpu.SemaphoreType.DMA(())],
+        scratch_shapes=[pltpu.SMEM((len(blocks) * (blocks[0].shape[0] + 1),), jnp.int32)],
         compiler_params=params(8),
         name="finish",
     )(table, *blocks, *parts)
@@ -935,18 +931,19 @@
     side = background.shape[-1]
     tile_side = math.isqrt(tile_cells)
     capacity = aperture.shape[1] // 4
+    n_shot = lax.axis_size("shot")
     steps = wavelet.shape[1]
     speed = background[0]
     u, d, w = u_now[0], du_now[0], w_now[0]
     up, dp, wp = u_prev[0], du_prev[0], w_prev[0]
 
-    tiling = (aperture, tile_slot, lat_dev, tile_side)
     u_halo = swap(first_edges([u_now]))
     dw_halo = swap(first_edges([du_now, w_now]))
-    outgoing, table = pack_call(aperture, tile_slot, model_tiles, capacity)
+    outgoing, table, place_row = pack_call(aperture, tile_slot, model_tiles, capacity)
     incoming = exchange(outgoing)
     count, outer = count_call(receiver_cells, depth, side)
-    perturb = perturb_call(aperture, tile_slot, incoming, side, lat_dev, tile_side)
+    perturb = perturb_call(place_row, incoming, side, tile_side, aperture.shape[1])
+    tiling = (place_row, n_shot, aperture.shape[1], tile_side)
 
     u_next, lap, corr, *edges = u_call(0, False, wavelet, source_cell, u, up, u_halo, speed, w_now, None, None, *tiling)
     u_halo = swap(edges)

time: 89.4 us -> 87.6 us (0.980)
  Pallas kernels: 26 us -> 23.9 us
    pallas_call x1, Pallas kernels: 1.95 us -> 0.96 us  [perturb_call(): pl.pallas_call(functools.partial(perturb_kernel, tile_side), out_shape=sd...]
  transfers between devices with their start and end apart: 33 -> 33, of which waited for: 14 -> 13; matrix products, arithmetic and copies ran while one was open for 0% -> 0% of each run, Pallas kernels for 23% -> 22%
where the time goes in v5:
time: 87.6 us; the launch traced here: 87.4 us
  starting transfers between devices  37.9 us (43%)
  Pallas kernels  23.9 us (27%)
  waiting for transfers between devices  23.6 us (27%)
  between operations  1.55 us (2%)
    ppermute x16, starting transfers between devices, swap(): got.append(lax.ppermute(edge, ('shot', 'slab'), sorted(pairs.items())))  18.8 us
    ppermute x14, starting transfers between devices, exchange(): got[k] = lax.ppermute(block, 'shot', moves) if moves else block  14.7 us
    ppermute x14, waiting for transfers between devices, exchange(): got[k] = lax.ppermute(block, 'shot', moves) if moves else block  13.2 us
    pallas_call x8, Pallas kernels, stencil_call(): pl.pallas_call(body, out_shape=outs, in_specs=in_specs, out_specs=kinds,...  12.6 us
    ppermute x16, waiting for transfers between devices, swap(): got.append(lax.ppermute(edge, ('shot', 'slab'), sorted(pairs.items())))  9.86 us
    ppermute x3, starting transfers between devices, slab_parts(): parts.append(lax.ppermute(part, 'slab', list(enumerate(to))))  4.39 us
    pallas_call x1, Pallas kernels, ahead_call(): pl.pallas_call(functools.partial(ahead_kernel, len(fields)), out_shape=ou...  2.94 us
    pallas_call x2, Pallas kernels, first_edges(): pl.pallas_call(functools.partial(edges_kernel, n), out_shape=[edge, edge]...  2.26 us
  transfers between devices with their start and end apart: 33, of which 13 were waited for; matrix products, arithmetic and copies ran while one was open for 0% of the time, Pallas kernels for 22%

profile of v5, /device:TPU:0, one launch (start us, length us, event | category | flops | bytes accessed | tf_op | source)
XLA Modules:
  0.0 87.4 jit_solution(4415384878671008909)
XLA Ops:
  0.6 1.5 %pack.1 = (f32[4,8,1024]{2,1,0:T(8,128)S(1)}, f32[4,8,1024]{2,1,0:T(8,128)S(1)}, f32[4,8,1024]{2,1,0:T(8,128)S(1)}, f32[4,8,1024]{2,1,0:T(8,128)S(1)}, f32[4,8,1...) custom-call(s32[8,16]{1,0:T(8,128)} %aperture_hbm.1, ...), custom_call_target="tpu_custom_call" | custom-call | tf_op jit(solution)/shard_map/pack/pallas_call | solution.py:705
  2.7 2.6 %collective-permute-start.7 = (f32[4,8,1024]{2,1,0:T(8,128)S(1)}, f32[4,8,1024]{2,1,0:T(8,128)S(1)}, u32[]{:S(2)}, u32[]{:S(2)}) collective-permute-start(f32[4,8,1024]{2,1,0:T(8,128)S(1)} %get-tuple-element.76), channel_id=1, source_target_pairs={{0,8},{4,12},{8,0},{12,4},{16,24},{20,28},{24,16},{28,20},{1,9},{5... | collective-permute-start | bytes 393224 | tf_op jit(solution)/shard_map/ppermute | solution.py:902
  6.5 1.6 %collective-permute-start.4 = (f32[2,4,128,128]{3,2,1,0:T(8,128)S(1)}, f32[2,4,128,128]{3,2,1,0:T(8,128)S(1)}, u32[]{:S(2)}, u32[]{:S(2)}) collective-permute-start(f32[2,4,128,128]{3,2,1,0:T(8,128)S(1)} %get-tuple-element.71), channel_id=1, source_target_pairs={{0,1},{1,0},{2,3},{3,2},{4,5},{5,4},{6,7},{7,6},{8,9},{9,8},{10,11... | collective-permute-start | bytes 1572872 | tf_op jit(solution)/shard_map/ppermute | solution.py:850
  8.8 1.5 %collective-permute-start.9 = (f32[4,8,1024]{2,1,0:T(8,128)S(1)}, f32[4,8,1024]{2,1,0:T(8,128)S(1)}, u32[]{:S(2)}, u32[]{:S(2)}) collective-permute-start(f32[4,8,1024]{2,1,0:T(8,128)S(1)} %get-tuple-element.78), channel_id=1, source_target_pairs={{0,16},{4,20},{8,24},{12,28},{16,0},{20,4},{24,8},{28,12},{1,17},{... | collective-permute-start | bytes 393224 | tf_op jit(solution)/shard_map/ppermute | solution.py:902
  10.3 2.9 %collective-permute-done.8.rest_3_ = f32[4,8,1024]{2,1,0:T(8,128)S(1)} collective-permute-done((f32[4,8,1024]{2,1,0:T(8,128)S(1)}, f32[4,8,1024]{2,1,0:T(8,128)S(1)}, u32[]{:S(2)}, u32[]{:S(2)}) %collective-permute-start.8) | collective-permute-done | bytes 131104 | tf_op jit(solution)/shard_map/ppermute | solution.py:902
  15.8 3.9 %collective-permute-start = (f32[1,4,128,128]{3,2,1,0:T(8,128)S(1)}, f32[1,4,128,128]{3,2,1,0:T(8,128)S(1)}, u32[]{:S(2)}, u32[]{:S(2)}) collective-permute-start(f32[1,4,128,128]{3,2,1,0:T(8,128)S(1)} %get-tuple-element.66), channel_id=1, source_target_pairs={{0,1},{1,0},{2,3},{3,2},{4,5},{5,4},{6,7},{7,6},{8,9},{9,8},{10,11... | collective-permute-start | bytes 786440 | tf_op jit(solution)/shard_map/ppermute | solution.py:850
  20.4 1.7 %collective-permute-start.12 = (f32[4,8,1024]{2,1,0:T(8,128)S(1)}, f32[4,8,1024]{2,1,0:T(8,128)S(1)}, u32[]{:S(2)}, u32[]{:S(2)}) collective-permute-start(f32[4,8,1024]{2,1,0:T(8,128)S(1)} %get-tuple-element.81), channel_id=1, source_target_pairs={{0,28},{4,24},{8,20},{12,16},{16,12},{20,8},{24,4},{28,0},{1,29},{... | collective-permute-start | bytes 393224 | tf_op jit(solution)/shard_map/ppermute | solution.py:902
  23.2 3.8 %collective-permute-done.12.rest_7_ = f32[4,8,1024]{2,1,0:T(8,128)S(1)} collective-permute-done((f32[4,8,1024]{2,1,0:T(8,128)S(1)}, f32[4,8,1024]{2,1,0:T(8,128)S(1)}, u32[]{:S(2)}, u32[]{:S(2)}) %collective-permute-start.12) | collective-permute-done | bytes 131104 | tf_op jit(solution)/shard_map/ppermute | solution.py:902
  28.3 1.9 %shard_map.165 = (f32[8,128,128]{2,1,0:T(8,128)S(1)}, f32[8,128,128]{2,1,0:T(8,128)S(1)}, f32[8,128,128]{2,1,0:T(8,128)S(1)}, f32[1,4,128,128]{3,2,1,0:T(8,128)S(1)}, f32[1,4,128,128]{3,2,1,0:T(8,128)S(1)}) custom-call(f32[8,128,128]{2,1,0:T(8,128)S(1)} %bitcast.17, f32[1,4,128,128]{3,2,1,0:T(8,128)S(1)} %collective-permute-done.refs_1_, ...), custom_call_target="tpu_custom_call" | custom-call | tf_op jit(solution)/shard_map/pallas_call | solution.py:436
  30.2 2.8 %collective-permute-start.2 = (f32[1,4,128,128]{3,2,1,0:T(8,128)S(1)}, f32[1,4,128,128]{3,2,1,0:T(8,128)S(1)}, u32[]{:S(2)}, u32[]{:S(2)}) collective-permute-start(f32[1,4,128,128]{3,2,1,0:T(8,128)S(1)} %get-tuple-element.69), channel_id=1, source_target_pairs={{0,1},{1,0},{2,3},{3,2},{4,5},{5,4},{6,7},{7,6},{8,9},{9,8},{10,11... | collective-permute-start | bytes 786440 | tf_op jit(solution)/shard_map/ppermute | solution.py:850
  36.7 2.0 %collective-permute-start.17 = (f32[1,4,128,128]{3,2,1,0:T(8,128)S(1)}, f32[1,4,128,128]{3,2,1,0:T(8,128)S(1)}, u32[]{:S(2)}, u32[]{:S(2)}) collective-permute-start(f32[1,4,128,128]{3,2,1,0:T(8,128)S(1)} %get-tuple-element.94), channel_id=1, source_target_pairs={{0,1},{1,0},{2,3},{3,2},{4,5},{5,4},{6,7},{7,6},{8,9},{9,8},{10,11... | collective-permute-start | bytes 786440 | tf_op jit(solution)/shard_map/ppermute | solution.py:850
  41.5 3.1 %collective-permute-start.13 = (f32[1,4,128,128]{3,2,1,0:T(8,128)S(1)}, f32[1,4,128,128]{3,2,1,0:T(8,128)S(1)}, u32[]{:S(2)}, u32[]{:S(2)}) collective-permute-start(f32[1,4,128,128]{3,2,1,0:T(8,128)S(1)} %get-tuple-element.88), channel_id=1, source_target_pairs={{0,1},{1,0},{2,3},{3,2},{4,5},{5,4},{6,7},{7,6},{8,9},{9,8},{10,11... | collective-permute-start | bytes 786440 | tf_op jit(solution)/shard_map/ppermute | solution.py:850
  45.8 2.9 %shard_map.170 = (f32[8,128,128]{2,1,0:T(8,128)S(1)}, f32[8,128,128]{2,1,0:T(8,128)S(1)}, f32[8,128,128]{2,1,0:T(8,128)S(1)}) custom-call(f32[8,128,128]{2,1,0:T(8,128)S(1)} %get-tuple-element.87.refs_0_.refs_7_, f32[8,128,128]{2,1,0:T(8,128)S(1)} %get-tuple-element.90.refs_1_.rest_0_, f32[8,128,128]{2,1,0:T(8,128)S(1)} %get-tuple-element.85.refs_3_.refs_2_.refs_1_), custom_call_target="tpu_custom_call" | custom-call | tf_op jit(solution)/shard_map/pallas_call | solution.py:182
  48.8 2.7 %collective-permute-done.17.refs_10_ = f32[1,4,128,128]{3,2,1,0:T(8,128)S(1)} collective-permute-done((f32[1,4,128,128]{3,2,1,0:T(8,128)S(1)}, f32[1,4,128,128]{3,2,1,0:T(8,128)S(1)}, u32[]{:S(2)}, u32[]{:S(2)}) %collective-permute-start.17) | collective-permute-done | bytes 262176 | tf_op jit(solution)/shard_map/ppermute | solution.py:850
  52.8 3.7 %collective-permute-done.13.refs_1_ = f32[1,4,128,128]{3,2,1,0:T(8,128)S(1)} collective-permute-done((f32[1,4,128,128]{3,2,1,0:T(8,128)S(1)}, f32[1,4,128,128]{3,2,1,0:T(8,128)S(1)}, u32[]{:S(2)}, u32[]{:S(2)}) %collective-permute-start.13) | collective-permute-done | bytes 262176 | tf_op jit(solution)/shard_map/ppermute | solution.py:850
  56.5 1.5 %shard_map.172 = (f32[8,128,128]{2,1,0:T(8,128)S(1)}, f32[4,8,1024]{2,1,0:T(8,128)S(1)}, f32[4,8,1024]{2,1,0:T(8,128)S(1)}, f32[4,8,1024]{2,1,0:T(8,128)S(1)}, f...) custom-call(f32[8,128,128]{2,1,0:T(8,128)S(1)} %get-tuple-element.87, ...), custom_call_target="tpu_custom_call" | custom-call | tf_op jit(solution)/shard_map/pallas_call | solution.py:436
  59.9 1.8 %collective-permute-start.26 = (f32[1,4,128,128]{3,2,1,0:T(8,128)S(1)}, f32[1,4,128,128]{3,2,1,0:T(8,128)S(1)}, u32[]{:S(2)}, u32[]{:S(2)}) collective-permute-start(f32[1,4,128,128]{3,2,1,0:T(8,128)S(1)} %get-tuple-element.111), channel_id=1, source_target_pairs={{0,1},{1,0},{2,3},{3,2},{4,5},{5,4},{6,7},{7,6},{8,9},{9,8},{10,11... | collective-permute-start | bytes 786440 | tf_op jit(solution)/shard_map/ppermute | solution.py:850
  64.5 1.8 %collective-permute-start.31 = (f32[1,4,128,128]{3,2,1,0:T(8,128)S(1)}, f32[1,4,128,128]{3,2,1,0:T(8,128)S(1)}, u32[]{:S(2)}, u32[]{:S(2)}) collective-permute-start(f32[1,4,128,128]{3,2,1,0:T(8,128)S(1)} %get-tuple-element.118), channel_id=1, source_target_pairs={{0,1},{1,0},{2,3},{3,2},{4,5},{5,4},{6,7},{7,6},{8,9},{9,8},{10,11... | collective-permute-start | bytes 786440 | tf_op jit(solution)/shard_map/ppermute | solution.py:850
  69.1 2.4 %collective-permute-start.24 = (f32[4,8,1024]{2,1,0:T(8,128)S(1)}, f32[4,8,1024]{2,1,0:T(8,128)S(1)}, u32[]{:S(2)}, u32[]{:S(2)}) collective-permute-start(f32[4,8,1024]{2,1,0:T(8,128)S(1)} %get-tuple-element.108), channel_id=1, source_target_pairs={{0,24},{4,28},{8,16},{12,20},{16,8},{20,12},{24,0},{28,4},{1,25},{... | collective-permute-start | bytes 393224 | tf_op jit(solution)/shard_map/ppermute | solution.py:902
  71.4 1.9 %shard_map.173 = (f32[1,256]{1,0:T(1,128)S(1)}, s32[1,256]{1,0:T(1,128)S(1)}) custom-call(s32[1,256]{1,0:T(1,128)S(1)} %copy-done.7, s32[1,256]{1,0:T(1,128)S(1)} %copy-done.7, f32[8,128,128]{2,1,0:T(8,128)S(1)} %get-tuple-element.90.refs_1_.rest_0_), custom_call_target="tpu_custom_call" | custom-call | tf_op jit(solution)/shard_map/pallas_call | solution.py:604
  73.4 1.9 %shard_map.174 = (f32[1,8,128,128]{3,2,1,0:T(8,128)}, f32[8,128,128]{2,1,0:T(8,128)S(1)}, f32[3,256]{1,0:T(4,128)S(1)}) custom-call(f32[8,128,128]{2,1,0:T(8,128)S(1)} %get-tuple-element.110.refs_0_, f32[8,128,128]{2,1,0:T(8,128)S(1)} %get-tuple-element.90.refs_1_.rest_0_, f32[1,4,128,128]{3,2,1,0:T(8,128)S(1)} %collective-permute-done.26.refs_2_, ...), custom_call_target="tpu_custom_call" | custom-call | tf_op jit(solution)/shard_map/pallas_call | solution.py:436
  75.3 3.7 %collective-permute-done.23.refs_5_ = f32[4,8,1024]{2,1,0:T(8,128)S(1)} collective-permute-done((f32[4,8,1024]{2,1,0:T(8,128)S(1)}, f32[4,8,1024]{2,1,0:T(8,128)S(1)}, u32[]{:S(2)}, u32[]{:S(2)}) %collective-permute-start.23) | collective-permute-done | bytes 131104 | tf_op jit(solution)/shard_map/ppermute | solution.py:902
  79.0 2.6 %collective-permute-start.28 = (f32[3,256]{1,0:T(4,128)S(1)}, f32[3,256]{1,0:T(4,128)S(1)}, u32[]{:S(2)}, u32[]{:S(2)}) collective-permute-start(f32[3,256]{1,0:T(4,128)S(1)} %get-tuple-element.116.refs_8_), channel_id=1, source_target_pairs={{0,3},{1,2},{2,1},{3,0},{4,7},{5,6},{6,5},{7,4},{8,11},{9,10},{10,... | collective-permute-start | bytes 9224 | tf_op jit(solution)/shard_map/ppermute | solution.py:911
  83.4 2.2 %shard_map.175 = (f32[1,8,128,128]{3,2,1,0:T(8,128)}, f32[1,8,128,128]{3,2,1,0:T(8,128)}) custom-call(f32[8,128,128]{2,1,0:T(8,128)S(1)} %get-tuple-element.99.refs_3_.refs_0_, f32[8,128,128]{2,1,0:T(8,128)S(1)} %get-tuple-element.85.refs_3_.refs_2_.refs_1_, f32[1,4,128,128]{3,2,1,0:T(8,128)S(1)} %collective-permute-done.31.refs_2_, ...), custom_call_target="tpu_custom_call" | custom-call | tf_op jit(solution)/shard_map/pallas_call | solution.py:436
  (74 shorter events, 27.5 us)
Async XLA Ops:
  2.7 7.6 %collective-permute-start.7 = (f32[4,8,1024]{2,1,0:T(8,128)S(1)}, f32[4,8,1024]{2,1,0:T(8,128)S(1)}, u32[]{:S(2)}, u32[]{:S(2)}) collective-permute-start(f32[4,8,1024]{2,1,0:T(8,128)S(1)} %get-tuple-element.76), channel_id=1, source_target_pairs={{0,8},{4,12},{8,0},{12,4},{16,24},{20,28},{24,16},{28,20},{1,9},{5... | collective-permute-start | bytes 393224 | tf_op jit(solution)/shard_map/ppermute | solution.py:902
  6.5 26.5 %collective-permute-start.4 = (f32[2,4,128,128]{3,2,1,0:T(8,128)S(1)}, f32[2,4,128,128]{3,2,1,0:T(8,128)S(1)}, u32[]{:S(2)}, u32[]{:S(2)}) collective-permute-start(f32[2,4,128,128]{3,2,1,0:T(8,128)S(1)} %get-tuple-element.71), channel_id=1, source_target_pairs={{0,1},{1,0},{2,3},{3,2},{4,5},{5,4},{6,7},{7,6},{8,9},{9,8},{10,11... | collective-permute-start | bytes 1572872 | tf_op jit(solution)/shard_map/ppermute | solution.py:850
  8.2 24.9 %collective-permute-start.5 = (f32[2,4,128,128]{3,2,1,0:T(8,128)S(1)}, f32[2,4,128,128]{3,2,1,0:T(8,128)S(1)}, u32[]{:S(2)}, u32[]{:S(2)}) collective-permute-start(f32[2,4,128,128]{3,2,1,0:T(8,128)S(1)} %get-tuple-element.72), channel_id=1, source_target_pairs={{0,4},{1,2},{2,1},{3,7},{4,0},{5,6},{6,5},{7,3},{8,12},{9,10},{10,... | collective-permute-start | bytes 1572872 | tf_op jit(solution)/shard_map/ppermute | solution.py:850
  8.8 7.0 %collective-permute-start.9 = (f32[4,8,1024]{2,1,0:T(8,128)S(1)}, f32[4,8,1024]{2,1,0:T(8,128)S(1)}, u32[]{:S(2)}, u32[]{:S(2)}) collective-permute-start(f32[4,8,1024]{2,1,0:T(8,128)S(1)} %get-tuple-element.78), channel_id=1, source_target_pairs={{0,16},{4,20},{8,24},{12,28},{16,0},{20,4},{24,8},{28,12},{1,17},{... | collective-permute-start | bytes 393224 | tf_op jit(solution)/shard_map/ppermute | solution.py:902
  10.3 9.4 %collective-permute-start.10 = (f32[4,8,1024]{2,1,0:T(8,128)S(1)}, f32[4,8,1024]{2,1,0:T(8,128)S(1)}, u32[]{:S(2)}, u32[]{:S(2)}) collective-permute-start(f32[4,8,1024]{2,1,0:T(8,128)S(1)} %get-tuple-element.79), channel_id=1, source_target_pairs={{0,20},{4,16},{8,28},{12,24},{16,4},{20,0},{24,12},{28,8},{1,21},{... | collective-permute-start | bytes 393224 | tf_op jit(solution)/shard_map/ppermute | solution.py:902
  13.3 7.1 %collective-permute-start.11 = (f32[4,8,1024]{2,1,0:T(8,128)S(1)}, f32[4,8,1024]{2,1,0:T(8,128)S(1)}, u32[]{:S(2)}, u32[]{:S(2)}) collective-permute-start(f32[4,8,1024]{2,1,0:T(8,128)S(1)} %get-tuple-element.80), channel_id=1, source_target_pairs={{0,24},{4,28},{8,16},{12,20},{16,8},{20,12},{24,0},{28,4},{1,25},{... | collective-permute-start | bytes 393224 | tf_op jit(solution)/shard_map/ppermute | solution.py:902
  15.8 12.1 %collective-permute-start = (f32[1,4,128,128]{3,2,1,0:T(8,128)S(1)}, f32[1,4,128,128]{3,2,1,0:T(8,128)S(1)}, u32[]{:S(2)}, u32[]{:S(2)}) collective-permute-start(f32[1,4,128,128]{3,2,1,0:T(8,128)S(1)} %get-tuple-element.66), channel_id=1, source_target_pairs={{0,1},{1,0},{2,3},{3,2},{4,5},{5,4},{6,7},{7,6},{8,9},{9,8},{10,11... | collective-permute-start | bytes 786440 | tf_op jit(solution)/shard_map/ppermute | solution.py:850
  19.7 8.2 %collective-permute-start.1 = (f32[1,4,128,128]{3,2,1,0:T(8,128)S(1)}, f32[1,4,128,128]{3,2,1,0:T(8,128)S(1)}, u32[]{:S(2)}, u32[]{:S(2)}) collective-permute-start(f32[1,4,128,128]{3,2,1,0:T(8,128)S(1)} %get-tuple-element.67), channel_id=1, source_target_pairs={{0,4},{1,2},{2,1},{3,7},{4,0},{5,6},{6,5},{7,3},{8,12},{9,10},{10,... | collective-permute-start | bytes 786440 | tf_op jit(solution)/shard_map/ppermute | solution.py:850
  30.2 10.0 %collective-permute-start.2 = (f32[1,4,128,128]{3,2,1,0:T(8,128)S(1)}, f32[1,4,128,128]{3,2,1,0:T(8,128)S(1)}, u32[]{:S(2)}, u32[]{:S(2)}) collective-permute-start(f32[1,4,128,128]{3,2,1,0:T(8,128)S(1)} %get-tuple-element.69), channel_id=1, source_target_pairs={{0,1},{1,0},{2,3},{3,2},{4,5},{5,4},{6,7},{7,6},{8,9},{9,8},{10,11... | collective-permute-start | bytes 786440 | tf_op jit(solution)/shard_map/ppermute | solution.py:850
  33.0 7.2 %collective-permute-start.3 = (f32[1,4,128,128]{3,2,1,0:T(8,128)S(1)}, f32[1,4,128,128]{3,2,1,0:T(8,128)S(1)}, u32[]{:S(2)}, u32[]{:S(2)}) collective-permute-start(f32[1,4,128,128]{3,2,1,0:T(8,128)S(1)} %get-tuple-element.70), channel_id=1, source_target_pairs={{0,4},{1,2},{2,1},{3,7},{4,0},{5,6},{6,5},{7,3},{8,12},{9,10},{10,... | collective-permute-start | bytes 786440 | tf_op jit(solution)/shard_map/ppermute | solution.py:850
  35.6 10.2 %collective-permute-start.15 = (f32[1,4,128,128]{3,2,1,0:T(8,128)S(1)}, f32[1,4,128,128]{3,2,1,0:T(8,128)S(1)}, u32[]{:S(2)}, u32[]{:S(2)}) collective-permute-start(f32[1,4,128,128]{3,2,1,0:T(8,128)S(1)} %get-tuple-element.92), channel_id=1, source_target_pairs={{0,1},{1,0},{2,3},{3,2},{4,5},{5,4},{6,7},{7,6},{8,9},{9,8},{10,11... | collective-permute-start | bytes 786440 | tf_op jit(solution)/shard_map/ppermute | solution.py:850
  36.7 12.0 %collective-permute-start.16 = (f32[1,4,128,128]{3,2,1,0:T(8,128)S(1)}, f32[1,4,128,128]{3,2,1,0:T(8,128)S(1)}, u32[]{:S(2)}, u32[]{:S(2)}) collective-permute-start(f32[1,4,128,128]{3,2,1,0:T(8,128)S(1)} %get-tuple-element.93), channel_id=1, source_target_pairs={{0,4},{1,2},{2,1},{3,7},{4,0},{5,6},{6,5},{7,3},{8,12},{9,10},{10,... | collective-permute-start | bytes 786440 | tf_op jit(solution)/shard_map/ppermute | solution.py:850
  36.7 14.7 %collective-permute-start.17 = (f32[1,4,128,128]{3,2,1,0:T(8,128)S(1)}, f32[1,4,128,128]{3,2,1,0:T(8,128)S(1)}, u32[]{:S(2)}, u32[]{:S(2)}) collective-permute-start(f32[1,4,128,128]{3,2,1,0:T(8,128)S(1)} %get-tuple-element.94), channel_id=1, source_target_pairs={{0,1},{1,0},{2,3},{3,2},{4,5},{5,4},{6,7},{7,6},{8,9},{9,8},{10,11... | collective-permute-start | bytes 786440 | tf_op jit(solution)/shard_map/ppermute | solution.py:850
  40.2 11.2 %collective-permute-start.18 = (f32[1,4,128,128]{3,2,1,0:T(8,128)S(1)}, f32[1,4,128,128]{3,2,1,0:T(8,128)S(1)}, u32[]{:S(2)}, u32[]{:S(2)}) collective-permute-start(f32[1,4,128,128]{3,2,1,0:T(8,128)S(1)} %get-tuple-element.95), channel_id=1, source_target_pairs={{0,4},{1,2},{2,1},{3,7},{4,0},{5,6},{6,5},{7,3},{8,12},{9,10},{10,... | collective-permute-start | bytes 786440 | tf_op jit(solution)/shard_map/ppermute | solution.py:850
  41.5 15.0 %collective-permute-start.13 = (f32[1,4,128,128]{3,2,1,0:T(8,128)S(1)}, f32[1,4,128,128]{3,2,1,0:T(8,128)S(1)}, u32[]{:S(2)}, u32[]{:S(2)}) collective-permute-start(f32[1,4,128,128]{3,2,1,0:T(8,128)S(1)} %get-tuple-element.88), channel_id=1, source_target_pairs={{0,1},{1,0},{2,3},{3,2},{4,5},{5,4},{6,7},{7,6},{8,9},{9,8},{10,11... | collective-permute-start | bytes 786440 | tf_op jit(solution)/shard_map/ppermute | solution.py:850
  45.8 10.7 %collective-permute-start.14 = (f32[1,4,128,128]{3,2,1,0:T(8,128)S(1)}, f32[1,4,128,128]{3,2,1,0:T(8,128)S(1)}, u32[]{:S(2)}, u32[]{:S(2)}) collective-permute-start(f32[1,4,128,128]{3,2,1,0:T(8,128)S(1)} %get-tuple-element.89), channel_id=1, source_target_pairs={{0,4},{1,2},{2,1},{3,7},{4,0},{5,6},{6,5},{7,3},{8,12},{9,10},{10,... | collective-permute-start | bytes 786440 | tf_op jit(solution)/shard_map/ppermute | solution.py:850
  59.3 7.0 %collective-permute-start.21 = (f32[4,8,1024]{2,1,0:T(8,128)S(1)}, f32[4,8,1024]{2,1,0:T(8,128)S(1)}, u32[]{:S(2)}, u32[]{:S(2)}) collective-permute-start(f32[4,8,1024]{2,1,0:T(8,128)S(1)} %get-tuple-element.105), channel_id=1, source_target_pairs={{0,12},{4,8},{8,4},{12,0},{16,28},{20,24},{24,20},{28,16},{1,13},{... | collective-permute-start | bytes 393224 | tf_op jit(solution)/shard_map/ppermute | solution.py:902
  59.9 9.2 %collective-permute-start.26 = (f32[1,4,128,128]{3,2,1,0:T(8,128)S(1)}, f32[1,4,128,128]{3,2,1,0:T(8,128)S(1)}, u32[]{:S(2)}, u32[]{:S(2)}) collective-permute-start(f32[1,4,128,128]{3,2,1,0:T(8,128)S(1)} %get-tuple-element.111), channel_id=1, source_target_pairs={{0,1},{1,0},{2,3},{3,2},{4,5},{5,4},{6,7},{7,6},{8,9},{9,8},{10,11... | collective-permute-start | bytes 786440 | tf_op jit(solution)/shard_map/ppermute | solution.py:850
  61.7 9.7 %collective-permute-start.27 = (f32[1,4,128,128]{3,2,1,0:T(8,128)S(1)}, f32[1,4,128,128]{3,2,1,0:T(8,128)S(1)}, u32[]{:S(2)}, u32[]{:S(2)}) collective-permute-start(f32[1,4,128,128]{3,2,1,0:T(8,128)S(1)} %get-tuple-element.112), channel_id=1, source_target_pairs={{0,4},{1,2},{2,1},{3,7},{4,0},{5,6},{6,5},{7,3},{8,12},{9,10},{10,... | collective-permute-start | bytes 786440 | tf_op jit(solution)/shard_map/ppermute | solution.py:850
  64.5 17.1 %collective-permute-start.31 = (f32[1,4,128,128]{3,2,1,0:T(8,128)S(1)}, f32[1,4,128,128]{3,2,1,0:T(8,128)S(1)}, u32[]{:S(2)}, u32[]{:S(2)}) collective-permute-start(f32[1,4,128,128]{3,2,1,0:T(8,128)S(1)} %get-tuple-element.118), channel_id=1, source_target_pairs={{0,1},{1,0},{2,3},{3,2},{4,5},{5,4},{6,7},{7,6},{8,9},{9,8},{10,11... | collective-permute-start | bytes 786440 | tf_op jit(solution)/shard_map/ppermute | solution.py:850
  66.3 16.3 %collective-permute-start.32 = (f32[1,4,128,128]{3,2,1,0:T(8,128)S(1)}, f32[1,4,128,128]{3,2,1,0:T(8,128)S(1)}, u32[]{:S(2)}, u32[]{:S(2)}) collective-permute-start(f32[1,4,128,128]{3,2,1,0:T(8,128)S(1)} %get-tuple-element.119), channel_id=1, source_target_pairs={{0,4},{1,2},{2,1},{3,7},{4,0},{5,6},{6,5},{7,3},{8,12},{9,10},{10,... | collective-permute-start | bytes 786440 | tf_op jit(solution)/shard_map/ppermute | solution.py:850
  67.6 11.4 %collective-permute-start.23 = (f32[4,8,1024]{2,1,0:T(8,128)S(1)}, f32[4,8,1024]{2,1,0:T(8,128)S(1)}, u32[]{:S(2)}, u32[]{:S(2)}) collective-permute-start(f32[4,8,1024]{2,1,0:T(8,128)S(1)} %get-tuple-element.107), channel_id=1, source_target_pairs={{0,20},{4,16},{8,28},{12,24},{16,4},{20,0},{24,12},{28,8},{1,21},{... | collective-permute-start | bytes 393224 | tf_op jit(solution)/shard_map/ppermute | solution.py:902
  69.1 16.5 %collective-permute-start.24 = (f32[4,8,1024]{2,1,0:T(8,128)S(1)}, f32[4,8,1024]{2,1,0:T(8,128)S(1)}, u32[]{:S(2)}, u32[]{:S(2)}) collective-permute-start(f32[4,8,1024]{2,1,0:T(8,128)S(1)} %get-tuple-element.108), channel_id=1, source_target_pairs={{0,24},{4,28},{8,16},{12,20},{16,8},{20,12},{24,0},{28,4},{1,25},{... | collective-permute-start | bytes 393224 | tf_op jit(solution)/shard_map/ppermute | solution.py:902
  71.4 14.2 %collective-permute-start.25 = (f32[4,8,1024]{2,1,0:T(8,128)S(1)}, f32[4,8,1024]{2,1,0:T(8,128)S(1)}, u32[]{:S(2)}, u32[]{:S(2)}) collective-permute-start(f32[4,8,1024]{2,1,0:T(8,128)S(1)} %get-tuple-element.109), channel_id=1, source_target_pairs={{0,28},{4,24},{8,20},{12,16},{16,12},{20,8},{24,4},{28,0},{1,29},{... | collective-permute-start | bytes 393224 | tf_op jit(solution)/shard_map/ppermute | solution.py:902
  (17 other events, 67.0 us)

commit v6 on v5

--- a/solution.py
+++ b/solution.py
@@ -858,9 +858,10 @@
     copies = []
     for out_ref, at in zip(outs, (low, depth - HALO - low)):
         for index, field_ref in enumerate(fields):
-            copies.append(
-                pltpu.make_async_copy(field_ref.at[0, pl.ds(at, HALO)], out_ref.at[index], sems.at[len(copies)])
-            )
+            for z in range(HALO):
+                copies.append(
+                    pltpu.make_async_copy(field_ref.at[0, at + z], out_ref.at[index, z], sems.at[len(copies)])
+                )
     for copy in copies:
         copy.start()
     for copy in copies:
@@ -875,7 +876,7 @@
         out_shape=[edge, edge],
         in_specs=[HBM] * n,
         out_specs=[VMEM, VMEM],
-        scratch_shapes=[pltpu.SemaphoreType.DMA((2 * n,))],
+        scratch_shapes=[pltpu.SemaphoreType.DMA((2 * n * HALO,))],
         compiler_params=params(8),
     )(*map(in_hbm, fields))
 

time: 87.6 us -> 87.9 us (level)
  transfers between devices with their start and end apart: 33 -> 33, of which waited for: 13 -> 13; matrix products, arithmetic and copies ran while one was open for 0% -> 0% of each run, Pallas kernels for 22% -> 23%
where the time goes in v6:
time: 87.9 us; the launch traced here: 87.5 us
  starting transfers between devices  37.9 us (43%)
  Pallas kernels  24.1 us (27%)
  waiting for transfers between devices  23.5 us (27%)
  between operations  1.55 us (2%)
    ppermute x16, starting transfers between devices, swap(): got.append(lax.ppermute(edge, ('shot', 'slab'), sorted(pairs.items())))  18.8 us
    ppermute x14, starting transfers between devices, exchange(): got[k] = lax.ppermute(block, 'shot', moves) if moves else block  14.7 us
    ppermute x14, waiting for transfers between devices, exchange(): got[k] = lax.ppermute(block, 'shot', moves) if moves else block  13.1 us
    pallas_call x8, Pallas kernels, stencil_call(): pl.pallas_call(body, out_shape=outs, in_specs=in_specs, out_specs=kinds,...  12.6 us
    ppermute x16, waiting for transfers between devices, swap(): got.append(lax.ppermute(edge, ('shot', 'slab'), sorted(pairs.items())))  9.86 us
    ppermute x3, starting transfers between devices, slab_parts(): parts.append(lax.ppermute(part, 'slab', list(enumerate(to))))  4.39 us
    pallas_call x1, Pallas kernels, ahead_call(): pl.pallas_call(functools.partial(ahead_kernel, len(fields)), out_shape=ou...  2.94 us
    pallas_call x2, Pallas kernels, first_edges(): pl.pallas_call(functools.partial(edges_kernel, n), out_shape=[edge, edge]...  2.5 us
  transfers between devices with their start and end apart: 33, of which 13 were waited for; matrix products, arithmetic and copies ran while one was open for 0% of the time, Pallas kernels for 23%

profile of v6, /device:TPU:0, one launch (start us, length us, event | category | flops | bytes accessed | tf_op | source)
XLA Modules:
  0.0 87.5 jit_solution(2817974890016538460)
XLA Ops:
  0.6 1.5 %pack.1 = (f32[4,8,1024]{2,1,0:T(8,128)S(1)}, f32[4,8,1024]{2,1,0:T(8,128)S(1)}, f32[4,8,1024]{2,1,0:T(8,128)S(1)}, f32[4,8,1024]{2,1,0:T(8,128)S(1)}, f32[4,8,1...) custom-call(s32[8,16]{1,0:T(8,128)} %aperture_hbm.1, ...), custom_call_target="tpu_custom_call" | custom-call | tf_op jit(solution)/shard_map/pack/pallas_call | solution.py:705
  2.7 2.6 %collective-permute-start.7 = (f32[4,8,1024]{2,1,0:T(8,128)S(1)}, f32[4,8,1024]{2,1,0:T(8,128)S(1)}, u32[]{:S(2)}, u32[]{:S(2)}) collective-permute-start(f32[4,8,1024]{2,1,0:T(8,128)S(1)} %get-tuple-element.76), channel_id=1, source_target_pairs={{0,8},{4,12},{8,0},{12,4},{16,24},{20,28},{24,16},{28,20},{1,9},{5... | collective-permute-start | bytes 393224 | tf_op jit(solution)/shard_map/ppermute | solution.py:903
  6.7 1.6 %collective-permute-start.4 = (f32[2,4,128,128]{3,2,1,0:T(8,128)S(1)}, f32[2,4,128,128]{3,2,1,0:T(8,128)S(1)}, u32[]{:S(2)}, u32[]{:S(2)}) collective-permute-start(f32[2,4,128,128]{3,2,1,0:T(8,128)S(1)} %get-tuple-element.71), channel_id=1, source_target_pairs={{0,1},{1,0},{2,3},{3,2},{4,5},{5,4},{6,7},{7,6},{8,9},{9,8},{10,11... | collective-permute-start | bytes 1572872 | tf_op jit(solution)/shard_map/ppermute | solution.py:850
  9.0 1.5 %collective-permute-start.9 = (f32[4,8,1024]{2,1,0:T(8,128)S(1)}, f32[4,8,1024]{2,1,0:T(8,128)S(1)}, u32[]{:S(2)}, u32[]{:S(2)}) collective-permute-start(f32[4,8,1024]{2,1,0:T(8,128)S(1)} %get-tuple-element.78), channel_id=1, source_target_pairs={{0,16},{4,20},{8,24},{12,28},{16,0},{20,4},{24,8},{28,12},{1,17},{... | collective-permute-start | bytes 393224 | tf_op jit(solution)/shard_map/ppermute | solution.py:903
  10.5 2.9 %collective-permute-done.8.rest_3_ = f32[4,8,1024]{2,1,0:T(8,128)S(1)} collective-permute-done((f32[4,8,1024]{2,1,0:T(8,128)S(1)}, f32[4,8,1024]{2,1,0:T(8,128)S(1)}, u32[]{:S(2)}, u32[]{:S(2)}) %collective-permute-start.8) | collective-permute-done | bytes 131104 | tf_op jit(solution)/shard_map/ppermute | solution.py:903
  16.1 3.9 %collective-permute-start = (f32[1,4,128,128]{3,2,1,0:T(8,128)S(1)}, f32[1,4,128,128]{3,2,1,0:T(8,128)S(1)}, u32[]{:S(2)}, u32[]{:S(2)}) collective-permute-start(f32[1,4,128,128]{3,2,1,0:T(8,128)S(1)} %get-tuple-element.66), channel_id=1, source_target_pairs={{0,1},{1,0},{2,3},{3,2},{4,5},{5,4},{6,7},{7,6},{8,9},{9,8},{10,11... | collective-permute-start | bytes 786440 | tf_op jit(solution)/shard_map/ppermute | solution.py:850
  20.5 1.7 %collective-permute-start.12 = (f32[4,8,1024]{2,1,0:T(8,128)S(1)}, f32[4,8,1024]{2,1,0:T(8,128)S(1)}, u32[]{:S(2)}, u32[]{:S(2)}) collective-permute-start(f32[4,8,1024]{2,1,0:T(8,128)S(1)} %get-tuple-element.81), channel_id=1, source_target_pairs={{0,28},{4,24},{8,20},{12,16},{16,12},{20,8},{24,4},{28,0},{1,29},{... | collective-permute-start | bytes 393224 | tf_op jit(solution)/shard_map/ppermute | solution.py:903
  23.3 3.8 %collective-permute-done.12.rest_7_ = f32[4,8,1024]{2,1,0:T(8,128)S(1)} collective-permute-done((f32[4,8,1024]{2,1,0:T(8,128)S(1)}, f32[4,8,1024]{2,1,0:T(8,128)S(1)}, u32[]{:S(2)}, u32[]{:S(2)}) %collective-permute-start.12) | collective-permute-done | bytes 131104 | tf_op jit(solution)/shard_map/ppermute | solution.py:903
  28.5 1.9 %shard_map.165 = (f32[8,128,128]{2,1,0:T(8,128)S(1)}, f32[8,128,128]{2,1,0:T(8,128)S(1)}, f32[8,128,128]{2,1,0:T(8,128)S(1)}, f32[1,4,128,128]{3,2,1,0:T(8,128)S(1)}, f32[1,4,128,128]{3,2,1,0:T(8,128)S(1)}) custom-call(f32[8,128,128]{2,1,0:T(8,128)S(1)} %bitcast.17, f32[1,4,128,128]{3,2,1,0:T(8,128)S(1)} %collective-permute-done.refs_1_, ...), custom_call_target="tpu_custom_call" | custom-call | tf_op jit(solution)/shard_map/pallas_call | solution.py:436
  30.3 2.8 %collective-permute-start.2 = (f32[1,4,128,128]{3,2,1,0:T(8,128)S(1)}, f32[1,4,128,128]{3,2,1,0:T(8,128)S(1)}, u32[]{:S(2)}, u32[]{:S(2)}) collective-permute-start(f32[1,4,128,128]{3,2,1,0:T(8,128)S(1)} %get-tuple-element.69), channel_id=1, source_target_pairs={{0,1},{1,0},{2,3},{3,2},{4,5},{5,4},{6,7},{7,6},{8,9},{9,8},{10,11... | collective-permute-start | bytes 786440 | tf_op jit(solution)/shard_map/ppermute | solution.py:850
  36.9 2.0 %collective-permute-start.17 = (f32[1,4,128,128]{3,2,1,0:T(8,128)S(1)}, f32[1,4,128,128]{3,2,1,0:T(8,128)S(1)}, u32[]{:S(2)}, u32[]{:S(2)}) collective-permute-start(f32[1,4,128,128]{3,2,1,0:T(8,128)S(1)} %get-tuple-element.94), channel_id=1, source_target_pairs={{0,1},{1,0},{2,3},{3,2},{4,5},{5,4},{6,7},{7,6},{8,9},{9,8},{10,11... | collective-permute-start | bytes 786440 | tf_op jit(solution)/shard_map/ppermute | solution.py:850
  41.6 3.1 %collective-permute-start.13 = (f32[1,4,128,128]{3,2,1,0:T(8,128)S(1)}, f32[1,4,128,128]{3,2,1,0:T(8,128)S(1)}, u32[]{:S(2)}, u32[]{:S(2)}) collective-permute-start(f32[1,4,128,128]{3,2,1,0:T(8,128)S(1)} %get-tuple-element.88), channel_id=1, source_target_pairs={{0,1},{1,0},{2,3},{3,2},{4,5},{5,4},{6,7},{7,6},{8,9},{9,8},{10,11... | collective-permute-start | bytes 786440 | tf_op jit(solution)/shard_map/ppermute | solution.py:850
  45.9 2.9 %shard_map.170 = (f32[8,128,128]{2,1,0:T(8,128)S(1)}, f32[8,128,128]{2,1,0:T(8,128)S(1)}, f32[8,128,128]{2,1,0:T(8,128)S(1)}) custom-call(f32[8,128,128]{2,1,0:T(8,128)S(1)} %get-tuple-element.87.refs_0_.refs_7_, f32[8,128,128]{2,1,0:T(8,128)S(1)} %get-tuple-element.90.refs_1_.rest_0_, f32[8,128,128]{2,1,0:T(8,128)S(1)} %get-tuple-element.85.refs_3_.refs_2_.refs_1_), custom_call_target="tpu_custom_call" | custom-call | tf_op jit(solution)/shard_map/pallas_call | solution.py:182
  48.9 2.7 %collective-permute-done.17.refs_10_ = f32[1,4,128,128]{3,2,1,0:T(8,128)S(1)} collective-permute-done((f32[1,4,128,128]{3,2,1,0:T(8,128)S(1)}, f32[1,4,128,128]{3,2,1,0:T(8,128)S(1)}, u32[]{:S(2)}, u32[]{:S(2)}) %collective-permute-start.17) | collective-permute-done | bytes 262176 | tf_op jit(solution)/shard_map/ppermute | solution.py:850
  52.9 3.7 %collective-permute-done.13.refs_1_ = f32[1,4,128,128]{3,2,1,0:T(8,128)S(1)} collective-permute-done((f32[1,4,128,128]{3,2,1,0:T(8,128)S(1)}, f32[1,4,128,128]{3,2,1,0:T(8,128)S(1)}, u32[]{:S(2)}, u32[]{:S(2)}) %collective-permute-start.13) | collective-permute-done | bytes 262176 | tf_op jit(solution)/shard_map/ppermute | solution.py:850
  56.6 1.5 %shard_map.172 = (f32[8,128,128]{2,1,0:T(8,128)S(1)}, f32[4,8,1024]{2,1,0:T(8,128)S(1)}, f32[4,8,1024]{2,1,0:T(8,128)S(1)}, f32[4,8,1024]{2,1,0:T(8,128)S(1)}, f...) custom-call(f32[8,128,128]{2,1,0:T(8,128)S(1)} %get-tuple-element.87, ...), custom_call_target="tpu_custom_call" | custom-call | tf_op jit(solution)/shard_map/pallas_call | solution.py:436
  60.0 1.8 %collective-permute-start.26 = (f32[1,4,128,128]{3,2,1,0:T(8,128)S(1)}, f32[1,4,128,128]{3,2,1,0:T(8,128)S(1)}, u32[]{:S(2)}, u32[]{:S(2)}) collective-permute-start(f32[1,4,128,128]{3,2,1,0:T(8,128)S(1)} %get-tuple-element.111), channel_id=1, source_target_pairs={{0,1},{1,0},{2,3},{3,2},{4,5},{5,4},{6,7},{7,6},{8,9},{9,8},{10,11... | collective-permute-start | bytes 786440 | tf_op jit(solution)/shard_map/ppermute | solution.py:850
  64.6 1.8 %collective-permute-start.31 = (f32[1,4,128,128]{3,2,1,0:T(8,128)S(1)}, f32[1,4,128,128]{3,2,1,0:T(8,128)S(1)}, u32[]{:S(2)}, u32[]{:S(2)}) collective-permute-start(f32[1,4,128,128]{3,2,1,0:T(8,128)S(1)} %get-tuple-element.118), channel_id=1, source_target_pairs={{0,1},{1,0},{2,3},{3,2},{4,5},{5,4},{6,7},{7,6},{8,9},{9,8},{10,11... | collective-permute-start | bytes 786440 | tf_op jit(solution)/shard_map/ppermute | solution.py:850
  69.2 2.4 %collective-permute-start.24 = (f32[4,8,1024]{2,1,0:T(8,128)S(1)}, f32[4,8,1024]{2,1,0:T(8,128)S(1)}, u32[]{:S(2)}, u32[]{:S(2)}) collective-permute-start(f32[4,8,1024]{2,1,0:T(8,128)S(1)} %get-tuple-element.108), channel_id=1, source_target_pairs={{0,24},{4,28},{8,16},{12,20},{16,8},{20,12},{24,0},{28,4},{1,25},{... | collective-permute-start | bytes 393224 | tf_op jit(solution)/shard_map/ppermute | solution.py:903
  71.6 1.9 %shard_map.173 = (f32[1,256]{1,0:T(1,128)S(1)}, s32[1,256]{1,0:T(1,128)S(1)}) custom-call(s32[1,256]{1,0:T(1,128)S(1)} %copy-done.7, s32[1,256]{1,0:T(1,128)S(1)} %copy-done.7, f32[8,128,128]{2,1,0:T(8,128)S(1)} %get-tuple-element.90.refs_1_.rest_0_), custom_call_target="tpu_custom_call" | custom-call | tf_op jit(solution)/shard_map/pallas_call | solution.py:604
  73.5 1.9 %shard_map.174 = (f32[1,8,128,128]{3,2,1,0:T(8,128)}, f32[8,128,128]{2,1,0:T(8,128)S(1)}, f32[3,256]{1,0:T(4,128)S(1)}) custom-call(f32[8,128,128]{2,1,0:T(8,128)S(1)} %get-tuple-element.110.refs_0_, f32[8,128,128]{2,1,0:T(8,128)S(1)} %get-tuple-element.90.refs_1_.rest_0_, f32[1,4,128,128]{3,2,1,0:T(8,128)S(1)} %collective-permute-done.26.refs_2_, ...), custom_call_target="tpu_custom_call" | custom-call | tf_op jit(solution)/shard_map/pallas_call | solution.py:436
  75.5 3.7 %collective-permute-done.23.refs_5_ = f32[4,8,1024]{2,1,0:T(8,128)S(1)} collective-permute-done((f32[4,8,1024]{2,1,0:T(8,128)S(1)}, f32[4,8,1024]{2,1,0:T(8,128)S(1)}, u32[]{:S(2)}, u32[]{:S(2)}) %collective-permute-start.23) | collective-permute-done | bytes 131104 | tf_op jit(solution)/shard_map/ppermute | solution.py:903
  79.1 2.6 %collective-permute-start.28 = (f32[3,256]{1,0:T(4,128)S(1)}, f32[3,256]{1,0:T(4,128)S(1)}, u32[]{:S(2)}, u32[]{:S(2)}) collective-permute-start(f32[3,256]{1,0:T(4,128)S(1)} %get-tuple-element.116.refs_8_), channel_id=1, source_target_pairs={{0,3},{1,2},{2,1},{3,0},{4,7},{5,6},{6,5},{7,4},{8,11},{9,10},{10,... | collective-permute-start | bytes 9224 | tf_op jit(solution)/shard_map/ppermute | solution.py:912
  83.5 2.2 %shard_map.175 = (f32[1,8,128,128]{3,2,1,0:T(8,128)}, f32[1,8,128,128]{3,2,1,0:T(8,128)}) custom-call(f32[8,128,128]{2,1,0:T(8,128)S(1)} %get-tuple-element.99.refs_3_.refs_0_, f32[8,128,128]{2,1,0:T(8,128)S(1)} %get-tuple-element.85.refs_3_.refs_2_.refs_1_, f32[1,4,128,128]{3,2,1,0:T(8,128)S(1)} %collective-permute-done.31.refs_2_, ...), custom_call_target="tpu_custom_call" | custom-call | tf_op jit(solution)/shard_map/pallas_call | solution.py:436
  (74 shorter events, 27.7 us)
Async XLA Ops:
  2.7 7.8 %collective-permute-start.7 = (f32[4,8,1024]{2,1,0:T(8,128)S(1)}, f32[4,8,1024]{2,1,0:T(8,128)S(1)}, u32[]{:S(2)}, u32[]{:S(2)}) collective-permute-start(f32[4,8,1024]{2,1,0:T(8,128)S(1)} %get-tuple-element.76), channel_id=1, source_target_pairs={{0,8},{4,12},{8,0},{12,4},{16,24},{20,28},{24,16},{28,20},{1,9},{5... | collective-permute-start | bytes 393224 | tf_op jit(solution)/shard_map/ppermute | solution.py:903
  6.7 26.5 %collective-permute-start.4 = (f32[2,4,128,128]{3,2,1,0:T(8,128)S(1)}, f32[2,4,128,128]{3,2,1,0:T(8,128)S(1)}, u32[]{:S(2)}, u32[]{:S(2)}) collective-permute-start(f32[2,4,128,128]{3,2,1,0:T(8,128)S(1)} %get-tuple-element.71), channel_id=1, source_target_pairs={{0,1},{1,0},{2,3},{3,2},{4,5},{5,4},{6,7},{7,6},{8,9},{9,8},{10,11... | collective-permute-start | bytes 1572872 | tf_op jit(solution)/shard_map/ppermute | solution.py:850
  8.3 24.9 %collective-permute-start.5 = (f32[2,4,128,128]{3,2,1,0:T(8,128)S(1)}, f32[2,4,128,128]{3,2,1,0:T(8,128)S(1)}, u32[]{:S(2)}, u32[]{:S(2)}) collective-permute-start(f32[2,4,128,128]{3,2,1,0:T(8,128)S(1)} %get-tuple-element.72), channel_id=1, source_target_pairs={{0,4},{1,2},{2,1},{3,7},{4,0},{5,6},{6,5},{7,3},{8,12},{9,10},{10,... | collective-permute-start | bytes 1572872 | tf_op jit(solution)/shard_map/ppermute | solution.py:850
  9.0 7.1 %collective-permute-start.9 = (f32[4,8,1024]{2,1,0:T(8,128)S(1)}, f32[4,8,1024]{2,1,0:T(8,128)S(1)}, u32[]{:S(2)}, u32[]{:S(2)}) collective-permute-start(f32[4,8,1024]{2,1,0:T(8,128)S(1)} %get-tuple-element.78), channel_id=1, source_target_pairs={{0,16},{4,20},{8,24},{12,28},{16,0},{20,4},{24,8},{28,12},{1,17},{... | collective-permute-start | bytes 393224 | tf_op jit(solution)/shard_map/ppermute | solution.py:903
  10.5 9.4 %collective-permute-start.10 = (f32[4,8,1024]{2,1,0:T(8,128)S(1)}, f32[4,8,1024]{2,1,0:T(8,128)S(1)}, u32[]{:S(2)}, u32[]{:S(2)}) collective-permute-start(f32[4,8,1024]{2,1,0:T(8,128)S(1)} %get-tuple-element.79), channel_id=1, source_target_pairs={{0,20},{4,16},{8,28},{12,24},{16,4},{20,0},{24,12},{28,8},{1,21},{... | collective-permute-start | bytes 393224 | tf_op jit(solution)/shard_map/ppermute | solution.py:903
  13.4 7.1 %collective-permute-start.11 = (f32[4,8,1024]{2,1,0:T(8,128)S(1)}, f32[4,8,1024]{2,1,0:T(8,128)S(1)}, u32[]{:S(2)}, u32[]{:S(2)}) collective-permute-start(f32[4,8,1024]{2,1,0:T(8,128)S(1)} %get-tuple-element.80), channel_id=1, source_target_pairs={{0,24},{4,28},{8,16},{12,20},{16,8},{20,12},{24,0},{28,4},{1,25},{... | collective-permute-start | bytes 393224 | tf_op jit(solution)/shard_map/ppermute | solution.py:903
  16.1 12.0 %collective-permute-start = (f32[1,4,128,128]{3,2,1,0:T(8,128)S(1)}, f32[1,4,128,128]{3,2,1,0:T(8,128)S(1)}, u32[]{:S(2)}, u32[]{:S(2)}) collective-permute-start(f32[1,4,128,128]{3,2,1,0:T(8,128)S(1)} %get-tuple-element.66), channel_id=1, source_target_pairs={{0,1},{1,0},{2,3},{3,2},{4,5},{5,4},{6,7},{7,6},{8,9},{9,8},{10,11... | collective-permute-start | bytes 786440 | tf_op jit(solution)/shard_map/ppermute | solution.py:850
  19.9 8.2 %collective-permute-start.1 = (f32[1,4,128,128]{3,2,1,0:T(8,128)S(1)}, f32[1,4,128,128]{3,2,1,0:T(8,128)S(1)}, u32[]{:S(2)}, u32[]{:S(2)}) collective-permute-start(f32[1,4,128,128]{3,2,1,0:T(8,128)S(1)} %get-tuple-element.67), channel_id=1, source_target_pairs={{0,4},{1,2},{2,1},{3,7},{4,0},{5,6},{6,5},{7,3},{8,12},{9,10},{10,... | collective-permute-start | bytes 786440 | tf_op jit(solution)/shard_map/ppermute | solution.py:850
  30.3 10.0 %collective-permute-start.2 = (f32[1,4,128,128]{3,2,1,0:T(8,128)S(1)}, f32[1,4,128,128]{3,2,1,0:T(8,128)S(1)}, u32[]{:S(2)}, u32[]{:S(2)}) collective-permute-start(f32[1,4,128,128]{3,2,1,0:T(8,128)S(1)} %get-tuple-element.69), channel_id=1, source_target_pairs={{0,1},{1,0},{2,3},{3,2},{4,5},{5,4},{6,7},{7,6},{8,9},{9,8},{10,11... | collective-permute-start | bytes 786440 | tf_op jit(solution)/shard_map/ppermute | solution.py:850
  33.2 7.2 %collective-permute-start.3 = (f32[1,4,128,128]{3,2,1,0:T(8,128)S(1)}, f32[1,4,128,128]{3,2,1,0:T(8,128)S(1)}, u32[]{:S(2)}, u32[]{:S(2)}) collective-permute-start(f32[1,4,128,128]{3,2,1,0:T(8,128)S(1)} %get-tuple-element.70), channel_id=1, source_target_pairs={{0,4},{1,2},{2,1},{3,7},{4,0},{5,6},{6,5},{7,3},{8,12},{9,10},{10,... | collective-permute-start | bytes 786440 | tf_op jit(solution)/shard_map/ppermute | solution.py:850
  35.8 10.2 %collective-permute-start.15 = (f32[1,4,128,128]{3,2,1,0:T(8,128)S(1)}, f32[1,4,128,128]{3,2,1,0:T(8,128)S(1)}, u32[]{:S(2)}, u32[]{:S(2)}) collective-permute-start(f32[1,4,128,128]{3,2,1,0:T(8,128)S(1)} %get-tuple-element.92), channel_id=1, source_target_pairs={{0,1},{1,0},{2,3},{3,2},{4,5},{5,4},{6,7},{7,6},{8,9},{9,8},{10,11... | collective-permute-start | bytes 786440 | tf_op jit(solution)/shard_map/ppermute | solution.py:850
  36.9 12.0 %collective-permute-start.16 = (f32[1,4,128,128]{3,2,1,0:T(8,128)S(1)}, f32[1,4,128,128]{3,2,1,0:T(8,128)S(1)}, u32[]{:S(2)}, u32[]{:S(2)}) collective-permute-start(f32[1,4,128,128]{3,2,1,0:T(8,128)S(1)} %get-tuple-element.93), channel_id=1, source_target_pairs={{0,4},{1,2},{2,1},{3,7},{4,0},{5,6},{6,5},{7,3},{8,12},{9,10},{10,... | collective-permute-start | bytes 786440 | tf_op jit(solution)/shard_map/ppermute | solution.py:850
  36.9 14.7 %collective-permute-start.17 = (f32[1,4,128,128]{3,2,1,0:T(8,128)S(1)}, f32[1,4,128,128]{3,2,1,0:T(8,128)S(1)}, u32[]{:S(2)}, u32[]{:S(2)}) collective-permute-start(f32[1,4,128,128]{3,2,1,0:T(8,128)S(1)} %get-tuple-element.94), channel_id=1, source_target_pairs={{0,1},{1,0},{2,3},{3,2},{4,5},{5,4},{6,7},{7,6},{8,9},{9,8},{10,11... | collective-permute-start | bytes 786440 | tf_op jit(solution)/shard_map/ppermute | solution.py:850
  40.3 11.2 %collective-permute-start.18 = (f32[1,4,128,128]{3,2,1,0:T(8,128)S(1)}, f32[1,4,128,128]{3,2,1,0:T(8,128)S(1)}, u32[]{:S(2)}, u32[]{:S(2)}) collective-permute-start(f32[1,4,128,128]{3,2,1,0:T(8,128)S(1)} %get-tuple-element.95), channel_id=1, source_target_pairs={{0,4},{1,2},{2,1},{3,7},{4,0},{5,6},{6,5},{7,3},{8,12},{9,10},{10,... | collective-permute-start | bytes 786440 | tf_op jit(solution)/shard_map/ppermute | solution.py:850
  41.6 15.0 %collective-permute-start.13 = (f32[1,4,128,128]{3,2,1,0:T(8,128)S(1)}, f32[1,4,128,128]{3,2,1,0:T(8,128)S(1)}, u32[]{:S(2)}, u32[]{:S(2)}) collective-permute-start(f32[1,4,128,128]{3,2,1,0:T(8,128)S(1)} %get-tuple-element.88), channel_id=1, source_target_pairs={{0,1},{1,0},{2,3},{3,2},{4,5},{5,4},{6,7},{7,6},{8,9},{9,8},{10,11... | collective-permute-start | bytes 786440 | tf_op jit(solution)/shard_map/ppermute | solution.py:850
  45.9 10.7 %collective-permute-start.14 = (f32[1,4,128,128]{3,2,1,0:T(8,128)S(1)}, f32[1,4,128,128]{3,2,1,0:T(8,128)S(1)}, u32[]{:S(2)}, u32[]{:S(2)}) collective-permute-start(f32[1,4,128,128]{3,2,1,0:T(8,128)S(1)} %get-tuple-element.89), channel_id=1, source_target_pairs={{0,4},{1,2},{2,1},{3,7},{4,0},{5,6},{6,5},{7,3},{8,12},{9,10},{10,... | collective-permute-start | bytes 786440 | tf_op jit(solution)/shard_map/ppermute | solution.py:850
  59.4 7.0 %collective-permute-start.21 = (f32[4,8,1024]{2,1,0:T(8,128)S(1)}, f32[4,8,1024]{2,1,0:T(8,128)S(1)}, u32[]{:S(2)}, u32[]{:S(2)}) collective-permute-start(f32[4,8,1024]{2,1,0:T(8,128)S(1)} %get-tuple-element.105), channel_id=1, source_target_pairs={{0,12},{4,8},{8,4},{12,0},{16,28},{20,24},{24,20},{28,16},{1,13},{... | collective-permute-start | bytes 393224 | tf_op jit(solution)/shard_map/ppermute | solution.py:903
  60.0 9.2 %collective-permute-start.26 = (f32[1,4,128,128]{3,2,1,0:T(8,128)S(1)}, f32[1,4,128,128]{3,2,1,0:T(8,128)S(1)}, u32[]{:S(2)}, u32[]{:S(2)}) collective-permute-start(f32[1,4,128,128]{3,2,1,0:T(8,128)S(1)} %get-tuple-element.111), channel_id=1, source_target_pairs={{0,1},{1,0},{2,3},{3,2},{4,5},{5,4},{6,7},{7,6},{8,9},{9,8},{10,11... | collective-permute-start | bytes 786440 | tf_op jit(solution)/shard_map/ppermute | solution.py:850
  61.9 9.7 %collective-permute-start.27 = (f32[1,4,128,128]{3,2,1,0:T(8,128)S(1)}, f32[1,4,128,128]{3,2,1,0:T(8,128)S(1)}, u32[]{:S(2)}, u32[]{:S(2)}) collective-permute-start(f32[1,4,128,128]{3,2,1,0:T(8,128)S(1)} %get-tuple-element.112), channel_id=1, source_target_pairs={{0,4},{1,2},{2,1},{3,7},{4,0},{5,6},{6,5},{7,3},{8,12},{9,10},{10,... | collective-permute-start | bytes 786440 | tf_op jit(solution)/shard_map/ppermute | solution.py:850
  64.6 17.1 %collective-permute-start.31 = (f32[1,4,128,128]{3,2,1,0:T(8,128)S(1)}, f32[1,4,128,128]{3,2,1,0:T(8,128)S(1)}, u32[]{:S(2)}, u32[]{:S(2)}) collective-permute-start(f32[1,4,128,128]{3,2,1,0:T(8,128)S(1)} %get-tuple-element.118), channel_id=1, source_target_pairs={{0,1},{1,0},{2,3},{3,2},{4,5},{5,4},{6,7},{7,6},{8,9},{9,8},{10,11... | collective-permute-start | bytes 786440 | tf_op jit(solution)/shard_map/ppermute | solution.py:850
  66.4 16.3 %collective-permute-start.32 = (f32[1,4,128,128]{3,2,1,0:T(8,128)S(1)}, f32[1,4,128,128]{3,2,1,0:T(8,128)S(1)}, u32[]{:S(2)}, u32[]{:S(2)}) collective-permute-start(f32[1,4,128,128]{3,2,1,0:T(8,128)S(1)} %get-tuple-element.119), channel_id=1, source_target_pairs={{0,4},{1,2},{2,1},{3,7},{4,0},{5,6},{6,5},{7,3},{8,12},{9,10},{10,... | collective-permute-start | bytes 786440 | tf_op jit(solution)/shard_map/ppermute | solution.py:850
  67.8 11.4 %collective-permute-start.23 = (f32[4,8,1024]{2,1,0:T(8,128)S(1)}, f32[4,8,1024]{2,1,0:T(8,128)S(1)}, u32[]{:S(2)}, u32[]{:S(2)}) collective-permute-start(f32[4,8,1024]{2,1,0:T(8,128)S(1)} %get-tuple-element.107), channel_id=1, source_target_pairs={{0,20},{4,16},{8,28},{12,24},{16,4},{20,0},{24,12},{28,8},{1,21},{... | collective-permute-start | bytes 393224 | tf_op jit(solution)/shard_map/ppermute | solution.py:903
  69.2 16.5 %collective-permute-start.24 = (f32[4,8,1024]{2,1,0:T(8,128)S(1)}, f32[4,8,1024]{2,1,0:T(8,128)S(1)}, u32[]{:S(2)}, u32[]{:S(2)}) collective-permute-start(f32[4,8,1024]{2,1,0:T(8,128)S(1)} %get-tuple-element.108), channel_id=1, source_target_pairs={{0,24},{4,28},{8,16},{12,20},{16,8},{20,12},{24,0},{28,4},{1,25},{... | collective-permute-start | bytes 393224 | tf_op jit(solution)/shard_map/ppermute | solution.py:903
  71.6 14.2 %collective-permute-start.25 = (f32[4,8,1024]{2,1,0:T(8,128)S(1)}, f32[4,8,1024]{2,1,0:T(8,128)S(1)}, u32[]{:S(2)}, u32[]{:S(2)}) collective-permute-start(f32[4,8,1024]{2,1,0:T(8,128)S(1)} %get-tuple-element.109), channel_id=1, source_target_pairs={{0,28},{4,24},{8,20},{12,16},{16,12},{20,8},{24,4},{28,0},{1,29},{... | collective-permute-start | bytes 393224 | tf_op jit(solution)/shard_map/ppermute | solution.py:903
  (17 other events, 67.1 us)
